TPU v7x, 128 devices: a whole 4x4x4 slice. The times are simulated.
128 devices in a mesh: table: 4 (over x), row: 32 (over z, y, core).
Axes of the slice: x: 4, y: 4, z: 4, core: 2. Of those that a mesh axis runs over, the one named last changes fastest.
Arguments:
- table: float32 [12288, 128, 128], P(('table', 'row')), may hold values from -2 to 2
- accumulator: float32 [12288, 128], P(('table', 'row')), may hold values from 0.05 to 2
- grads_one: float32 [131072, 128], P(('table', 'row')), may hold values from -6 to 6
- ids_one: int32 [131072], P(('table', 'row')), may hold values from 0 to 1572863, as said below
- grads_two: float32 [131072, 128], P(('table', 'row')), may hold values from -6 to 6
- ids_two: int32 [131072], P(('table', 'row')), may hold values from 0 to 1572863, as said below
- new_slot: int32 [12288], replicated, may hold values from 0 to 12287, as said below
Outputs:
- table_out: float32 [12288, 128, 128], P(('table', 'row'))
- accum_out: float32 [12288, 128], P(('table', 'row'))
Inputs may be any that keep to these rules, and one draw needn't show every extreme that they name: `ids_one`: the ids of one device are distinct. The owner of row r is device r // 12288; at most 16 of one device's ids fall on one owner, and on every device exactly 16 fall on some owner. `ids_two`: the ids of one device are distinct. After the move the owner of row r is device new_slot[r // 128] // 96; at most 16 of one device's ids fall on one such owner, and on every device exactly 16 fall on some owner. `new_slot`: A permutation. Each device keeps all but exactly 12 of its blocks in their slots; its leaving blocks go to 12 different other devices of its table group, one each, into slots freed there, so each device also receives exactly 12 blocks from different devices of its group.
All inputs are finite; a program needn't handle non-finite values.
Results may differ from a plain program's by a relative error of at most 0.00002.
Values sent between devices are 32-bit elements; how exact they have to be, the bound alone decides.
No kernel may reach another device: no remote copies, remote signals or barrier semaphores. Data moves between devices by JAX's collectives and lax.ppermute only.
A program may use at most 64 MiB of HBM per device.

v0:
```python
import jax
import jax.numpy as jnp
from jax import lax
from jax.sharding import PartitionSpec as P

LEARN = 0.5
EPSILON = 1e-08


def in_blocks(array, dim, devices):
    before, after = (array.shape[:dim], array.shape[dim + 1 :])
    return jnp.moveaxis(array.reshape(*before, devices, -1, *after), dim, 0)


def joined_along(pieces, dim):
    pieces = jnp.moveaxis(pieces, 0, dim)
    dims = pieces.shape
    return pieces.reshape(*dims[:dim], dims[dim] * dims[dim + 1], *dims[dim + 2 :])


def one_exchange(array, axis, axes, splits, concats):
    sizes = [lax.axis_size(a) for a in axes]
    pieces = in_blocks(array, splits[0], sizes[0])
    pieces = jnp.moveaxis(in_blocks(pieces, splits[1] + 1, sizes[1]), 0, 1)
    inside = pieces.shape[2:]
    pieces = pieces.reshape(-1, *inside)
    pieces = lax.all_to_all(pieces, axis, split_axis=0, concat_axis=0, tiled=True)
    pieces = joined_along(pieces.reshape(*sizes, *inside), concats[0] + 1)
    return joined_along(pieces, concats[1])


def side_by_side(arrays, axis, split_dim, concat_dim, along):
    columns = [a.reshape(*a.shape[:along], -1) for a in arrays]
    both = jnp.concatenate(columns, axis=along)
    result, at, done = (
        lax.all_to_all(both, axis, split_axis=split_dim, concat_axis=concat_dim, tiled=True),
        0,
        [],
    )
    for a, column in zip(arrays, columns):
        section = result[..., at : at + column.shape[along]]
        done.append(section.reshape(*section.shape[:along], *a.shape[along:]))
        at += column.shape[along]
    return tuple(done)


def adagrad(weights, accums, gradient):
    fresh = accums + jnp.mean(gradient * gradient, axis=-1)
    return (weights - LEARN * gradient / (jnp.sqrt(fresh)[:, None] + EPSILON), fresh)


def pack(gradient, owners, local_row, total_devices, capacity, row_count):
    feature = gradient.shape[1]
    onehot = (owners[:, None] == jnp.arange(total_devices, dtype=jnp.int32)[None, :]).astype(
        jnp.int32
    )
    within = jnp.sum((jnp.cumsum(onehot, axis=0) - onehot) * onehot, axis=1)
    places = owners * capacity + within
    outgoing = jnp.zeros((total_devices * capacity, feature), jnp.float32).at[places].set(gradient)
    targets = jnp.full((total_devices * capacity,), row_count, jnp.int32).at[places].set(local_row)
    return (
        outgoing.reshape(total_devices, capacity, feature),
        targets.reshape(total_devices, capacity),
    )


def transmit(payload, total_devices):
    tables = lax.axis_size("table")
    shaped = tuple(
        (item.reshape((tables, total_devices // tables) + item.shape[1:]) for item in payload)
    )
    return jax.tree.map(
        lambda part: one_exchange(part, ("table", "row"), ("table", "row"), (0, 1), (0, 1)), shaped
    )


def accumulate(arrived, landing, row_count):
    feature = arrived.shape[-1]
    return (
        jnp.zeros((row_count, feature), jnp.float32)
        .at[landing.reshape(-1)]
        .add(arrived.reshape(-1, feature), mode="drop")
    )


def on_device(table, accumulator, grads_one, ids_one, grads_two, ids_two, new_slot):
    blocks_here, block_rows, feature = table.shape
    row_count = blocks_here * block_rows
    groups = lax.axis_size("row")
    total_devices = lax.axis_size("table") * groups
    device = lax.axis_index("table") * groups + lax.axis_index("row")
    capacity = 2 * grads_one.shape[0] // total_devices
    first_rows, first_targets = pack(
        grads_one, ids_one // row_count, ids_one % row_count, total_devices, capacity, row_count
    )
    slot_ids = new_slot[ids_two // block_rows]
    second_rows, second_targets = pack(
        grads_two,
        slot_ids // blocks_here,
        slot_ids % blocks_here * block_rows + ids_two % block_rows,
        total_devices,
        capacity,
        row_count,
    )
    first_arrived, first_landing = transmit((first_rows, first_targets), total_devices)
    summed = accumulate(first_arrived, first_landing, row_count)
    weights, accums = adagrad(
        table.reshape(row_count, feature), accumulator.reshape(row_count), summed
    )
    weights = weights.reshape(blocks_here, block_rows, feature)
    accums = accums.reshape(blocks_here, block_rows)
    targets = lax.dynamic_slice_in_dim(new_slot, device * blocks_here, blocks_here)
    target_device = targets // blocks_here
    peer_row = jnp.where(target_device != device, target_device % groups, groups)
    out_rows = (
        jnp.zeros((groups, block_rows, feature), jnp.float32).at[peer_row].set(weights, mode="drop")
    )
    out_accums = jnp.zeros((groups, block_rows), jnp.float32).at[peer_row].set(accums, mode="drop")
    out_slots = (
        jnp.full((groups,), blocks_here, jnp.int32)
        .at[peer_row]
        .set(targets % blocks_here, mode="drop")
    )
    got_rows, got_accums, got_slots = (
        *side_by_side((out_rows, out_accums), "row", 0, 0, 2),
        lax.all_to_all(out_slots, "row", split_axis=0, concat_axis=0, tiled=True),
    )
    weights = weights.at[got_slots].set(got_rows, mode="drop")
    accums = accums.at[got_slots].set(got_accums, mode="drop")
    second_arrived, second_landing = transmit((second_rows, second_targets), total_devices)
    summed = accumulate(second_arrived, second_landing, row_count)
    weights, accums = adagrad(
        weights.reshape(row_count, feature), accums.reshape(row_count), summed
    )
    return (
        weights.reshape(blocks_here, block_rows, feature),
        accums.reshape(blocks_here, block_rows),
    )


def solution(mesh):
    in_specs = (
        P(("table", "row"), None, None),
        P(("table", "row"), None),
        P(("table", "row"), None),
        P(("table", "row")),
        P(("table", "row"), None),
        P(("table", "row")),
        P(),
    )
    out_specs = (P(("table", "row"), None, None), P(("table", "row"), None))
    return jax.shard_map(
        on_device, mesh=mesh, in_specs=in_specs, out_specs=out_specs, check_vma=False
    )
```

profile of v0, /device:TPU:0, one launch (start us, length us, event | category | flops | bytes accessed | tf_op | source)
XLA Modules:
  0.0 195.6 jit_solution(16869291521604033131)
XLA Ops:
  0.7 0.7 add_select_fusion.6
  2.2 0.7 add_select_fusion.5
  3.0 4.3 %scatter_custom_fusion = s32[2048]{0:T(1024)S(1)} fusion(s32[1024]{0:T(1024)S(1)} %get-tuple-element.9, s32[1024]{0:T(1024)S(1)} %get-tuple-element.8, s32[]{:T(128)} %constant.99.clone.1), kind=kCustom, calls=%fused_computation.81 | custom fusion | bytes 8196 | tf_op jit(solution)/shard_map/scatter | solution.py:60
  8.0 11.2 %all-to-all-start = ((s32[128,1,1,16]{3,2,1,0:T(1,128)}), s32[128,1,1,16]{3,2,1,0:T(1,128)S(1)}, u32[]{:S(2)}, u32[]{:S(2)}) async-start(s32[128,1,1,16]{3,2,1,0:T(1,128)} %bitcast.5), calls=%async_computation | async-start | bytes 131072 | tf_op jit(solution)/shard_map/all_to_all | solution.py:27
  19.9 6.2 %gather_fusion = s32[1024]{0:T(1024)S(1)} fusion(s32[12288]{0:T(1024)S(1)} %copy-done, s32[1024]{0:T(1024)S(1)} %fusion.26), kind=kCustom, calls=%fused_computation | custom fusion | bytes 12288 | tf_op jit(solution)/shard_map/gather | solution.py:96
  26.5 0.9 scatter_custom_fusion.3
  28.1 4.5 %scatter_custom_fusion.1 = f32[2048,128]{1,0:T(8,128)} fusion(s32[1024]{0:T(1024)S(1)} %get-tuple-element.9, f32[1024,128]{1,0:T(8,128)} %param.9, f32[]{:T(128)} %constant.98.clone.1), kind=kCustom, calls=%fused_computation.33 | custom fusion | bytes 1049088 | tf_op jit(solution)/shard_map/scatter | solution.py:59
  32.6 9.8 %all-to-all-start.1 = ((f32[128,1,1,16,128]{4,3,2,1,0:T(8,128)}), f32[128,1,1,16,128]{4,3,2,1,0:T(8,128)S(1)}, u32[]{:S(2)}, u32[]{:S(2)}) async-start(f32[128,1,1,16,128]{4,3,2,1,0:T(8,128)} %bitcast.12), calls=%async_computation.1 | async-start | bytes 2097152 | tf_op jit(solution)/shard_map/all_to_all | solution.py:27
  42.9 4.3 %scatter_custom_fusion.7 = s32[2048]{0:T(1024)S(1)} fusion(s32[1024]{0:T(1024)S(1)} %bitcast.133, s32[1024]{0:T(1024)S(1)} %get-tuple-element.6, s32[]{:T(128)} %constant.99.clone.1), kind=kCustom, calls=%fused_computation.79 | custom fusion | bytes 8196 | tf_op jit(solution)/shard_map/scatter | solution.py:60
  47.2 0.7 reshape_transpose_transpose_reshape_reshape_reshape_reshape.14
  47.9 4.5 %scatter_custom_fusion.8 = f32[2048,128]{1,0:T(8,128)} fusion(s32[1024]{0:T(1024)S(1)} %bitcast.134, f32[1024,128]{1,0:T(8,128)} %param.11, f32[]{:T(128)} %constant.98.clone.1), kind=kCustom, calls=%fused_computation.31 | custom fusion | bytes 1049088 | tf_op jit(solution)/shard_map/scatter | solution.py:59
  52.6 8.9 %all-to-all-done.1 = f32[128,1,1,16,128]{4,3,2,1,0:T(8,128)S(1)} async-done(((f32[128,1,1,16,128]{4,3,2,1,0:T(8,128)}), f32[128,1,1,16,128]{4,3,2,1,0:T(8,128)S(1)}, u32[]{:S(2)}, u32[]{:S(2)}) %all-to-all-start.1) | async-done | bytes 1048608 | tf_op jit(solution)/shard_map/all_to_all | solution.py:27
  61.5 3.8 %all-to-all-start.2 = ((s32[32,1,1]{2,1,0:T(1,128)}), s32[32,1,1]{2,1,0:T(1,128)S(1)}, u32[]{:S(2)}, u32[]{:S(2)}) async-start(s32[32,1,1]{2,1,0:T(1,128)} %copy.37), calls=%async_computation.2 | async-start | bytes 32768 | tf_op jit(solution)/shard_map/all_to_all | solution.py:126
  65.3 14.5 %scatter_custom_fusion.2 = f32[12288,128]{1,0:T(8,128)} fusion(s32[2048]{0:T(1024)S(1)} %bitcast.131, f32[2048,128]{1,0:T(8,128)S(1)} %bitcast.124, f32[]{:T(128)} %constant.98.clone.1), kind=kCustom, calls=%fused_computation.19 | custom fusion | flops 262144 | bytes 6291460 | tf_op jit(solution)/shard_map/scatter-add | solution.py:82
  79.9 3.7 %multiply_reduce_fusion.1 = f32[12288]{0:T(1024)S(1)} fusion(f32[12288,128]{1,0:T(8,128)} %scatter_custom_fusion.2), kind=kLoop, calls=%fused_computation.15 | loop fusion | flops 3133440 | bytes 6340608 | tf_op jit(solution)/shard_map/reduce_sum | solution.py:48
  83.6 8.2 %all-to-all-start.4 = ((s32[128,1,1,16]{3,2,1,0:T(1,128)}), s32[128,1,1,16]{3,2,1,0:T(1,128)S(1)}, u32[]{:S(2)}, u32[]{:S(2)}) async-start(s32[128,1,1,16]{3,2,1,0:T(1,128)} %bitcast.33), calls=%async_computation.4 | async-start | bytes 131072 | tf_op jit(solution)/shard_map/all_to_all | solution.py:27
  91.9 9.3 %all-to-all-done.4 = s32[128,1,1,16]{3,2,1,0:T(1,128)S(1)} async-done(((s32[128,1,1,16]{3,2,1,0:T(1,128)}), s32[128,1,1,16]{3,2,1,0:T(1,128)S(1)}, u32[]{:S(2)}, u32[]{:S(2)}) %all-to-all-start.4) | async-done | bytes 8224 | tf_op jit(solution)/shard_map/all_to_all | solution.py:27
  101.2 4.8 %all-to-all-start.5 = ((f32[128,1,1,16,128]{4,3,2,1,0:T(8,128)}), f32[128,1,1,16,128]{4,3,2,1,0:T(8,128)S(1)}, u32[]{:S(2)}, u32[]{:S(2)}) async-start(f32[128,1,1,16,128]{4,3,2,1,0:T(8,128)} %bitcast.40), calls=%async_computation.5 | async-start | bytes 2097152 | tf_op jit(solution)/shard_map/all_to_all | solution.py:27
  106.0 8.7 %bitcast_subtract_fusion.1 = f32[12288,128]{1,0:T(8,128)} fusion(f32[96,128,128]{2,1,0:T(8,128)} %param.7, f32[12288,128]{1,0:T(8,128)} %scatter_custom_fusion.2, f32[12288]{0:T(1024)S(1)} %fusion.21), kind=kLoop, calls=%fused_computation.13 | loop fusion | flops 4718592 | bytes 18923520 | tf_op jit(solution)/shard_map/sub | solution.py:49
  114.7 0.8 scatter_custom_fusion.5
  115.5 2.0 %copy.38 = f32[32,128,1]{2,1,0:T(8,128)} copy(f32[32,128,1]{1,0,2:T(8,128)S(1)} %bitcast.127) | data formatting | bytes 32768 | tf_op jit(solution)/shard_map/reshape | solution.py:33
  117.7 10.9 %scatter_fusion = f32[32,128,128]{2,1,0:T(8,128)S(1)} fusion(f32[32,128,128]{2,1,0:T(8,128)S(1)} %broadcast_in_dim.13, s32[96]{0:T(128)S(1)} %get-tuple-element.5, f32[96,128,128]{2,1,0:T(8,128)} %bitcast.120), kind=kCustom, calls=%fused_computation.5 | custom fusion | bytes 18874752 | tf_op jit(solution)/shard_map/scatter | solution.py:116
  128.6 4.0 %pad_maximum_fusion = f32[32,128,129]{2,1,0:T(8,128)} fusion(f32[32,128,1]{2,1,0:T(8,128)} %copy.38, f32[32,128,128]{2,1,0:T(8,128)S(1)} %scatter_fusion), kind=kLoop, calls=%fused_computation.16 | loop fusion | flops 528384 | bytes 4227072 | tf_op jit(solution)/shard_map/concatenate | solution.py:34
  132.7 5.0 %copy.39 = f32[32,128,129]{1,2,0:T(8,128)} copy(f32[32,128,129]{2,1,0:T(8,128)} %pad_maximum_fusion) | data formatting | bytes 4227072 | tf_op jit(solution)/shard_map/concatenate | solution.py:34
  137.7 7.1 %all-to-all-start.3 = ((f32[32,128,129]{1,2,0:T(8,128)}), f32[32,128,129]{1,2,0:T(8,128)S(1)}, u32[]{:S(2)}, u32[]{:S(2)}) async-start(f32[32,128,129]{1,2,0:T(8,128)} %copy.39), calls=%async_computation.3 | async-start | bytes 4456448 | tf_op jit(solution)/shard_map/all_to_all | solution.py:36
  145.5 14.5 %scatter_custom_fusion.9 = f32[12288,128]{1,0:T(8,128)} fusion(s32[2048]{0:T(1024)S(1)} %bitcast.132, f32[2048,128]{1,0:T(8,128)S(1)} %bitcast.123, f32[]{:T(128)} %constant.98.clone.1), kind=kCustom, calls=%fused_computation.17 | custom fusion | flops 262144 | bytes 6291460 | tf_op jit(solution)/shard_map/scatter-add | solution.py:82
  160.1 3.7 %multiply_reduce_fusion = f32[12288]{0:T(1024)S(1)} fusion(f32[12288,128]{1,0:T(8,128)} %scatter_custom_fusion.9), kind=kLoop, calls=%fused_computation.14 | loop fusion | flops 3133440 | bytes 6340608 | tf_op jit(solution)/shard_map/reduce_sum | solution.py:48
  163.8 12.5 %all-to-all-done.3 = f32[32,128,129]{1,2,0:T(8,128)S(1)} async-done(((f32[32,128,129]{1,2,0:T(8,128)}), f32[32,128,129]{1,2,0:T(8,128)S(1)}, u32[]{:S(2)}, u32[]{:S(2)}) %all-to-all-start.3) | async-done | bytes 2113568 | tf_op jit(solution)/shard_map/all_to_all | solution.py:36
  177.7 1.6 slice.28
  179.3 1.9 copy.40
  181.2 5.7 %scatter_fusion.1 = f32[96,128,128]{2,1,0:T(8,128)} fusion(f32[96,128,128]{2,1,0:T(8,128)} %bitcast.121, s32[32]{0:T(128)S(1)} %fusion.38, f32[32,128,128]{2,1,0:T(8,128)S(1)} %copy.40), kind=kCustom, calls=%fused_computation.7 | custom fusion | bytes 6291584 | tf_op jit(solution)/shard_map/scatter | solution.py:128
  186.9 8.6 %bitcast_subtract_fusion = f32[12288,128]{1,0:T(8,128)} fusion(f32[96,128,128]{2,1,0:T(8,128)} %scatter_fusion.1, f32[12288,128]{1,0:T(8,128)} %scatter_custom_fusion.9, f32[12288]{0:T(1024)S(1)} %fusion.19), kind=kLoop, calls=%fused_computation.12 | loop fusion | flops 4718592 | bytes 18923520 | tf_op jit(solution)/shard_map/sub | solution.py:49
  (45 shorter events, 6.4 us)
Async XLA Ops:
  0.6 25.4 %copy-start.2 = (s32[1024]{0:T(1024)S(1)}, s32[1024]{0:T(1024)}, u32[]{:S(2)}) copy-start(s32[1024]{0:T(1024)} %param.12) | copy-start | bytes 12292
  0.6 19.2 %copy-start = (s32[12288]{0:T(1024)S(1)}, s32[12288]{0:T(1024)}, u32[]{:S(2)}) copy-start(s32[12288]{0:T(1024)} %param.13) | copy-start | bytes 147460
  8.0 24.6 %all-to-all-start = ((s32[128,1,1,16]{3,2,1,0:T(1,128)}), s32[128,1,1,16]{3,2,1,0:T(1,128)S(1)}, u32[]{:S(2)}, u32[]{:S(2)}) async-start(s32[128,1,1,16]{3,2,1,0:T(1,128)} %bitcast.5), calls=%async_computation | async-start | bytes 131072 | tf_op jit(solution)/shard_map/all_to_all | solution.py:27
  32.6 28.9 %all-to-all-start.1 = ((f32[128,1,1,16,128]{4,3,2,1,0:T(8,128)}), f32[128,1,1,16,128]{4,3,2,1,0:T(8,128)S(1)}, u32[]{:S(2)}, u32[]{:S(2)}) async-start(f32[128,1,1,16,128]{4,3,2,1,0:T(8,128)} %bitcast.12), calls=%async_computation.1 | async-start | bytes 2097152 | tf_op jit(solution)/shard_map/all_to_all | solution.py:27
  61.5 22.1 %all-to-all-start.2 = ((s32[32,1,1]{2,1,0:T(1,128)}), s32[32,1,1]{2,1,0:T(1,128)S(1)}, u32[]{:S(2)}, u32[]{:S(2)}) async-start(s32[32,1,1]{2,1,0:T(1,128)} %copy.37), calls=%async_computation.2 | async-start | bytes 32768 | tf_op jit(solution)/shard_map/all_to_all | solution.py:126
  65.3 26.5 %copy-start.1 = (f32[96,128]{1,0:T(8,128)S(1)}, f32[96,128]{1,0:T(8,128)}, u32[]{:S(2)}) copy-start(f32[96,128]{1,0:T(8,128)} %param.8) | copy-start | bytes 147460
  83.6 17.6 %all-to-all-start.4 = ((s32[128,1,1,16]{3,2,1,0:T(1,128)}), s32[128,1,1,16]{3,2,1,0:T(1,128)S(1)}, u32[]{:S(2)}, u32[]{:S(2)}) async-start(s32[128,1,1,16]{3,2,1,0:T(1,128)} %bitcast.33), calls=%async_computation.4 | async-start | bytes 131072 | tf_op jit(solution)/shard_map/all_to_all | solution.py:27
  101.2 36.5 %all-to-all-start.5 = ((f32[128,1,1,16,128]{4,3,2,1,0:T(8,128)}), f32[128,1,1,16,128]{4,3,2,1,0:T(8,128)S(1)}, u32[]{:S(2)}, u32[]{:S(2)}) async-start(f32[128,1,1,16,128]{4,3,2,1,0:T(8,128)} %bitcast.40), calls=%async_computation.5 | async-start | bytes 2097152 | tf_op jit(solution)/shard_map/all_to_all | solution.py:27
  137.7 38.6 %all-to-all-start.3 = ((f32[32,128,129]{1,2,0:T(8,128)}), f32[32,128,129]{1,2,0:T(8,128)S(1)}, u32[]{:S(2)}, u32[]{:S(2)}) async-start(f32[32,128,129]{1,2,0:T(8,128)} %copy.39), calls=%async_computation.3 | async-start | bytes 4456448 | tf_op jit(solution)/shard_map/all_to_all | solution.py:36
where the time goes:
time: 197 us; the launch traced here: 196 us
  other arithmetic  63.6 us (32%)
  local copies, waits for them, and re-layouts  55.4 us (28%)
  starting transfers between devices  44.9 us (23%)
  waiting for transfers between devices  30.7 us (16%)
    all_to_all x4, starting transfers between devices, one_exchange(): lax.all_to_all(pieces, axis, split_axis=0, concat_axis=0, tiled=True)  34 us
    scatter-add x2, other arithmetic, accumulate(): return jnp.zeros((row_count, feature), jnp.float32).at[landing.reshape(-1...  29 us
    all_to_all x4, waiting for transfers between devices, one_exchange(): lax.all_to_all(pieces, axis, split_axis=0, concat_axis=0, tiled=True)  18.2 us
    sub x2, other arithmetic, adagrad(): weights - LEARN * gradient / (jnp.sqrt(fresh)[:, None] + EPSILON)  17.3 us
    all_to_all x1, waiting for transfers between devices, side_by_side(): lax.all_to_all(both, axis, split_axis=split_dim, concat_axis=concat_dim,...  12.5 us
    scatter x1, local copies, waits for them, and re-layouts, on_device(): jnp.zeros((groups, block_rows, feature), jnp.float32).at[peer_row]  10.9 us
    scatter x2, local copies, waits for them, and re-layouts, pack(): jnp.zeros((total_devices * capacity, feature), jnp.float32).at[places]  9 us
    scatter x2, local copies, waits for them, and re-layouts, pack(): jnp.full((total_devices * capacity,), row_count, jnp.int32).at[places]  8.63 us
  transfers between devices with their start and end apart: 6, of which 3 were waited for; matrix products, arithmetic and copies ran while one was open for 47% of the time, Pallas kernels for 0%

commit v1 on v0

v1 whole, which is shorter than its diff:
```python
import jax
import jax.numpy as jnp
from jax import lax
from jax.experimental import pallas as pl
from jax.experimental.pallas import tpu as pltpu
from jax.sharding import PartitionSpec as P

LEARN = 0.5
EPSILON = 1e-08
LANES = 128
MOVES = 12
VM = pltpu.VMEM
SM = pltpu.SMEM
MIB = 1024 * 1024


def iota(shape, dim):
    return lax.broadcasted_iota(jnp.int32, shape, dim)


def dot(a, b, contract):
    return lax.dot_general(a, b, ((contract[:1], contract[1:]), ((), ())), preferred_element_type=jnp.float32)


def lookup(which_ref, indices):
    low, high = which_ref.shape
    pick = (iota((high, indices.shape[1]), 0) == (indices >> 7)).astype(jnp.bfloat16)
    found = jnp.zeros((low, indices.shape[1]), jnp.float32)
    table = which_ref[...]
    for part, scale in ((table >> 7, 128.0), (table & 127, 1.0)):
        found += dot(part.astype(jnp.float32).astype(jnp.bfloat16), pick, (1, 0)) * scale
    here = iota(found.shape, 0) == (indices & 127)
    return jnp.sum(jnp.where(here, found, 0.0), axis=0, keepdims=True).astype(jnp.int32)


def pack_kernel(one_ids, two_ids, slot_ref, one_hbm, two_hbm, out_ref, one_ref, two_ref, place_v, place_s, names_v, sems, *, total, blocks, cap):
    stride = 2 * cap + 1
    rows = one_ref.shape[0]
    chunks = rows // LANES
    copies = [
        pltpu.make_async_copy(one_hbm, one_ref, sems.at[0]),
        pltpu.make_async_copy(two_hbm, two_ref, sems.at[1]),
    ]
    for copy in copies:
        copy.start()
    ids = one_ids[...]
    ids2 = two_ids[...]
    block_slots = (ids >> 7, lookup(slot_ref, ids2 >> 7))
    inner = (ids & 127, ids2 & 127)
    upper = jnp.where(iota((LANES, 2 * LANES), 0) < iota((LANES, 2 * LANES), 1), 1.0, 0.0).astype(jnp.bfloat16)
    lane_slot = iota((LANES, LANES), 0) & (2 * cap - 1)
    high = jnp.zeros((total, LANES), jnp.float32)
    low = jnp.zeros((total, LANES), jnp.float32)
    for step in range(2):
        slot = block_slots[step]
        owner = (slot * 43691) >> 22
        named = (slot - owner * blocks) * LANES + inner[step] + 1
        carry = jnp.zeros((total, LANES), jnp.float32)
        for c in range(chunks):
            at = slice(c * LANES, (c + 1) * LANES)
            own = owner[:, at]
            name = named[:, at]
            mine = iota((total, LANES), 0) == own
            counted = dot(jnp.where(mine, 1.0, 0.0).astype(jnp.bfloat16), upper, (1, 0))
            before = counted[:, :LANES] + carry
            carry = carry + counted[:, LANES:]
            within = jnp.sum(jnp.where(mine, before, 0.0), axis=0, keepdims=True).astype(jnp.int32) + step * cap
            place_v[pl.ds(step * chunks + c, 1), :] = own * stride + within
            where = jnp.where(lane_slot == within, 1.0, 0.0).astype(jnp.bfloat16)
            high += dot(jnp.where(mine, (name >> 7).astype(jnp.float32), 0.0).astype(jnp.bfloat16), where, (1, 1))
            low += dot(jnp.where(mine, (name & 127).astype(jnp.float32), 0.0).astype(jnp.bfloat16), where, (1, 1))
    to_scalar = pltpu.make_async_copy(place_v, place_s, sems.at[2])
    to_scalar.start()
    names_v[...] = high * 128.0 + low

    def names(d, _):
        base = d * 8
        tile = names_v[pl.ds(base, 8), :]
        for j in range(8):
            out_ref[(base + j) * stride + stride - 1] = tile[j : j + 1, :]
        return 0

    lax.fori_loop(0, total // 8, names, 0, unroll=2)
    to_scalar.wait()
    for copy in copies:
        copy.wait()

    def move(i, _):
        base = i * 8
        for step, src in enumerate((one_ref, two_ref)):
            tile = src[pl.ds(base, 8), :]
            for j in range(8):
                out_ref[place_s[step * chunks + (i >> 4), ((i & 15) * 8) + j]] = tile[j : j + 1, :]
        return 0

    lax.fori_loop(0, rows // 8, move, 0, unroll=2)


def pack(one_ids, two_ids, slots, one, two, total, blocks, cap):
    rows, feature = one.shape
    vm = pl.BlockSpec(memory_space=VM)
    hbm = pl.BlockSpec(memory_space=pl.ANY)
    stride = 2 * cap + 1
    return pl.pallas_call(
        lambda *refs: pack_kernel(*refs, total=total, blocks=blocks, cap=cap),
        out_shape=jax.ShapeDtypeStruct((total * stride, 1, feature), jnp.float32),
        in_specs=[vm, vm, vm, hbm, hbm],
        out_specs=vm,
        scratch_shapes=[
            VM((rows, feature), jnp.float32),
            VM((rows, feature), jnp.float32),
            VM((2 * rows // LANES, LANES), jnp.int32),
            SM((2 * rows // LANES, LANES), jnp.int32),
            VM((total, LANES), jnp.float32),
            pltpu.SemaphoreType.DMA((3,)),
        ],
        compiler_params=pltpu.CompilerParams(vmem_limit_bytes=16 * MIB),
        name="pack",
    )(one_ids, two_ids, slots, one, two)


def read_names(got_ref, names_v, names_s, sem, *, total, cap, dump):
    width = 2 * cap
    stride = width + 1
    per = LANES // width
    group = iota((1, LANES), 1) // width
    for a in range(total // per):
        row = got_ref[a * per * stride + stride - 1]
        for k in range(1, per):
            row = jnp.where(group == k, got_ref[(a * per + k) * stride + stride - 1], row)
        names_v[pl.ds(a, 1), :] = row.astype(jnp.int32)
    named = names_v[...]
    names_v[...] = jnp.where(named > 0, named - 1, dump)
    copy = pltpu.make_async_copy(names_v, names_s, sem)
    copy.start()
    copy.wait()


def add_rows(names_s, got_ref, sums_ref, *, total, cap, offset):
    width = 2 * cap
    stride = width + 1
    per = LANES // width

    def step(a, _):
        for k in range(per):
            base = (a * per + k) * stride + offset
            rows = [names_s[a, k * width + offset + j] for j in range(cap)]
            new = [sums_ref[pl.ds(r, 1), :] + got_ref[base + j] for j, r in enumerate(rows)]
            for r, value in zip(rows, new):
                sums_ref[pl.ds(r, 1), :] = value
        return 0

    lax.fori_loop(0, total // per, step, 0)


def square_sums(block):
    return jnp.sum(block * block, axis=1, keepdims=True)


def rate(accums):
    return LEARN / (jnp.sqrt(accums) + EPSILON)


def lane_of(columns, k):
    return columns[:, k : k + 1]


def leave_kernel(from_ref, to_ref, table_ref, acc_ref, got_ref, names_out, out_ref, sums_ref, old_ref, names_v, names_s, sems, *, total, cap):
    block, feature = table_ref.shape[1:]
    rows = table_ref.shape[0] * block

    def fetch(k):
        return pltpu.make_async_copy(table_ref.at[from_ref[k]], out_ref.at[to_ref[k], pl.ds(0, block)], sems.at[k])

    for k in range(MOVES):
        fetch(k).start()
    spans = [pl.ds(pl.multiple_of(from_ref[k] * block, block), block) for k in range(MOVES)]
    for k in range(MOVES):
        sums_ref[spans[k], :] = jnp.zeros((block, feature), jnp.float32)
        old_ref[pl.ds(k, 1), :] = acc_ref[pl.ds(from_ref[k], 1), :]
    read_names(got_ref, names_v, names_s, sems.at[MOVES], total=total, cap=cap, dump=rows)
    names_out[...] = names_v[...]
    add_rows(names_s, got_ref, sums_ref, total=total, cap=cap, offset=0)
    lane = iota((block, LANES), 1)
    squares = jnp.zeros((block, LANES), jnp.float32)
    for k in range(MOVES):
        squares = jnp.where(lane == k, square_sums(sums_ref[spans[k], :]), squares)
    fresh = jnp.transpose(old_ref[...]) + squares * (1.0 / feature)
    rates = rate(jnp.where(lane < MOVES, fresh, 1.0))
    old_ref[...] = jnp.transpose(fresh)
    for k in range(MOVES):
        fetch(k).wait()
    for k in range(MOVES):
        weights = out_ref[to_ref[k], pl.ds(0, block), :]
        out_ref[to_ref[k], pl.ds(0, block), :] = weights - lane_of(rates, k) * sums_ref[spans[k], :]
        out_ref[to_ref[k], pl.ds(block, 1), :] = old_ref[pl.ds(k, 1), :]


def leave(came_from, go_to, table, acc, got, peers, total, cap):
    blocks, block, feature = table.shape
    vm = pl.BlockSpec(memory_space=VM)
    sm = pl.BlockSpec(memory_space=SM)
    names = (total * 2 * cap // LANES, LANES)
    return pl.pallas_call(
        lambda *refs: leave_kernel(*refs, total=total, cap=cap),
        out_shape=(
            jax.ShapeDtypeStruct(names, jnp.int32),
            jax.ShapeDtypeStruct((peers, block + 8, feature), jnp.float32),
        ),
        in_specs=[sm, sm, pl.BlockSpec(memory_space=pl.ANY), vm, vm],
        out_specs=(vm, vm),
        scratch_shapes=[
            VM((blocks * block + 8, feature), jnp.float32),
            VM((LANES, LANES), jnp.float32),
            VM(names, jnp.int32),
            SM(names, jnp.int32),
            pltpu.SemaphoreType.DMA((MOVES + 1,)),
        ],
        compiler_params=pltpu.CompilerParams(vmem_limit_bytes=20 * MIB),
        name="leave",
    )(came_from, go_to, table, acc, got)


def stay_kernel(names_ref, slots_ref, table_ref, acc_ref, got_ref, out_ref, accout_ref, arrive_ref, one_ref, two_ref, rates_ref, *, total, cap, blocks):
    i = pl.program_id(0)
    each, block, feature = table_ref.shape

    @pl.when(i == 0)
    def _():
        def clear(b, _):
            at = pl.ds(pl.multiple_of(b * block, block), block)
            one_ref[at, :] = jnp.zeros((block, feature), jnp.float32)
            two_ref[at, :] = jnp.zeros((block, feature), jnp.float32)
            return 0

        lax.fori_loop(0, blocks, clear, 0)
        add_rows(names_ref, got_ref, one_ref, total=total, cap=cap, offset=0)
        add_rows(names_ref, got_ref, two_ref, total=total, cap=cap, offset=cap)
        lane = iota((block, LANES), 1)

        def squares(g, sums):
            sums = list(sums)
            for k in range(4):
                b = g * 4 + k
                at = pl.ds(pl.multiple_of(b * block, block), block)
                for n, ref in enumerate((one_ref, two_ref)):
                    sums[n] = jnp.where(lane == b, square_sums(ref[at, :]), sums[n])
            return tuple(sums)

        zero = jnp.zeros((block, LANES), jnp.float32)
        first, second = lax.fori_loop(0, blocks // 4, squares, (zero, zero))
        old = jnp.concatenate([acc_ref[...], jnp.ones((LANES - blocks, LANES), jnp.float32)], axis=0)
        fresh = jnp.transpose(old) + first * (1.0 / feature)
        rates_ref[0] = rate(fresh)
        fresh = fresh + second * (1.0 / feature)
        rates_ref[1] = rate(fresh)
        accout_ref[...] = jnp.transpose(fresh)[:blocks, :]
        for k in range(MOVES):
            at = pl.ds(pl.multiple_of(slots_ref[k] * block, block), block)
            arrive_ref[k] = two_ref[at, :]

    turn = (LANES - each * i) % LANES
    one_rate = pltpu.roll(rates_ref[0], turn, 1)
    two_rate = pltpu.roll(rates_ref[1], turn, 1)
    for k in range(each):
        at = pl.ds(pl.multiple_of((i * each + k) * block, block), block)
        weights = table_ref[k] - lane_of(one_rate, k) * one_ref[at, :]
        out_ref[k] = weights - lane_of(two_rate, k) * two_ref[at, :]


def stay(names, slots, table, acc, got, total, cap, each=8):
    blocks, block, feature = table.shape
    vm = pl.BlockSpec(memory_space=VM)
    sm = pl.BlockSpec(memory_space=SM)
    piece = pl.BlockSpec((each, block, feature), lambda i: (i, 0, 0))
    return pl.pallas_call(
        lambda *refs: stay_kernel(*refs, total=total, cap=cap, blocks=blocks),
        grid=(blocks // each,),
        out_shape=(
            jax.ShapeDtypeStruct(table.shape, jnp.float32),
            jax.ShapeDtypeStruct(acc.shape, jnp.float32),
            jax.ShapeDtypeStruct((MOVES, block, feature), jnp.float32),
        ),
        in_specs=[sm, sm, piece, vm, vm],
        out_specs=(piece, vm, vm),
        scratch_shapes=[
            VM((blocks * block + 8, feature), jnp.float32),
            VM((blocks * block + 8, feature), jnp.float32),
            VM((2, LANES, LANES), jnp.float32),
        ],
        compiler_params=pltpu.CompilerParams(vmem_limit_bytes=28 * MIB),
        name="stay",
    )(names, slots, table, acc, got)


def arrive_kernel(peers_ref, slots_ref, got_ref, second_ref, stayed_ref, accstay_ref, out_ref, acc_ref, buf_ref, old_ref, sems):
    block, feature = stayed_ref.shape[1:]
    lane = iota((block, LANES), 1)
    for k in range(MOVES):
        old_ref[pl.ds(k, 1), :] = got_ref[peers_ref[k], pl.ds(block, 1), :]
    squares = jnp.zeros((block, LANES), jnp.float32)
    for k in range(MOVES):
        squares = jnp.where(lane == k, square_sums(second_ref[k]), squares)
    fresh = jnp.transpose(old_ref[...]) + squares * (1.0 / feature)
    rates = rate(jnp.where(lane < MOVES, fresh, 1.0))
    copies = []
    for k in range(MOVES):
        buf_ref[k] = got_ref[peers_ref[k], pl.ds(0, block), :] - lane_of(rates, k) * second_ref[k]
        copies.append(pltpu.make_async_copy(buf_ref.at[k], out_ref.at[slots_ref[k]], sems.at[k]))
        copies[-1].start()
    old_ref[...] = jnp.transpose(fresh)
    acc_ref[...] = accstay_ref[...]
    for k in range(MOVES):
        acc_ref[pl.ds(slots_ref[k], 1), :] = old_ref[pl.ds(k, 1), :]
    for copy in copies:
        copy.wait()


def arrive(peers, slots, got, second, stayed, accstay):
    blocks, block, feature = stayed.shape
    vm = pl.BlockSpec(memory_space=VM)
    sm = pl.BlockSpec(memory_space=SM)
    hbm = pl.BlockSpec(memory_space=pl.ANY)
    return pl.pallas_call(
        arrive_kernel,
        out_shape=(
            jax.ShapeDtypeStruct(stayed.shape, jnp.float32),
            jax.ShapeDtypeStruct(accstay.shape, jnp.float32),
        ),
        in_specs=[sm, sm, vm, vm, hbm, vm],
        out_specs=(hbm, vm),
        scratch_shapes=[
            VM((MOVES, block, feature), jnp.float32),
            VM((LANES, LANES), jnp.float32),
            pltpu.SemaphoreType.DMA((MOVES,)),
        ],
        input_output_aliases={4: 0},
        compiler_params=pltpu.CompilerParams(vmem_limit_bytes=12 * MIB),
        name="arrive",
    )(peers, slots, got, second, stayed, accstay)


def listed(mask, values):
    position = jnp.cumsum(mask.astype(jnp.int32)) - 1
    hit = mask[None, :] & (position[None, :] == jnp.arange(MOVES, dtype=jnp.int32)[:, None])
    return [jnp.sum(jnp.where(hit, v[None, :], 0), axis=1) for v in values]


def on_device(table, accumulator, grads_one, ids_one, grads_two, ids_two, new_slot):
    blocks, block, feature = table.shape
    peers = lax.axis_size("row")
    total = lax.axis_size("table") * peers
    group = lax.axis_index("table")
    mine = lax.axis_index("row")
    device = group * peers + mine
    rows = grads_one.shape[0]
    cap = 2 * rows // total

    slot_table = new_slot.reshape(-1, LANES).T
    outgoing = pack(ids_one.reshape(1, rows), ids_two.reshape(1, rows), slot_table, grads_one, grads_two, total, blocks, cap)
    got = lax.all_to_all(outgoing, ("table", "row"), split_axis=0, concat_axis=0, tiled=True)

    here = lax.dynamic_slice_in_dim(new_slot, group * peers * blocks, peers * blocks).reshape(peers, blocks)
    own = lax.dynamic_slice_in_dim(new_slot, device * blocks, blocks)
    came_from, go_to = listed(own // blocks != device, (jnp.arange(blocks, dtype=jnp.int32), own // blocks % peers))
    peer = jnp.arange(peers, dtype=jnp.int32)
    to_me = (here // blocks == device) & (peer != mine)[:, None]
    slots = jnp.sum(jnp.where(to_me, here - device * blocks + 1, 0), axis=1)
    from_peer, slots = listed(slots > 0, (peer, slots - 1))

    names, moving = leave(came_from, go_to, table, accumulator, got, peers, total, cap)
    moved = lax.all_to_all(moving, "row", split_axis=0, concat_axis=0, tiled=True)
    stayed, accstay, second = stay(names, slots, table, accumulator, got, total, cap)
    return arrive(from_peer, slots, moved, second, stayed, accstay)


def solution(mesh):
    in_specs = (
        P(("table", "row"), None, None),
        P(("table", "row"), None),
        P(("table", "row"), None),
        P(("table", "row")),
        P(("table", "row"), None),
        P(("table", "row")),
        P(),
    )
    out_specs = (P(("table", "row"), None, None), P(("table", "row"), None))
    return jax.shard_map(
        on_device, mesh=mesh, in_specs=in_specs, out_specs=out_specs, check_vma=False
    )
```

time: 197 us -> 109 us (0.55)
  other arithmetic: 63.6 us -> 0.97 us
  local copies, waits for them, and re-layouts: 55.4 us -> 13 us
  Pallas kernels: 0 us -> 39.8 us
  starting transfers between devices: 44.9 us -> 16 us
  waiting for transfers between devices: 30.7 us -> 38 us
    pallas_call x0 -> x4, Pallas kernels: none -> 39.8 us  [the longest x1 20.5 us: stay(): pl.pallas_call(lambda *refs: stay_kernel(*refs, total=total, cap=cap, blo...]
    scatter x8 -> x0, local copies, waits for them, and re-layouts: 35.8 us -> none  [the longest x1 10.9 us: on_device(): jnp.zeros((groups, block_rows, feature), jnp.float32).at[peer_row]]
    scatter-add x2 -> x0, other arithmetic: 29 us -> none  [accumulate(): return jnp.zeros((row_count, feature), jnp.float32).at[landing.reshape(-1...]
    all_to_all x6 -> x2, starting transfers between devices: 44.9 us -> 16 us  [the longest x1 11.2 us: on_device(): lax.all_to_all(outgoing, ('table', 'row'), split_axis=0, concat_axis=0, t...]
    sub x2 -> x3, other arithmetic: 17.3 us -> 0.22 us  [the longest x2 0.22 us: listed(): position = jnp.cumsum(mask.astype(jnp.int32)) - 1]
    unnamed x6 -> x20, local copies, waits for them, and re-layouts: 0.02 us -> 11.7 us
    reduce_sum x4 -> x3, other arithmetic: 8.19 us -> 0.42 us  [the longest x2 0.24 us: listed(): return [jnp.sum(jnp.where(hit, v[None, :], 0), axis=1) for v in values]]
    all_to_all x6 -> x2, waiting for transfers between devices: 30.7 us -> 38 us  [the longest x1 30.5 us: on_device(): lax.all_to_all(outgoing, ('table', 'row'), split_axis=0, concat_axis=0, t...]
  transfers between devices with their start and end apart: 6 -> 2, of which waited for: 3 -> 2; matrix products, arithmetic and copies ran while one was open for 47% -> 1% of each run, Pallas kernels for 0% -> 19%
where the time goes in v1:
time: 109 us
  Pallas kernels  39.8 us (37%)
  waiting for transfers between devices  38 us (35%)
  starting transfers between devices  16 us (15%)
  local copies, waits for them, and re-layouts  13 us (12%)
    all_to_all x1, waiting for transfers between devices, on_device(): lax.all_to_all(outgoing, ('table', 'row'), split_axis=0, concat_axis=0, t...  30.5 us
    pallas_call x1, Pallas kernels, stay(): pl.pallas_call(lambda *refs: stay_kernel(*refs, total=total, cap=cap, blo...  20.5 us
    unnamed x20, local copies, waits for them, and re-layouts  11.7 us
    all_to_all x1, starting transfers between devices, on_device(): lax.all_to_all(outgoing, ('table', 'row'), split_axis=0, concat_axis=0, t...  11.2 us
    pallas_call x1, Pallas kernels, pack(): pl.pallas_call(lambda *refs: pack_kernel(*refs, total=total, blocks=block...  9.55 us
    all_to_all x1, waiting for transfers between devices, on_device(): lax.all_to_all(moving, 'row', split_axis=0, concat_axis=0, tiled=True)  7.46 us
    pallas_call x1, Pallas kernels, leave(): pl.pallas_call(lambda *refs: leave_kernel(*refs, total=total, cap=cap), o...  6.1 us
    all_to_all x1, starting transfers between devices, on_device(): lax.all_to_all(moving, 'row', split_axis=0, concat_axis=0, tiled=True)  4.79 us
  transfers between devices with their start and end apart: 2, of which 2 were waited for; matrix products, arithmetic and copies ran while one was open for 1% of the time, Pallas kernels for 19%

profile of v1, /device:TPU:0, one launch (start us, length us, event | category | flops | bytes accessed | tf_op | source)
XLA Modules:
  0.0 108.5 jit_solution(16714809598096643513)
XLA Ops:
  0.6 0.9 copy.17
  1.5 0.0 copy-start.4
  1.5 1.0 copy-done.4
  2.6 1.0 copy-done.5
  3.6 0.7 copy-done.7
  4.3 0.7 copy-done.8
  5.0 9.6 %pack.1 = f32[4224,1,128]{2,1,0:T(1,128)S(1)} custom-call(s32[1,1024]{1,0:T(1,128)S(1)} %bitcast.9, s32[1,1024]{1,0:T(1,128)S(1)} %bitcast.10, s32[128,96]{1,0:T(8,128)S(1)} %bitcast.8, f32[1024,128]{1,0:T(8,128)S(1)} %copy-done.4, f32[1024,128]{1,0:T(8,128)S(1)} %copy-done.5), custom_call_target="tpu_custom_call" | custom-call | tf_op jit(solution)/shard_map/pack/pallas_call | solution.py:104
  14.5 0.0 copy-start.2
  14.6 1.3 %copy-done.2 = f32[4224,1,128]{2,1,0:T(1,128)} copy-done((f32[4224,1,128]{2,1,0:T(1,128)}, f32[4224,1,128]{2,1,0:T(1,128)S(1)}, u32[]{:S(2)}) %copy-start.2) | copy-done | bytes 2162712
  15.9 11.2 %all-to-all-start = ((f32[4224,1,128]{2,1,0:T(1,128)}), f32[4224,1,128]{2,1,0:T(1,128)S(1)}, u32[]{:S(2)}, u32[]{:S(2)}) async-start(f32[4224,1,128]{2,1,0:T(1,128)} %copy-done.2), calls=%async_computation | async-start | bytes 4325376 | tf_op jit(solution)/shard_map/all_to_all | solution.py:361
  27.1 0.1 convert_bitcast_fusion
  27.2 0.1 copy.16
  27.3 0.1 reduce-window.17
  27.4 0.1 add_reduce_fusion
  27.6 0.1 select_reduce_fusion.1
  27.7 30.5 %all-to-all-done.refs_4_ = f32[4224,1,128]{2,1,0:T(1,128)S(1)} async-done(((f32[4224,1,128]{2,1,0:T(1,128)}), f32[4224,1,128]{2,1,0:T(1,128)S(1)}, u32[]{:S(2)}, u32[]{:S(2)}) %all-to-all-start) | async-done | bytes 2162720 | tf_op jit(solution)/shard_map/all_to_all | solution.py:361
  58.2 2.8 %copy-done = f32[96,128,128]{2,1,0:T(8,128)S(1)} copy-done((f32[96,128,128]{2,1,0:T(8,128)S(1)}, f32[96,128,128]{2,1,0:T(8,128)}, u32[]{:S(2)}) %copy-start) | copy-done | bytes 6291480
  61.0 6.1 %leave.1 = (s32[32,128]{1,0:T(8,128)S(1)}, f32[32,136,128]{2,1,0:T(8,128)S(1)}) custom-call(s32[12]{0:T(128)S(1)} %get-tuple-element.13.refs_0_, s32[12]{0:T(128)S(1)} %get-tuple-element.12.refs_1_, f32[96,128,128]{2,1,0:T(8,128)S(1)} %copy-done, f32[96,128]{1,0:T(8,128)S(1)} %copy-done.6, f32[4224,1,128]{2,1,0:T(1,128)S(1)} %all-to-all-done.refs_4_), custom_call_target="tpu_custom_call" | custom-call | tf_op jit(solution)/shard_map/leave/pallas_call | solution.py:204
  67.1 1.4 %copy-done.3 = f32[32,136,128]{2,1,0:T(8,128)} copy-done((f32[32,136,128]{2,1,0:T(8,128)}, f32[32,136,128]{2,1,0:T(8,128)S(1)}, u32[]{:S(2)}) %copy-start.3) | copy-done | bytes 2228248
  68.4 4.8 %all-to-all-start.1 = ((f32[32,136,128]{2,1,0:T(8,128)}), f32[32,136,128]{2,1,0:T(8,128)}, u32[]{:S(2)}, u32[]{:S(2)}) async-start(f32[32,136,128]{2,1,0:T(8,128)} %copy-done.3), calls=%async_computation.1 | async-start | bytes 4456448 | tf_op jit(solution)/shard_map/all_to_all | solution.py:372
  73.3 0.1 and.44
  73.4 0.1 div.18
  73.4 0.1 add.44
  73.5 0.2 select_reduce_fusion
  73.7 0.1 copy.15
  73.8 0.1 reduce-window.16
  73.9 0.1 add_reduce_fusion.1
  74.0 0.1 select_reduce_fusion.3
  74.1 2.8 %copy-done.1 = f32[96,128,128]{2,1,0:T(8,128)S(1)} copy-done((f32[96,128,128]{2,1,0:T(8,128)S(1)}, f32[96,128,128]{2,1,0:T(8,128)}, u32[]{:S(2)}) %copy-start.1) | copy-done | bytes 6291480
  76.9 20.5 %stay.1 = (f32[96,128,128]{2,1,0:T(8,128)}, f32[96,128]{1,0:T(8,128)S(1)}, f32[12,128,128]{2,1,0:T(8,128)S(1)}) custom-call(s32[32,128]{1,0:T(8,128)S(1)} %get-tuple-element.8.refs_0_, s32[12]{0:T(128)S(1)} %get-tuple-element.14.refs_1_.slots_ref, f32[96,128,128]{2,1,0:T(8,128)S(1)} %copy-done.1, f32[96,128]{1,0:T(8,128)S(1)} %copy-done.6, ...), custom_call_target="tpu_custom_call" | custom-call | tf_op jit(solution)/shard_map/stay/pallas_call | solution.py:276
  97.4 7.5 %all-to-all-done.1.got_ref = f32[32,136,128]{2,1,0:T(8,128)} async-done(((f32[32,136,128]{2,1,0:T(8,128)}), f32[32,136,128]{2,1,0:T(8,128)}, u32[]{:S(2)}, u32[]{:S(2)}) %all-to-all-start.1) | async-done | bytes 2228256 | tf_op jit(solution)/shard_map/all_to_all | solution.py:372
  104.8 3.7 %arrive.1 = (f32[96,128,128]{2,1,0:T(8,128)}, f32[96,128]{1,0:T(8,128)}) custom-call(s32[12]{0:T(128)S(1)} %get-tuple-element.15.peers_ref, s32[12]{0:T(128)S(1)} %get-tuple-element.14.refs_1_.slots_ref, f32[32,136,128]{2,1,0:T(8,128)} %all-to-all-done.1.got_ref, f32[12,128,128]{2,1,0:T(8,128)S(1)} %get-tuple-element.9.second_ref, ...), custom_call_target="tpu_custom_call", output_to_operand_aliasing={{0}: (4, {})} | custom-call | tf_op jit(solution)/shard_map/arrive/pallas_call | solution.py:324
  (16 shorter events, 0.1 us)
Async XLA Ops:
  1.5 1.0 copy-start.4
  2.6 1.0 copy-start.5
  3.6 0.7 copy-start.7
  4.3 0.7 copy-start.8
  14.5 1.3 %copy-start.2 = (f32[4224,1,128]{2,1,0:T(1,128)}, f32[4224,1,128]{2,1,0:T(1,128)S(1)}, u32[]{:S(2)}) copy-start(f32[4224,1,128]{2,1,0:T(1,128)S(1)} %pack.1) | copy-start | bytes 6488068
  15.9 11.2 %copy-start.9 = (s32[12288]{0:T(1024)S(1)}, s32[12288]{0:T(1024)}, u32[]{:S(2)}) copy-start(s32[12288]{0:T(1024)} %param.13) | copy-start | bytes 147460
  15.9 42.3 %copy-start.6 = (f32[96,128]{1,0:T(8,128)S(1)}, f32[96,128]{1,0:T(8,128)}, u32[]{:S(2)}) copy-start(f32[96,128]{1,0:T(8,128)} %refs_3_.5) | copy-start | bytes 147460
  15.9 42.3 %all-to-all-start = ((f32[4224,1,128]{2,1,0:T(1,128)}), f32[4224,1,128]{2,1,0:T(1,128)S(1)}, u32[]{:S(2)}, u32[]{:S(2)}) async-start(f32[4224,1,128]{2,1,0:T(1,128)} %copy-done.2), calls=%async_computation | async-start | bytes 4325376 | tf_op jit(solution)/shard_map/all_to_all | solution.py:361
  58.2 2.8 %copy-start = (f32[96,128,128]{2,1,0:T(8,128)S(1)}, f32[96,128,128]{2,1,0:T(8,128)}, u32[]{:S(2)}) copy-start(f32[96,128,128]{2,1,0:T(8,128)} %refs_2_.3) | copy-start | bytes 18874372
  67.1 1.4 %copy-start.3 = (f32[32,136,128]{2,1,0:T(8,128)}, f32[32,136,128]{2,1,0:T(8,128)S(1)}, u32[]{:S(2)}) copy-start(f32[32,136,128]{2,1,0:T(8,128)S(1)} %get-tuple-element.7) | copy-start | bytes 6684676
  68.4 36.4 %all-to-all-start.1 = ((f32[32,136,128]{2,1,0:T(8,128)}), f32[32,136,128]{2,1,0:T(8,128)}, u32[]{:S(2)}, u32[]{:S(2)}) async-start(f32[32,136,128]{2,1,0:T(8,128)} %copy-done.3), calls=%async_computation.1 | async-start | bytes 4456448 | tf_op jit(solution)/shard_map/all_to_all | solution.py:372
  74.1 2.8 %copy-start.1 = (f32[96,128,128]{2,1,0:T(8,128)S(1)}, f32[96,128,128]{2,1,0:T(8,128)}, u32[]{:S(2)}) copy-start(f32[96,128,128]{2,1,0:T(8,128)} %refs_2_.3) | copy-start | bytes 18874372

commit v2 on v1

--- a/solution.py
+++ b/solution.py
@@ -11,6 +11,8 @@
 MOVES = 12
 VM = pltpu.VMEM
 SM = pltpu.SMEM
+ALL_VMEM = 67043328
+LEAVE_ROOM = 14000000
 MIB = 1024 * 1024
 
 
@@ -23,28 +25,29 @@
 
 
 def lookup(which_ref, indices):
-    low, high = which_ref.shape
+    high, low = which_ref.shape
     pick = (iota((high, indices.shape[1]), 0) == (indices >> 7)).astype(jnp.bfloat16)
     found = jnp.zeros((low, indices.shape[1]), jnp.float32)
-    table = which_ref[...]
+    table = jnp.concatenate([which_ref[...].astype(jnp.float32), jnp.zeros((low - high, low), jnp.float32)], axis=0)
+    table = jnp.transpose(table)[:, :high].astype(jnp.int32)
     for part, scale in ((table >> 7, 128.0), (table & 127, 1.0)):
         found += dot(part.astype(jnp.float32).astype(jnp.bfloat16), pick, (1, 0)) * scale
     here = iota(found.shape, 0) == (indices & 127)
     return jnp.sum(jnp.where(here, found, 0.0), axis=0, keepdims=True).astype(jnp.int32)
 
 
-def pack_kernel(one_ids, two_ids, slot_ref, one_hbm, two_hbm, out_ref, one_ref, two_ref, place_v, place_s, names_v, sems, *, total, blocks, cap):
+def pack_kernel(one_ids, two_ids, slot_hbm, one_hbm, two_hbm, out_hbm, one_ref, two_ref, ids_ref, ids2_ref, slot_ref, place_v, place_s, names_v, out_ref, sems, *, total, blocks, cap):
     stride = 2 * cap + 1
     rows = one_ref.shape[0]
     chunks = rows // LANES
-    copies = [
-        pltpu.make_async_copy(one_hbm, one_ref, sems.at[0]),
-        pltpu.make_async_copy(two_hbm, two_ref, sems.at[1]),
-    ]
+    pairs = ((one_ids, ids_ref), (two_ids, ids2_ref), (slot_hbm, slot_ref), (one_hbm, one_ref), (two_hbm, two_ref))
+    copies = [pltpu.make_async_copy(src, dst, sems.at[n]) for n, (src, dst) in enumerate(pairs)]
     for copy in copies:
         copy.start()
-    ids = one_ids[...]
-    ids2 = two_ids[...]
+    for copy in copies[:3]:
+        copy.wait()
+    ids = ids_ref[...]
+    ids2 = ids2_ref[...]
     block_slots = (ids >> 7, lookup(slot_ref, ids2 >> 7))
     inner = (ids & 127, ids2 & 127)
     upper = jnp.where(iota((LANES, 2 * LANES), 0) < iota((LANES, 2 * LANES), 1), 1.0, 0.0).astype(jnp.bfloat16)
@@ -69,7 +72,7 @@
             where = jnp.where(lane_slot == within, 1.0, 0.0).astype(jnp.bfloat16)
             high += dot(jnp.where(mine, (name >> 7).astype(jnp.float32), 0.0).astype(jnp.bfloat16), where, (1, 1))
             low += dot(jnp.where(mine, (name & 127).astype(jnp.float32), 0.0).astype(jnp.bfloat16), where, (1, 1))
-    to_scalar = pltpu.make_async_copy(place_v, place_s, sems.at[2])
+    to_scalar = pltpu.make_async_copy(place_v, place_s, sems.at[5])
     to_scalar.start()
     names_v[...] = high * 128.0 + low
 
@@ -82,39 +85,45 @@
 
     lax.fori_loop(0, total // 8, names, 0, unroll=2)
     to_scalar.wait()
-    for copy in copies:
+    for copy in copies[3:]:
         copy.wait()
-
-    def move(i, _):
-        base = i * 8
-        for step, src in enumerate((one_ref, two_ref)):
-            tile = src[pl.ds(base, 8), :]
-            for j in range(8):
-                out_ref[place_s[step * chunks + (i >> 4), ((i & 15) * 8) + j]] = tile[j : j + 1, :]
-        return 0
-
-    lax.fori_loop(0, rows // 8, move, 0, unroll=2)
+    for step, src in enumerate((one_ref, two_ref)):
+
+        def move(c, _):
+            for g in range(LANES // 8):
+                tile = src[pl.ds(c * LANES + g * 8, 8), :]
+                for j in range(8):
+                    out_ref[place_s[step * chunks + c, g * 8 + j]] = tile[j : j + 1, :]
+            return 0
+
+        lax.fori_loop(0, chunks, move, 0)
+    whole = pltpu.make_async_copy(out_ref, out_hbm, sems.at[6])
+    whole.start()
+    whole.wait()
 
 
 def pack(one_ids, two_ids, slots, one, two, total, blocks, cap):
     rows, feature = one.shape
-    vm = pl.BlockSpec(memory_space=VM)
-    hbm = pl.BlockSpec(memory_space=pl.ANY)
+    hbm = pl.BlockSpec(memory_space=pltpu.HBM)
     stride = 2 * cap + 1
     return pl.pallas_call(
         lambda *refs: pack_kernel(*refs, total=total, blocks=blocks, cap=cap),
         out_shape=jax.ShapeDtypeStruct((total * stride, 1, feature), jnp.float32),
-        in_specs=[vm, vm, vm, hbm, hbm],
-        out_specs=vm,
+        in_specs=[hbm] * 5,
+        out_specs=hbm,
         scratch_shapes=[
             VM((rows, feature), jnp.float32),
             VM((rows, feature), jnp.float32),
+            VM((1, rows), jnp.int32),
+            VM((1, rows), jnp.int32),
+            VM(slots.shape, jnp.int32),
             VM((2 * rows // LANES, LANES), jnp.int32),
             SM((2 * rows // LANES, LANES), jnp.int32),
             VM((total, LANES), jnp.float32),
-            pltpu.SemaphoreType.DMA((3,)),
+            VM((total * stride, 1, feature), jnp.float32),
+            pltpu.SemaphoreType.DMA((7,)),
         ],
-        compiler_params=pltpu.CompilerParams(vmem_limit_bytes=16 * MIB),
+        compiler_params=pltpu.CompilerParams(vmem_limit_bytes=ALL_VMEM),
         name="pack",
     )(one_ids, two_ids, slots, one, two)
 
@@ -165,19 +174,39 @@
     return columns[:, k : k + 1]
 
 
-def leave_kernel(from_ref, to_ref, table_ref, acc_ref, got_ref, names_out, out_ref, sums_ref, old_ref, names_v, names_s, sems, *, total, cap):
+def fetch_kernel(from_ref, table_ref, acc_ref, out_ref, old_ref, sems):
+    copies = [pltpu.make_async_copy(table_ref.at[from_ref[k]], out_ref.at[k], sems.at[k]) for k in range(MOVES)]
+    for copy in copies:
+        copy.start()
+    old_ref[...] = jnp.zeros_like(old_ref)
+    for k in range(MOVES):
+        old_ref[pl.ds(k, 1), :] = acc_ref[pl.ds(from_ref[k], 1), :]
+    for copy in copies:
+        copy.wait()
+
+
+def fetch(came_from, table, acc):
+    vm = pl.BlockSpec(memory_space=VM)
+    hbm = pl.BlockSpec(memory_space=pltpu.HBM)
+    return pl.pallas_call(
+        fetch_kernel,
+        out_shape=(
+            jax.ShapeDtypeStruct((MOVES,) + table.shape[1:], jnp.float32),
+            jax.ShapeDtypeStruct((LANES, LANES), jnp.float32),
+        ),
+        in_specs=[pl.BlockSpec(memory_space=SM), hbm, vm],
+        out_specs=(vm, vm),
+        scratch_shapes=[pltpu.SemaphoreType.DMA((MOVES,))],
+        compiler_params=pltpu.CompilerParams(vmem_limit_bytes=ALL_VMEM - LEAVE_ROOM),
+        name="fetch",
+    )(came_from, table, acc)
+
+
+def leave_kernel(from_ref, to_ref, table_ref, acc_ref, got_ref, names_out, out_hbm, out_ref, sums_ref, old_ref, names_v, names_s, sems, *, total, cap, rows):
     block, feature = table_ref.shape[1:]
-    rows = table_ref.shape[0] * block
-
-    def fetch(k):
-        return pltpu.make_async_copy(table_ref.at[from_ref[k]], out_ref.at[to_ref[k], pl.ds(0, block)], sems.at[k])
-
-    for k in range(MOVES):
-        fetch(k).start()
     spans = [pl.ds(pl.multiple_of(from_ref[k] * block, block), block) for k in range(MOVES)]
     for k in range(MOVES):
         sums_ref[spans[k], :] = jnp.zeros((block, feature), jnp.float32)
-        old_ref[pl.ds(k, 1), :] = acc_ref[pl.ds(from_ref[k], 1), :]
     read_names(got_ref, names_v, names_s, sems.at[MOVES], total=total, cap=cap, dump=rows)
     names_out[...] = names_v[...]
     add_rows(names_s, got_ref, sums_ref, total=total, cap=cap, offset=0)
@@ -185,38 +214,41 @@
     squares = jnp.zeros((block, LANES), jnp.float32)
     for k in range(MOVES):
         squares = jnp.where(lane == k, square_sums(sums_ref[spans[k], :]), squares)
-    fresh = jnp.transpose(old_ref[...]) + squares * (1.0 / feature)
+    fresh = jnp.transpose(acc_ref[...]) + squares * (1.0 / feature)
     rates = rate(jnp.where(lane < MOVES, fresh, 1.0))
     old_ref[...] = jnp.transpose(fresh)
-    for k in range(MOVES):
-        fetch(k).wait()
-    for k in range(MOVES):
-        weights = out_ref[to_ref[k], pl.ds(0, block), :]
-        out_ref[to_ref[k], pl.ds(0, block), :] = weights - lane_of(rates, k) * sums_ref[spans[k], :]
-        out_ref[to_ref[k], pl.ds(block, 1), :] = old_ref[pl.ds(k, 1), :]
-
-
-def leave(came_from, go_to, table, acc, got, peers, total, cap):
-    blocks, block, feature = table.shape
+    sends = []
+    for k in range(MOVES):
+        out_ref[k, pl.ds(block, 1), :] = old_ref[pl.ds(k, 1), :]
+        out_ref[k, pl.ds(0, block), :] = table_ref[k] - lane_of(rates, k) * sums_ref[spans[k], :]
+        sends.append(pltpu.make_async_copy(out_ref.at[k], out_hbm.at[to_ref[k]], sems.at[k]))
+        sends[-1].start()
+    for send in sends:
+        send.wait()
+
+
+def leave(came_from, go_to, table, acc, got, peers, total, cap, rows):
+    block, feature = table.shape[1:]
     vm = pl.BlockSpec(memory_space=VM)
     sm = pl.BlockSpec(memory_space=SM)
     names = (total * 2 * cap // LANES, LANES)
     return pl.pallas_call(
-        lambda *refs: leave_kernel(*refs, total=total, cap=cap),
+        lambda *refs: leave_kernel(*refs, total=total, cap=cap, rows=rows),
         out_shape=(
             jax.ShapeDtypeStruct(names, jnp.int32),
             jax.ShapeDtypeStruct((peers, block + 8, feature), jnp.float32),
         ),
-        in_specs=[sm, sm, pl.BlockSpec(memory_space=pl.ANY), vm, vm],
-        out_specs=(vm, vm),
+        in_specs=[sm, sm, vm, vm, vm],
+        out_specs=(vm, pl.BlockSpec(memory_space=pltpu.HBM)),
         scratch_shapes=[
-            VM((blocks * block + 8, feature), jnp.float32),
+            VM((MOVES, block + 8, feature), jnp.float32),
+            VM((rows + 8, feature), jnp.float32),
             VM((LANES, LANES), jnp.float32),
             VM(names, jnp.int32),
             SM(names, jnp.int32),
             pltpu.SemaphoreType.DMA((MOVES + 1,)),
         ],
-        compiler_params=pltpu.CompilerParams(vmem_limit_bytes=20 * MIB),
+        compiler_params=pltpu.CompilerParams(vmem_limit_bytes=ALL_VMEM - LEAVE_ROOM),
         name="leave",
     )(came_from, go_to, table, acc, got)
 
@@ -293,19 +325,23 @@
     )(names, slots, table, acc, got)
 
 
-def arrive_kernel(peers_ref, slots_ref, got_ref, second_ref, stayed_ref, accstay_ref, out_ref, acc_ref, buf_ref, old_ref, sems):
+def arrive_kernel(peers_ref, slots_ref, got_hbm, second_ref, stayed_ref, accstay_ref, out_ref, acc_ref, got_ref, buf_ref, old_ref, sems):
+    takes = [pltpu.make_async_copy(got_hbm.at[peers_ref[k]], got_ref.at[k], sems.at[k]) for k in range(MOVES)]
+    for take in takes:
+        take.start()
     block, feature = stayed_ref.shape[1:]
     lane = iota((block, LANES), 1)
-    for k in range(MOVES):
-        old_ref[pl.ds(k, 1), :] = got_ref[peers_ref[k], pl.ds(block, 1), :]
     squares = jnp.zeros((block, LANES), jnp.float32)
     for k in range(MOVES):
         squares = jnp.where(lane == k, square_sums(second_ref[k]), squares)
+    for k in range(MOVES):
+        takes[k].wait()
+        old_ref[pl.ds(k, 1), :] = got_ref[k, pl.ds(block, 1), :]
     fresh = jnp.transpose(old_ref[...]) + squares * (1.0 / feature)
     rates = rate(jnp.where(lane < MOVES, fresh, 1.0))
     copies = []
     for k in range(MOVES):
-        buf_ref[k] = got_ref[peers_ref[k], pl.ds(0, block), :] - lane_of(rates, k) * second_ref[k]
+        buf_ref[k] = got_ref[k, pl.ds(0, block), :] - lane_of(rates, k) * second_ref[k]
         copies.append(pltpu.make_async_copy(buf_ref.at[k], out_ref.at[slots_ref[k]], sems.at[k]))
         copies[-1].start()
     old_ref[...] = jnp.transpose(fresh)
@@ -320,22 +356,23 @@
     blocks, block, feature = stayed.shape
     vm = pl.BlockSpec(memory_space=VM)
     sm = pl.BlockSpec(memory_space=SM)
-    hbm = pl.BlockSpec(memory_space=pl.ANY)
+    hbm = pl.BlockSpec(memory_space=pltpu.HBM)
     return pl.pallas_call(
         arrive_kernel,
         out_shape=(
             jax.ShapeDtypeStruct(stayed.shape, jnp.float32),
             jax.ShapeDtypeStruct(accstay.shape, jnp.float32),
         ),
-        in_specs=[sm, sm, vm, vm, hbm, vm],
+        in_specs=[sm, sm, hbm, vm, hbm, vm],
         out_specs=(hbm, vm),
         scratch_shapes=[
+            VM((MOVES,) + got.shape[1:], jnp.float32),
             VM((MOVES, block, feature), jnp.float32),
             VM((LANES, LANES), jnp.float32),
             pltpu.SemaphoreType.DMA((MOVES,)),
         ],
         input_output_aliases={4: 0},
-        compiler_params=pltpu.CompilerParams(vmem_limit_bytes=12 * MIB),
+        compiler_params=pltpu.CompilerParams(vmem_limit_bytes=ALL_VMEM),
         name="arrive",
     )(peers, slots, got, second, stayed, accstay)
 
@@ -356,7 +393,7 @@
     rows = grads_one.shape[0]
     cap = 2 * rows // total
 
-    slot_table = new_slot.reshape(-1, LANES).T
+    slot_table = new_slot.reshape(-1, LANES)
     outgoing = pack(ids_one.reshape(1, rows), ids_two.reshape(1, rows), slot_table, grads_one, grads_two, total, blocks, cap)
     got = lax.all_to_all(outgoing, ("table", "row"), split_axis=0, concat_axis=0, tiled=True)
 
@@ -368,7 +405,8 @@
     slots = jnp.sum(jnp.where(to_me, here - device * blocks + 1, 0), axis=1)
     from_peer, slots = listed(slots > 0, (peer, slots - 1))
 
-    names, moving = leave(came_from, go_to, table, accumulator, got, peers, total, cap)
+    gone, old = fetch(came_from, table, accumulator)
+    names, moving = leave(came_from, go_to, gone, old, got, peers, total, cap, blocks * block)
     moved = lax.all_to_all(moving, "row", split_axis=0, concat_axis=0, tiled=True)
     stayed, accstay, second = stay(names, slots, table, accumulator, got, total, cap)
     return arrive(from_peer, slots, moved, second, stayed, accstay)

time: 109 us -> 97.9 us (0.90)
  local copies, waits for them, and re-layouts: 13 us -> 4.73 us
  waiting for transfers between devices: 38 us -> 34.1 us
    unnamed x20 -> x12, local copies, waits for them, and re-layouts: 11.7 us -> 4.31 us
    all_to_all x1, waiting for transfers between devices: 7.46 us -> 5.44 us  [on_device(): lax.all_to_all(moving, 'row', split_axis=0, concat_axis=0, tiled=True)]
    all_to_all x1, waiting for transfers between devices: 30.5 us -> 28.7 us  [on_device(): lax.all_to_all(outgoing, ('table', 'row'), split_axis=0, concat_axis=0, t...]
    pallas_call x1, Pallas kernels: 9.55 us -> 8.04 us  [pack(): pl.pallas_call(lambda *refs: pack_kernel(*refs, total=total, blocks=block...]
    pallas_call x1 -> x2, Pallas kernels: 6.1 us -> 7.54 us  [the longest x1 5.73 us: leave(): pl.pallas_call(lambda *refs: leave_kernel(*refs, total=total, cap=cap, ro...]
  transfers between devices with their start and end apart: 2 -> 2, of which waited for: 2 -> 2; matrix products, arithmetic and copies ran while one was open for 1% -> 2% of each run, Pallas kernels for 19% -> 23%
where the time goes in v2:
time: 97.9 us; the launch traced here: 97.4 us
  Pallas kernels  40.3 us (41%)
  waiting for transfers between devices  34.1 us (35%)
  starting transfers between devices  16 us (16%)
  local copies, waits for them, and re-layouts  4.73 us (5%)
  other arithmetic  1.48 us (2%)
    all_to_all x1, waiting for transfers between devices, on_device(): lax.all_to_all(outgoing, ('table', 'row'), split_axis=0, concat_axis=0, t...  28.7 us
    pallas_call x1, Pallas kernels, stay(): pl.pallas_call(lambda *refs: stay_kernel(*refs, total=total, cap=cap, blo...  20.5 us
    all_to_all x1, starting transfers between devices, on_device(): lax.all_to_all(outgoing, ('table', 'row'), split_axis=0, concat_axis=0, t...  11.2 us
    pallas_call x1, Pallas kernels, pack(): pl.pallas_call(lambda *refs: pack_kernel(*refs, total=total, blocks=block...  8.04 us
    pallas_call x1, Pallas kernels, leave(): pl.pallas_call(lambda *refs: leave_kernel(*refs, total=total, cap=cap, ro...  5.73 us
    all_to_all x1, waiting for transfers between devices, on_device(): lax.all_to_all(moving, 'row', split_axis=0, concat_axis=0, tiled=True)  5.44 us
    all_to_all x1, starting transfers between devices, on_device(): lax.all_to_all(moving, 'row', split_axis=0, concat_axis=0, tiled=True)  4.8 us
    unnamed x12, local copies, waits for them, and re-layouts  4.31 us
  transfers between devices with their start and end apart: 2, of which 2 were waited for; matrix products, arithmetic and copies ran while one was open for 2% of the time, Pallas kernels for 23%

profile of v2, /device:TPU:0, one launch (start us, length us, event | category | flops | bytes accessed | tf_op | source)
XLA Modules:
  0.0 97.4 jit_solution(7179132279871023896)
XLA Ops:
  0.6 8.0 %pack.1 = f32[4224,1,128]{2,1,0:T(1,128)} custom-call(s32[1,1024]{1,0:T(1,128)} %bitcast.8, s32[1,1024]{1,0:T(1,128)} %bitcast.9, s32[96,128]{1,0:T(8,128)} %bitcast.7, f32[1024,128]{1,0:T(8,128)} %refs_3_.2, f32[1024,128]{1,0:T(8,128)} %refs_4_.1), custom_call_target="tpu_custom_call" | custom-call | tf_op jit(solution)/shard_map/pack/pallas_call | solution.py:109
  8.7 0.0 copy-start.5
  8.7 0.0 copy-start.2
  8.7 11.2 %all-to-all-start = ((f32[4224,1,128]{2,1,0:T(1,128)}), f32[4224,1,128]{2,1,0:T(1,128)S(1)}, u32[]{:S(2)}, u32[]{:S(2)}) async-start(f32[4224,1,128]{2,1,0:T(1,128)} %pack.1), calls=%async_computation | async-start | bytes 4325376 | tf_op jit(solution)/shard_map/all_to_all | solution.py:398
  19.9 0.0 copy-done.5
  19.9 0.1 convert_bitcast_fusion
  20.0 0.1 copy.15
  20.1 0.1 reduce-window.17
  20.2 0.1 add_reduce_fusion
  20.4 0.1 select_reduce_fusion.1
  20.5 0.0 copy-done.2
  20.5 1.8 %fetch.1 = (f32[12,128,128]{2,1,0:T(8,128)S(1)}, f32[128,128]{1,0:T(8,128)S(1)}) custom-call(s32[12]{0:T(128)S(1)} %get-tuple-element.17.from_ref.refs_0_, f32[96,128,128]{2,1,0:T(8,128)} %refs_2_.1, f32[96,128]{1,0:T(8,128)S(1)} %copy-done.2), custom_call_target="tpu_custom_call" | custom-call | tf_op jit(solution)/shard_map/fetch/pallas_call | solution.py:191
  22.3 28.7 %all-to-all-done.refs_4_ = f32[4224,1,128]{2,1,0:T(1,128)S(1)} async-done(((f32[4224,1,128]{2,1,0:T(1,128)}), f32[4224,1,128]{2,1,0:T(1,128)S(1)}, u32[]{:S(2)}, u32[]{:S(2)}) %all-to-all-start) | async-done | bytes 2162720 | tf_op jit(solution)/shard_map/all_to_all | solution.py:398
  51.0 5.7 %leave.1 = (s32[32,128]{1,0:T(8,128)S(1)}, f32[32,136,128]{2,1,0:T(8,128)}) custom-call(s32[12]{0:T(128)S(1)} %get-tuple-element.17.from_ref.refs_0_, s32[12]{0:T(128)S(1)} %get-tuple-element.16.refs_1_, f32[12,128,128]{2,1,0:T(8,128)S(1)} %get-tuple-element.9.refs_2_, f32[128,128]{1,0:T(8,128)S(1)} %get-tuple-element.10.refs_3_, ...), custom_call_target="tpu_custom_call" | custom-call | tf_op jit(solution)/shard_map/leave/pallas_call | solution.py:235
  56.7 4.8 %all-to-all-start.1 = ((f32[32,136,128]{2,1,0:T(8,128)}), f32[32,136,128]{2,1,0:T(8,128)}, u32[]{:S(2)}, u32[]{:S(2)}) async-start(f32[32,136,128]{2,1,0:T(8,128)} %get-tuple-element.11), calls=%async_computation.1 | async-start | bytes 4456448 | tf_op jit(solution)/shard_map/all_to_all | solution.py:410
  61.6 0.1 and.44
  61.7 0.1 div.18
  61.7 0.1 add.44
  61.8 0.2 select_reduce_fusion
  62.0 0.1 copy.14
  62.1 0.1 reduce-window.16
  62.2 0.1 add_reduce_fusion.1
  62.3 0.6 select_reduce_fusion.3
  62.9 0.0 copy-start.4
  62.9 0.0 copy-start
  62.9 2.8 %copy-done = f32[96,128,128]{2,1,0:T(8,128)S(1)} copy-done((f32[96,128,128]{2,1,0:T(8,128)S(1)}, f32[96,128,128]{2,1,0:T(8,128)}, u32[]{:S(2)}) %copy-start) | copy-done | bytes 6291480
  65.7 20.5 %stay.1 = (f32[96,128,128]{2,1,0:T(8,128)}, f32[96,128]{1,0:T(8,128)S(1)}, f32[12,128,128]{2,1,0:T(8,128)S(1)}) custom-call(s32[32,128]{1,0:T(8,128)S(1)} %get-tuple-element.12.refs_0_, s32[12]{0:T(128)S(1)} %get-tuple-element.18.refs_1_.slots_ref, f32[96,128,128]{2,1,0:T(8,128)S(1)} %copy-done, f32[96,128]{1,0:T(8,128)S(1)} %copy-done.2, ...), custom_call_target="tpu_custom_call" | custom-call | tf_op jit(solution)/shard_map/stay/pallas_call | solution.py:308
  86.1 0.0 copy-done.4
  86.2 0.9 copy-done.1
  87.0 0.6 copy-done.3
  87.7 5.4 %all-to-all-done.1.got_hbm = f32[32,136,128]{2,1,0:T(8,128)} async-done(((f32[32,136,128]{2,1,0:T(8,128)}), f32[32,136,128]{2,1,0:T(8,128)}, u32[]{:S(2)}, u32[]{:S(2)}) %all-to-all-start.1) | async-done | bytes 2228256 | tf_op jit(solution)/shard_map/all_to_all | solution.py:410
  93.1 4.3 %arrive.1 = (f32[96,128,128]{2,1,0:T(8,128)}, f32[96,128]{1,0:T(8,128)}) custom-call(s32[12]{0:T(128)} %get-tuple-element.19.peers_ref, s32[12]{0:T(128)} %copy-done.4, f32[32,136,128]{2,1,0:T(8,128)} %all-to-all-done.1.got_hbm, f32[12,128,128]{2,1,0:T(8,128)} %copy-done.1, ...), custom_call_target="tpu_custom_call", output_to_operand_aliasing={{0}: (4, {})} | custom-call | tf_op jit(solution)/shard_map/arrive/pallas_call | solution.py:360
  (8 shorter events, 0.1 us)
Async XLA Ops:
  8.7 11.2 %copy-start.5 = (s32[12288]{0:T(1024)S(1)}, s32[12288]{0:T(1024)}, u32[]{:S(2)}) copy-start(s32[12288]{0:T(1024)} %param.13) | copy-start | bytes 147460
  8.7 11.8 %copy-start.2 = (f32[96,128]{1,0:T(8,128)S(1)}, f32[96,128]{1,0:T(8,128)}, u32[]{:S(2)}) copy-start(f32[96,128]{1,0:T(8,128)} %refs_3_.3) | copy-start | bytes 147460
  8.7 42.3 %all-to-all-start = ((f32[4224,1,128]{2,1,0:T(1,128)}), f32[4224,1,128]{2,1,0:T(1,128)S(1)}, u32[]{:S(2)}, u32[]{:S(2)}) async-start(f32[4224,1,128]{2,1,0:T(1,128)} %pack.1), calls=%async_computation | async-start | bytes 4325376 | tf_op jit(solution)/shard_map/all_to_all | solution.py:398
  56.7 36.4 %all-to-all-start.1 = ((f32[32,136,128]{2,1,0:T(8,128)}), f32[32,136,128]{2,1,0:T(8,128)}, u32[]{:S(2)}, u32[]{:S(2)}) async-start(f32[32,136,128]{2,1,0:T(8,128)} %get-tuple-element.11), calls=%async_computation.1 | async-start | bytes 4456448 | tf_op jit(solution)/shard_map/all_to_all | solution.py:410
  62.9 23.2 %copy-start.4 = (s32[12]{0:T(128)}, s32[12]{0:T(128)S(1)}, u32[]{:S(2)}) copy-start(s32[12]{0:T(128)S(1)} %get-tuple-element.18.refs_1_.slots_ref) | copy-start | bytes 148
  62.9 2.8 %copy-start = (f32[96,128,128]{2,1,0:T(8,128)S(1)}, f32[96,128,128]{2,1,0:T(8,128)}, u32[]{:S(2)}) copy-start(f32[96,128,128]{2,1,0:T(8,128)} %refs_2_.1) | copy-start | bytes 18874372
  86.2 0.9 copy-start.1
  87.0 0.6 copy-start.3

commit v3 on v2

v3 whole, which is shorter than its diff:
```python
import jax
import jax.numpy as jnp
from jax import lax
from jax.experimental import pallas as pl
from jax.experimental.pallas import tpu as pltpu
from jax.sharding import PartitionSpec as P

LEARN = 0.5
EPSILON = 1e-08
LANES = 128
MOVES = 12
VM = pltpu.VMEM
SM = pltpu.SMEM
ALL_VMEM = 67043328
ROOM = 14000000


def iota(shape, dim):
    return lax.broadcasted_iota(jnp.int32, shape, dim)


def dot(a, b, contract):
    return lax.dot_general(a, b, ((contract[:1], contract[1:]), ((), ())), preferred_element_type=jnp.float32)


def lookup(which_ref, indices):
    high, low = which_ref.shape
    pick = (iota((high, indices.shape[1]), 0) == (indices >> 7)).astype(jnp.bfloat16)
    found = jnp.zeros((low, indices.shape[1]), jnp.float32)
    table = jnp.concatenate([which_ref[...].astype(jnp.float32), jnp.zeros((low - high, low), jnp.float32)], axis=0)
    table = jnp.transpose(table)[:, :high].astype(jnp.int32)
    for part, scale in ((table >> 7, 128.0), (table & 127, 1.0)):
        found += dot(part.astype(jnp.float32).astype(jnp.bfloat16), pick, (1, 0)) * scale
    here = iota(found.shape, 0) == (indices & 127)
    return jnp.sum(jnp.where(here, found, 0.0), axis=0, keepdims=True).astype(jnp.int32)


def pack_kernel(one_ids, two_ids, slot_hbm, one_hbm, two_hbm, out_hbm, one_ref, two_ref, ids_ref, ids2_ref, slot_ref, place_v, place2_v, place_s, place2_s, names_v, out_ref, sems, *, blocks, cap):
    total, stride = out_ref.shape[:2]
    rows = one_ref.shape[0]
    chunks = rows // LANES
    pairs = ((one_ids, ids_ref), (two_ids, ids2_ref), (slot_hbm, slot_ref), (one_hbm, one_ref), (two_hbm, two_ref))
    copies = [pltpu.make_async_copy(src, dst, sems.at[n]) for n, (src, dst) in enumerate(pairs)]
    for copy in copies:
        copy.start()
    for copy in copies[:3]:
        copy.wait()
    ids = ids_ref[...]
    ids2 = ids2_ref[...]
    held = ids >> 7
    leaving = lookup(slot_ref, held) != held
    block_slots = (held, lookup(slot_ref, ids2 >> 7))
    inner = (ids & 127, ids2 & 127)
    upper = jnp.where(iota((LANES, 2 * LANES), 0) < iota((LANES, 2 * LANES), 1), 1.0, 0.0).astype(jnp.bfloat16)
    everywhere = jnp.ones((LANES, LANES), jnp.bfloat16)
    lane_slot = iota((LANES, LANES), 0) & (2 * cap - 1)
    high = jnp.zeros((total, LANES), jnp.float32)
    low = jnp.zeros((total, LANES), jnp.float32)
    places = ((place_v, place_s), (place2_v, place2_s))
    to_scalar = [pltpu.make_async_copy(v, s, sems.at[5 + n]) for n, (v, s) in enumerate(places)]
    for step in range(2):
        slot = block_slots[step]
        owner = (slot * 43691) >> 22
        named = (slot - owner * blocks) * LANES + inner[step] + 1
        carry = jnp.zeros((total, LANES), jnp.float32)
        carry_first = jnp.zeros((total, LANES), jnp.float32)
        spots = [slice(c * LANES, (c + 1) * LANES) for c in range(chunks)]
        if step == 0:
            firsts = jnp.zeros((total, LANES), jnp.float32)
            for at in spots:
                mine = (iota((total, LANES), 0) == owner[:, at]) & leaving[:, at]
                firsts += dot(jnp.where(mine, 1.0, 0.0).astype(jnp.bfloat16), everywhere, (1, 0))
        for c, at in enumerate(spots):
            own = owner[:, at]
            name = named[:, at]
            mine = iota((total, LANES), 0) == own
            counted = dot(jnp.where(mine, 1.0, 0.0).astype(jnp.bfloat16), upper, (1, 0))
            before = counted[:, :LANES] + carry
            carry = carry + counted[:, LANES:]
            if step == 0:
                early = leaving[:, at]
                counted = dot(jnp.where(mine & early, 1.0, 0.0).astype(jnp.bfloat16), upper, (1, 0))
                before_first = counted[:, :LANES] + carry_first
                carry_first = carry_first + counted[:, LANES:]
                before = jnp.where(early, before_first, firsts + before - before_first)
            within = jnp.sum(jnp.where(mine, before, 0.0), axis=0, keepdims=True).astype(jnp.int32) + step * cap
            places[step][0][pl.ds(c, 1), :] = own * stride + within
            where = jnp.where(lane_slot == within, 1.0, 0.0).astype(jnp.bfloat16)
            high += dot(jnp.where(mine, (name >> 7).astype(jnp.float32), 0.0).astype(jnp.bfloat16), where, (1, 1))
            low += dot(jnp.where(mine, (name & 127).astype(jnp.float32), 0.0).astype(jnp.bfloat16), where, (1, 1))
        to_scalar[step].start()
    names_v[...] = high * 128.0 + low
    flat = out_ref.reshape(total * stride, 1, LANES)

    def move(src, place):
        def chunk(c, _):
            for g in range(LANES // 8):
                tile = src[pl.ds(c * LANES + g * 8, 8), :]
                for j in range(8):
                    flat[place[c, g * 8 + j]] = tile[j : j + 1, :]
            return 0

        lax.fori_loop(0, chunks, chunk, 0)

    to_scalar[0].wait()
    copies[3].wait()
    move(one_ref, place_s)
    first = pltpu.make_async_copy(out_ref.at[:, pl.ds(0, cap)], out_hbm.at[:, pl.ds(0, cap)], sems.at[7])
    first.start()

    def names(d, _):
        base = d * 8
        tile = names_v[pl.ds(base, 8), :]
        for j in range(8):
            out_ref[base + j, stride - 1] = tile[j : j + 1, :]
        return 0

    lax.fori_loop(0, total // 8, names, 0, unroll=2)
    to_scalar[1].wait()
    copies[4].wait()
    move(two_ref, place2_s)
    second = pltpu.make_async_copy(out_ref.at[:, pl.ds(cap, cap + 1)], out_hbm.at[:, pl.ds(cap, cap + 1)], sems.at[8])
    second.start()
    first.wait()
    second.wait()


def pack(one_ids, two_ids, slots, one, two, total, blocks, cap):
    rows, feature = one.shape
    hbm = pl.BlockSpec(memory_space=pltpu.HBM)
    message = (total, 2 * cap + 1, 1, feature)
    place = (rows // LANES, LANES)
    return pl.pallas_call(
        lambda *refs: pack_kernel(*refs, blocks=blocks, cap=cap),
        out_shape=jax.ShapeDtypeStruct(message, jnp.float32),
        in_specs=[hbm] * 5,
        out_specs=hbm,
        scratch_shapes=[
            VM((rows, feature), jnp.float32),
            VM((rows, feature), jnp.float32),
            VM((1, rows), jnp.int32),
            VM((1, rows), jnp.int32),
            VM(slots.shape, jnp.int32),
            VM(place, jnp.int32),
            VM(place, jnp.int32),
            SM(place, jnp.int32),
            SM(place, jnp.int32),
            VM((total, LANES), jnp.float32),
            VM(message, jnp.float32),
            pltpu.SemaphoreType.DMA((9,)),
        ],
        compiler_params=pltpu.CompilerParams(vmem_limit_bytes=ALL_VMEM),
        name="pack",
    )(one_ids, two_ids, slots, one, two)


def read_names(got_ref, names_v, copy, *, dump):
    total, stride = got_ref.shape[:2]
    width = stride - 1
    per = LANES // width
    group = iota((1, LANES), 1) // width
    for a in range(total // per):
        row = got_ref[a * per, width]
        for k in range(1, per):
            row = jnp.where(group == k, got_ref[a * per + k, width], row)
        names_v[pl.ds(a, 1), :] = row.astype(jnp.int32)
    named = names_v[...]
    named = jnp.where(named > 0, named - 1, dump)
    names_v[...] = named
    copy.start()
    return named


def add_rows(names_s, got_ref, sums_refs, *, offset, count):
    total, stride = got_ref.shape[:2]
    width = stride - 1
    per = LANES // width

    def step(a, _):
        for k in range(per):
            sums_ref = sums_refs[k % len(sums_refs)]
            rows = [names_s[a, k * width + offset + j] for j in range(count)]
            new = [sums_ref[pl.ds(r, 1), :] + got_ref[a * per + k, offset + j] for j, r in enumerate(rows)]
            for r, value in zip(rows, new):
                sums_ref[pl.ds(r, 1), :] = value
        return 0

    lax.fori_loop(0, total // per, step, 0)


def square_sums(block):
    return jnp.sum(block * block, axis=1, keepdims=True)


def rate(accums):
    return LEARN / (jnp.sqrt(accums) + EPSILON)


def lane_of(columns, k):
    return columns[:, k : k + 1]


def fetch_kernel(from_ref, table_ref, acc_ref, out_ref, old_ref, sems):
    copies = [pltpu.make_async_copy(table_ref.at[from_ref[k]], out_ref.at[k], sems.at[k]) for k in range(MOVES)]
    for copy in copies:
        copy.start()
    old_ref[...] = jnp.zeros_like(old_ref)
    for k in range(MOVES):
        old_ref[pl.ds(k, 1), :] = acc_ref[pl.ds(from_ref[k], 1), :]
    for copy in copies:
        copy.wait()


def fetch(came_from, table, acc):
    vm = pl.BlockSpec(memory_space=VM)
    hbm = pl.BlockSpec(memory_space=pltpu.HBM)
    return pl.pallas_call(
        fetch_kernel,
        out_shape=(
            jax.ShapeDtypeStruct((MOVES,) + table.shape[1:], jnp.float32),
            jax.ShapeDtypeStruct((LANES, LANES), jnp.float32),
        ),
        in_specs=[pl.BlockSpec(memory_space=SM), hbm, vm],
        out_specs=(vm, vm),
        scratch_shapes=[pltpu.SemaphoreType.DMA((MOVES,))],
        compiler_params=pltpu.CompilerParams(vmem_limit_bytes=ALL_VMEM - ROOM),
        name="fetch",
    )(came_from, table, acc)


ROUND = 4


def leave_kernel(from_ref, to_ref, table_ref, acc_ref, got_ref, names_out, out_hbm, out_ref, even_ref, odd_ref, old_ref, names_v, names_s, sems, *, cap, rows):
    block, feature = table_ref.shape[1:]
    spans = [pl.ds(pl.multiple_of(from_ref[k] * block, block), block) for k in range(MOVES)]
    to_scalar = pltpu.make_async_copy(names_v, names_s, sems.at[MOVES])
    named = read_names(got_ref, names_v, to_scalar, dump=rows)
    names_out[...] = named
    at = iota(named.shape, 1) & (2 * cap - 1)
    goes = jnp.zeros(named.shape, jnp.bool_)
    for k in range(MOVES):
        goes = goes | ((named >> 7) == from_ref[k])
    needed = jnp.max(jnp.where(goes & (at < cap), at + 1, 0))
    for k in range(MOVES):
        even_ref[spans[k], :] = jnp.zeros((block, feature), jnp.float32)
        odd_ref[spans[k], :] = jnp.zeros((block, feature), jnp.float32)
    to_scalar.wait()

    def some(r, _):
        add_rows(names_s, got_ref, (even_ref, odd_ref), offset=r * ROUND, count=ROUND)
        return 0

    lax.fori_loop(0, (needed + ROUND - 1) // ROUND, some, 0)
    lane = iota((block, LANES), 1)
    squares = jnp.zeros((block, LANES), jnp.float32)
    for k in range(MOVES):
        gradient = even_ref[spans[k], :] + odd_ref[spans[k], :]
        even_ref[spans[k], :] = gradient
        squares = jnp.where(lane == k, square_sums(gradient), squares)
    fresh = jnp.transpose(acc_ref[...]) + squares * (1.0 / feature)
    rates = rate(jnp.where(lane < MOVES, fresh, 1.0))
    old_ref[...] = jnp.transpose(fresh)
    sends = []
    for k in range(MOVES):
        out_ref[k, pl.ds(block, 1), :] = old_ref[pl.ds(k, 1), :]
        out_ref[k, pl.ds(0, block), :] = table_ref[k] - lane_of(rates, k) * even_ref[spans[k], :]
        sends.append(pltpu.make_async_copy(out_ref.at[k], out_hbm.at[to_ref[k]], sems.at[k]))
        sends[-1].start()
    for send in sends:
        send.wait()


def leave(came_from, go_to, table, acc, got, peers, cap, rows):
    block, feature = table.shape[1:]
    vm = pl.BlockSpec(memory_space=VM)
    sm = pl.BlockSpec(memory_space=SM)
    names = (got.shape[0] * 2 * cap // LANES, LANES)
    return pl.pallas_call(
        lambda *refs: leave_kernel(*refs, cap=cap, rows=rows),
        out_shape=(
            jax.ShapeDtypeStruct(names, jnp.int32),
            jax.ShapeDtypeStruct((peers, block + 8, feature), jnp.float32),
        ),
        in_specs=[sm, sm, vm, vm, vm],
        out_specs=(vm, pl.BlockSpec(memory_space=pltpu.HBM)),
        scratch_shapes=[
            VM((MOVES, block + 8, feature), jnp.float32),
            VM((rows + 8, feature), jnp.float32),
            VM((rows + 8, feature), jnp.float32),
            VM((LANES, LANES), jnp.float32),
            VM(names, jnp.int32),
            SM(names, jnp.int32),
            pltpu.SemaphoreType.DMA((MOVES + 1,)),
        ],
        compiler_params=pltpu.CompilerParams(vmem_limit_bytes=ALL_VMEM - ROOM),
        name="leave",
    )(came_from, go_to, table, acc, got)


def stay_kernel(names_ref, slots_ref, table_ref, acc_ref, got_ref, out_ref, accout_ref, arrive_ref, squares_ref, one_ref, two_ref, rates_ref, *, cap, blocks):
    i = pl.program_id(0)
    each, block, feature = table_ref.shape

    @pl.when(i == 0)
    def _():
        def clear(b, _):
            at = pl.ds(pl.multiple_of(b * block, block), block)
            one_ref[at, :] = jnp.zeros((block, feature), jnp.float32)
            two_ref[at, :] = jnp.zeros((block, feature), jnp.float32)
            return 0

        lax.fori_loop(0, blocks, clear, 0)
        add_rows(names_ref, got_ref, (one_ref,), offset=0, count=cap)
        add_rows(names_ref, got_ref, (two_ref,), offset=cap, count=cap)
        lane = iota((block, LANES), 1)

        def squares(g, sums):
            sums = list(sums)
            for k in range(4):
                b = g * 4 + k
                at = pl.ds(pl.multiple_of(b * block, block), block)
                for n, ref in enumerate((one_ref, two_ref)):
                    sums[n] = jnp.where(lane == b, square_sums(ref[at, :]), sums[n])
            return tuple(sums)

        zero = jnp.zeros((block, LANES), jnp.float32)
        first, second = lax.fori_loop(0, blocks // 4, squares, (zero, zero))
        old = jnp.concatenate([acc_ref[...], jnp.ones((LANES - blocks, LANES), jnp.float32)], axis=0)
        fresh = jnp.transpose(old) + first * (1.0 / feature)
        rates_ref[0] = rate(fresh)
        fresh = fresh + second * (1.0 / feature)
        rates_ref[1] = rate(fresh)
        accout_ref[...] = jnp.transpose(fresh)[:blocks, :]
        arriving = zero
        for k in range(MOVES):
            at = pl.ds(pl.multiple_of(slots_ref[k] * block, block), block)
            arrive_ref[k] = two_ref[at, :]
            arriving = jnp.where(lane == k, square_sums(two_ref[at, :]), arriving)
        squares_ref[...] = arriving

    turn = (LANES - each * i) % LANES
    one_rate = pltpu.roll(rates_ref[0], turn, 1)
    two_rate = pltpu.roll(rates_ref[1], turn, 1)
    for k in range(each):
        at = pl.ds(pl.multiple_of((i * each + k) * block, block), block)
        weights = table_ref[k] - lane_of(one_rate, k) * one_ref[at, :]
        out_ref[k] = weights - lane_of(two_rate, k) * two_ref[at, :]


def stay(names, slots, table, acc, got, cap, each=8):
    blocks, block, feature = table.shape
    vm = pl.BlockSpec(memory_space=VM)
    sm = pl.BlockSpec(memory_space=SM)
    piece = pl.BlockSpec((each, block, feature), lambda i: (i, 0, 0))
    return pl.pallas_call(
        lambda *refs: stay_kernel(*refs, cap=cap, blocks=blocks),
        grid=(blocks // each,),
        out_shape=(
            jax.ShapeDtypeStruct(table.shape, jnp.float32),
            jax.ShapeDtypeStruct(acc.shape, jnp.float32),
            jax.ShapeDtypeStruct((MOVES, block, feature), jnp.float32),
            jax.ShapeDtypeStruct((LANES, LANES), jnp.float32),
        ),
        in_specs=[sm, sm, piece, vm, vm],
        out_specs=(piece, vm, vm, vm),
        scratch_shapes=[
            VM((blocks * block + 8, feature), jnp.float32),
            VM((blocks * block + 8, feature), jnp.float32),
            VM((2, LANES, LANES), jnp.float32),
        ],
        compiler_params=pltpu.CompilerParams(vmem_limit_bytes=ALL_VMEM - ROOM),
        name="stay",
    )(names, slots, table, acc, got)


def arrive_kernel(peers_ref, slots_ref, got_hbm, second_hbm, squares_hbm, stayed_ref, accstay_hbm, out_ref, acc_hbm, got_ref, second_ref, squares_ref, acc_ref, buf_ref, old_ref, sems):
    block, feature = stayed_ref.shape[1:]
    takes = [pltpu.make_async_copy(got_hbm.at[peers_ref[k]], got_ref.at[k], sems.at[k]) for k in range(MOVES)]
    pairs = ((squares_hbm, squares_ref), (accstay_hbm, acc_ref), (second_hbm, second_ref))
    rest = [pltpu.make_async_copy(src, dst, sems.at[MOVES + n]) for n, (src, dst) in enumerate(pairs)]
    for take in takes + rest:
        take.start()
    lane = iota((block, LANES), 1)
    for k in range(MOVES):
        takes[k].wait()
        old_ref[pl.ds(k, 1), :] = got_ref[k, pl.ds(block, 1), :]
    rest[0].wait()
    fresh = jnp.transpose(old_ref[...]) + squares_ref[...] * (1.0 / feature)
    rates = rate(jnp.where(lane < MOVES, fresh, 1.0))
    old_ref[...] = jnp.transpose(fresh)
    rest[1].wait()
    for k in range(MOVES):
        acc_ref[pl.ds(slots_ref[k], 1), :] = old_ref[pl.ds(k, 1), :]
    copies = [pltpu.make_async_copy(acc_ref, acc_hbm, sems.at[MOVES])]
    copies[0].start()
    rest[2].wait()
    for k in range(MOVES):
        buf_ref[k] = got_ref[k, pl.ds(0, block), :] - lane_of(rates, k) * second_ref[k]
        copies.append(pltpu.make_async_copy(buf_ref.at[k], out_ref.at[slots_ref[k]], sems.at[k]))
        copies[-1].start()
    for copy in copies:
        copy.wait()


def arrive(peers, slots, got, second, squares, stayed, accstay):
    blocks, block, feature = stayed.shape
    sm = pl.BlockSpec(memory_space=SM)
    hbm = pl.BlockSpec(memory_space=pltpu.HBM)
    return pl.pallas_call(
        arrive_kernel,
        out_shape=(
            jax.ShapeDtypeStruct(stayed.shape, jnp.float32),
            jax.ShapeDtypeStruct(accstay.shape, jnp.float32),
        ),
        in_specs=[sm, sm, hbm, hbm, hbm, hbm, hbm],
        out_specs=(hbm, hbm),
        scratch_shapes=[
            VM((MOVES,) + got.shape[1:], jnp.float32),
            VM(second.shape, jnp.float32),
            VM(squares.shape, jnp.float32),
            VM(accstay.shape, jnp.float32),
            VM((MOVES, block, feature), jnp.float32),
            VM((LANES, LANES), jnp.float32),
            pltpu.SemaphoreType.DMA((MOVES + 3,)),
        ],
        input_output_aliases={5: 0},
        compiler_params=pltpu.CompilerParams(vmem_limit_bytes=ALL_VMEM),
        name="arrive",
    )(peers, slots, got, second, squares, stayed, accstay)


def listed(mask, values):
    position = jnp.cumsum(mask.astype(jnp.int32)) - 1
    hit = mask[None, :] & (position[None, :] == jnp.arange(MOVES, dtype=jnp.int32)[:, None])
    return [jnp.sum(jnp.where(hit, v[None, :], 0), axis=1) for v in values]


def on_device(table, accumulator, grads_one, ids_one, grads_two, ids_two, new_slot):
    blocks, block, feature = table.shape
    peers = lax.axis_size("row")
    total = lax.axis_size("table") * peers
    group = lax.axis_index("table")
    mine = lax.axis_index("row")
    device = group * peers + mine
    rows = grads_one.shape[0]
    cap = 2 * rows // total

    slot_table = new_slot.reshape(-1, LANES)
    outgoing = pack(ids_one.reshape(1, rows), ids_two.reshape(1, rows), slot_table, grads_one, grads_two, total, blocks, cap)
    got = lax.all_to_all(outgoing, ("table", "row"), split_axis=0, concat_axis=0, tiled=True)

    here = lax.dynamic_slice_in_dim(new_slot, group * peers * blocks, peers * blocks).reshape(peers, blocks)
    own = lax.dynamic_slice_in_dim(new_slot, device * blocks, blocks)
    came_from, go_to = listed(own // blocks != device, (jnp.arange(blocks, dtype=jnp.int32), own // blocks % peers))
    peer = jnp.arange(peers, dtype=jnp.int32)
    to_me = (here // blocks == device) & (peer != mine)[:, None]
    slots = jnp.sum(jnp.where(to_me, here - device * blocks + 1, 0), axis=1)
    from_peer, slots = listed(slots > 0, (peer, slots - 1))

    gone, old = fetch(came_from, table, accumulator)
    names, moving = leave(came_from, go_to, gone, old, got, peers, cap, blocks * block)
    moved = lax.all_to_all(moving, "row", split_axis=0, concat_axis=0, tiled=True)
    stayed, accstay, second, squares = stay(names, slots, table, accumulator, got, cap)
    return arrive(from_peer, slots, moved, second, squares, stayed, accstay)


def solution(mesh):
    in_specs = (
        P(("table", "row"), None, None),
        P(("table", "row"), None),
        P(("table", "row"), None),
        P(("table", "row")),
        P(("table", "row"), None),
        P(("table", "row")),
        P(),
    )
    out_specs = (P(("table", "row"), None, None), P(("table", "row"), None))
    return jax.shard_map(
        on_device, mesh=mesh, in_specs=in_specs, out_specs=out_specs, check_vma=False
    )
```

time: 97.9 us -> 95.5 us (0.975)
  local copies, waits for them, and re-layouts: 4.73 us -> 2.56 us
    unnamed x12, local copies, waits for them, and re-layouts: 4.31 us -> 2.14 us
    pallas_call x3, Pallas kernels: 34.2 us -> 35.6 us  [the longest x1 23.5 us: stay(): pl.pallas_call(lambda *refs: stay_kernel(*refs, cap=cap, blocks=blocks),...]
    pallas_call x1, Pallas kernels: 4.26 us -> 3.28 us  [arrive(): pl.pallas_call(arrive_kernel, out_shape=(jax.ShapeDtypeStruct(stayed.shap...]
  transfers between devices with their start and end apart: 2 -> 2, of which waited for: 2 -> 2; matrix products, arithmetic and copies ran while one was open for 2% -> 2% of each run, Pallas kernels for 23% -> 27%
where the time goes in v3:
time: 95.5 us; the launch traced here: 94.7 us
  Pallas kernels  40.7 us (43%)
  waiting for transfers between devices  33.2 us (35%)
  starting transfers between devices  16 us (17%)
  local copies, waits for them, and re-layouts  2.56 us (3%)
  other arithmetic  1.57 us (2%)
    all_to_all x1, waiting for transfers between devices, on_device(): lax.all_to_all(outgoing, ('table', 'row'), split_axis=0, concat_axis=0, t...  28.7 us
    pallas_call x1, Pallas kernels, stay(): pl.pallas_call(lambda *refs: stay_kernel(*refs, cap=cap, blocks=blocks),...  23.5 us
    all_to_all x1, starting transfers between devices, on_device(): lax.all_to_all(outgoing, ('table', 'row'), split_axis=0, concat_axis=0, t...  11.2 us
    pallas_call x1, Pallas kernels, pack(): pl.pallas_call(lambda *refs: pack_kernel(*refs, blocks=blocks, cap=cap),...  7.8 us
    all_to_all x1, starting transfers between devices, on_device(): lax.all_to_all(moving, 'row', split_axis=0, concat_axis=0, tiled=True)  4.8 us
    all_to_all x1, waiting for transfers between devices, on_device(): lax.all_to_all(moving, 'row', split_axis=0, concat_axis=0, tiled=True)  4.5 us
    pallas_call x1, Pallas kernels, leave(): pl.pallas_call(lambda *refs: leave_kernel(*refs, cap=cap, rows=rows), out...  4.29 us
    pallas_call x1, Pallas kernels, arrive(): pl.pallas_call(arrive_kernel, out_shape=(jax.ShapeDtypeStruct(stayed.shap...  3.28 us
  transfers between devices with their start and end apart: 2, of which 2 were waited for; matrix products, arithmetic and copies ran while one was open for 2% of the time, Pallas kernels for 27%

profile of v3, /device:TPU:0, one launch (start us, length us, event | category | flops | bytes accessed | tf_op | source)
XLA Modules:
  0.0 94.7 jit_solution(15145562219768444737)
XLA Ops:
  0.6 7.8 %pack.1 = f32[128,33,1,128]{3,2,1,0:T(1,128)} custom-call(s32[1,1024]{1,0:T(1,128)} %bitcast.8, s32[1,1024]{1,0:T(1,128)} %bitcast.9, s32[96,128]{1,0:T(8,128)} %bitcast.7, f32[1024,128]{1,0:T(8,128)} %refs_3_.2, f32[1024,128]{1,0:T(8,128)} %refs_4_.1), custom_call_target="tpu_custom_call" | custom-call | tf_op jit(solution)/shard_map/pack/pallas_call | solution.py:133
  8.4 0.0 copy-start.5
  8.4 0.0 copy-start.1
  8.5 11.2 %all-to-all-start = ((f32[128,33,1,128]{3,2,1,0:T(1,128)}), f32[128,33,1,128]{3,2,1,0:T(1,128)S(1)}, u32[]{:S(2)}, u32[]{:S(2)}) async-start(f32[128,33,1,128]{3,2,1,0:T(1,128)} %pack.1), calls=%async_computation | async-start | bytes 4325376 | tf_op jit(solution)/shard_map/all_to_all | solution.py:451
  19.7 0.0 copy-done.5
  19.7 0.1 convert_bitcast_fusion
  19.8 0.1 copy.15
  19.9 0.1 reduce-window.17
  20.0 0.1 add_reduce_fusion
  20.1 0.1 select_reduce_fusion.1
  20.2 0.0 copy-done.1
  20.2 1.8 %fetch.1 = (f32[12,128,128]{2,1,0:T(8,128)S(1)}, f32[128,128]{1,0:T(8,128)S(1)}) custom-call(s32[12]{0:T(128)S(1)} %get-tuple-element.19.from_ref.refs_0_, f32[96,128,128]{2,1,0:T(8,128)} %refs_2_.1, f32[96,128]{1,0:T(8,128)S(1)} %copy-done.1), custom_call_target="tpu_custom_call" | custom-call | tf_op jit(solution)/shard_map/fetch/pallas_call | solution.py:217
  22.1 28.7 %all-to-all-done.refs_4_ = f32[128,33,1,128]{3,2,1,0:T(1,128)S(1)} async-done(((f32[128,33,1,128]{3,2,1,0:T(1,128)}), f32[128,33,1,128]{3,2,1,0:T(1,128)S(1)}, u32[]{:S(2)}, u32[]{:S(2)}) %all-to-all-start) | async-done | bytes 2162720 | tf_op jit(solution)/shard_map/all_to_all | solution.py:451
  50.7 4.3 %leave.1 = (s32[32,128]{1,0:T(8,128)S(1)}, f32[32,136,128]{2,1,0:T(8,128)}) custom-call(s32[12]{0:T(128)S(1)} %get-tuple-element.19.from_ref.refs_0_, s32[12]{0:T(128)S(1)} %get-tuple-element.18.refs_1_, f32[12,128,128]{2,1,0:T(8,128)S(1)} %get-tuple-element.10.refs_2_, f32[128,128]{1,0:T(8,128)S(1)} %get-tuple-element.11.refs_3_, ...), custom_call_target="tpu_custom_call" | custom-call | tf_op jit(solution)/shard_map/leave/pallas_call | solution.py:279
  55.0 4.8 %all-to-all-start.1 = ((f32[32,136,128]{2,1,0:T(8,128)}), f32[32,136,128]{2,1,0:T(8,128)}, u32[]{:S(2)}, u32[]{:S(2)}) async-start(f32[32,136,128]{2,1,0:T(8,128)} %get-tuple-element.12), calls=%async_computation.1 | async-start | bytes 4456448 | tf_op jit(solution)/shard_map/all_to_all | solution.py:463
  59.9 0.1 and.44
  60.0 0.1 div.18
  60.1 0.1 add.44
  60.1 0.2 select_reduce_fusion
  60.3 0.1 copy.14
  60.4 0.1 reduce-window.16
  60.5 0.1 add_reduce_fusion.1
  60.6 0.7 select_reduce_fusion.3
  61.3 0.0 copy-start.4
  61.3 23.5 %stay.1 = (f32[96,128,128]{2,1,0:T(8,128)}, f32[96,128]{1,0:T(8,128)S(1)}, f32[12,128,128]{2,1,0:T(8,128)S(1)}, f32[128,128]{1,0:T(8,128)S(1)}) custom-call(s32[32,128]{1,0:T(8,128)S(1)} %get-tuple-element.13.refs_0_, s32[12]{0:T(128)S(1)} %get-tuple-element.20.refs_1_.slots_ref, f32[96,128,128]{2,1,0:T(8,128)} %refs_2_.1, f32[96,128]{1,0:T(8,128)S(1)} %copy-done.1, ...), custom_call_target="tpu_custom_call" | custom-call | tf_op jit(solution)/shard_map/stay/pallas_call | solution.py:356
  84.8 0.0 copy-done.4
  84.8 0.0 copy-start
  84.8 0.9 copy-done
  85.7 0.6 copy-done.2
  86.3 0.6 copy-done.3
  86.9 4.5 %all-to-all-done.1.got_hbm = f32[32,136,128]{2,1,0:T(8,128)} async-done(((f32[32,136,128]{2,1,0:T(8,128)}), f32[32,136,128]{2,1,0:T(8,128)}, u32[]{:S(2)}, u32[]{:S(2)}) %all-to-all-start.1) | async-done | bytes 2228256 | tf_op jit(solution)/shard_map/all_to_all | solution.py:463
  91.4 3.3 %arrive.1 = (f32[96,128,128]{2,1,0:T(8,128)}, f32[96,128]{1,0:T(8,128)}) custom-call(s32[12]{0:T(128)} %get-tuple-element.21.peers_ref, s32[12]{0:T(128)} %copy-done.4, f32[32,136,128]{2,1,0:T(8,128)} %all-to-all-done.1.got_hbm, f32[12,128,128]{2,1,0:T(8,128)} %copy-done, f32[128,128]{1,0:T(8,128)} %copy-done.2, ...), custom_call_target="tpu_custom_call", output_to_operand_aliasing={{0}: (5, {})} | custom-call | tf_op jit(solution)/shard_map/arrive/pallas_call | solution.py:410
  (8 shorter events, 0.1 us)
Async XLA Ops:
  8.4 11.2 %copy-start.5 = (s32[12288]{0:T(1024)S(1)}, s32[12288]{0:T(1024)}, u32[]{:S(2)}) copy-start(s32[12288]{0:T(1024)} %param.13) | copy-start | bytes 147460
  8.4 11.8 %copy-start.1 = (f32[96,128]{1,0:T(8,128)S(1)}, f32[96,128]{1,0:T(8,128)}, u32[]{:S(2)}) copy-start(f32[96,128]{1,0:T(8,128)} %refs_3_.3) | copy-start | bytes 147460
  8.5 42.3 %all-to-all-start = ((f32[128,33,1,128]{3,2,1,0:T(1,128)}), f32[128,33,1,128]{3,2,1,0:T(1,128)S(1)}, u32[]{:S(2)}, u32[]{:S(2)}) async-start(f32[128,33,1,128]{3,2,1,0:T(1,128)} %pack.1), calls=%async_computation | async-start | bytes 4325376 | tf_op jit(solution)/shard_map/all_to_all | solution.py:451
  55.0 36.4 %all-to-all-start.1 = ((f32[32,136,128]{2,1,0:T(8,128)}), f32[32,136,128]{2,1,0:T(8,128)}, u32[]{:S(2)}, u32[]{:S(2)}) async-start(f32[32,136,128]{2,1,0:T(8,128)} %get-tuple-element.12), calls=%async_computation.1 | async-start | bytes 4456448 | tf_op jit(solution)/shard_map/all_to_all | solution.py:463
  61.3 23.5 %copy-start.4 = (s32[12]{0:T(128)}, s32[12]{0:T(128)S(1)}, u32[]{:S(2)}) copy-start(s32[12]{0:T(128)S(1)} %get-tuple-element.20.refs_1_.slots_ref) | copy-start | bytes 148
  84.8 0.9 copy-start
  85.7 0.6 copy-start.2
  86.3 0.6 copy-start.3

commit v4 on v3

--- a/solution.py
+++ b/solution.py
@@ -9,10 +9,12 @@
 EPSILON = 1e-08
 LANES = 128
 MOVES = 12
+FROM, TO, SLOT, PEER = 0, MOVES, 2 * MOVES, 3 * MOVES
 VM = pltpu.VMEM
 SM = pltpu.SMEM
 ALL_VMEM = 67043328
 ROOM = 14000000
+LAST_ROOM = 11500000
 
 
 def iota(shape, dim):
@@ -200,18 +202,18 @@
     return columns[:, k : k + 1]
 
 
-def fetch_kernel(from_ref, table_ref, acc_ref, out_ref, old_ref, sems):
-    copies = [pltpu.make_async_copy(table_ref.at[from_ref[k]], out_ref.at[k], sems.at[k]) for k in range(MOVES)]
+def fetch_kernel(list_ref, table_ref, acc_ref, out_ref, old_ref, sems):
+    copies = [pltpu.make_async_copy(table_ref.at[list_ref[FROM + k]], out_ref.at[k], sems.at[k]) for k in range(MOVES)]
     for copy in copies:
         copy.start()
     old_ref[...] = jnp.zeros_like(old_ref)
     for k in range(MOVES):
-        old_ref[pl.ds(k, 1), :] = acc_ref[pl.ds(from_ref[k], 1), :]
+        old_ref[pl.ds(k, 1), :] = acc_ref[pl.ds(list_ref[FROM + k], 1), :]
     for copy in copies:
         copy.wait()
 
 
-def fetch(came_from, table, acc):
+def fetch(lists, table, acc):
     vm = pl.BlockSpec(memory_space=VM)
     hbm = pl.BlockSpec(memory_space=pltpu.HBM)
     return pl.pallas_call(
@@ -225,22 +227,22 @@
         scratch_shapes=[pltpu.SemaphoreType.DMA((MOVES,))],
         compiler_params=pltpu.CompilerParams(vmem_limit_bytes=ALL_VMEM - ROOM),
         name="fetch",
-    )(came_from, table, acc)
+    )(lists, table, acc)
 
 
 ROUND = 4
 
 
-def leave_kernel(from_ref, to_ref, table_ref, acc_ref, got_ref, names_out, out_hbm, out_ref, even_ref, odd_ref, old_ref, names_v, names_s, sems, *, cap, rows):
+def leave_kernel(list_ref, table_ref, acc_ref, got_ref, names_out, out_hbm, out_ref, even_ref, odd_ref, old_ref, names_v, names_s, sems, *, cap, rows):
     block, feature = table_ref.shape[1:]
-    spans = [pl.ds(pl.multiple_of(from_ref[k] * block, block), block) for k in range(MOVES)]
+    spans = [pl.ds(pl.multiple_of(list_ref[FROM + k] * block, block), block) for k in range(MOVES)]
     to_scalar = pltpu.make_async_copy(names_v, names_s, sems.at[MOVES])
     named = read_names(got_ref, names_v, to_scalar, dump=rows)
     names_out[...] = named
     at = iota(named.shape, 1) & (2 * cap - 1)
     goes = jnp.zeros(named.shape, jnp.bool_)
     for k in range(MOVES):
-        goes = goes | ((named >> 7) == from_ref[k])
+        goes = goes | ((named >> 7) == list_ref[FROM + k])
     needed = jnp.max(jnp.where(goes & (at < cap), at + 1, 0))
     for k in range(MOVES):
         even_ref[spans[k], :] = jnp.zeros((block, feature), jnp.float32)
@@ -265,13 +267,13 @@
     for k in range(MOVES):
         out_ref[k, pl.ds(block, 1), :] = old_ref[pl.ds(k, 1), :]
         out_ref[k, pl.ds(0, block), :] = table_ref[k] - lane_of(rates, k) * even_ref[spans[k], :]
-        sends.append(pltpu.make_async_copy(out_ref.at[k], out_hbm.at[to_ref[k]], sems.at[k]))
+        sends.append(pltpu.make_async_copy(out_ref.at[k], out_hbm.at[list_ref[TO + k]], sems.at[k]))
         sends[-1].start()
     for send in sends:
         send.wait()
 
 
-def leave(came_from, go_to, table, acc, got, peers, cap, rows):
+def leave(lists, table, acc, got, peers, cap, rows):
     block, feature = table.shape[1:]
     vm = pl.BlockSpec(memory_space=VM)
     sm = pl.BlockSpec(memory_space=SM)
@@ -282,7 +284,7 @@
             jax.ShapeDtypeStruct(names, jnp.int32),
             jax.ShapeDtypeStruct((peers, block + 8, feature), jnp.float32),
         ),
-        in_specs=[sm, sm, vm, vm, vm],
+        in_specs=[sm, vm, vm, vm],
         out_specs=(vm, pl.BlockSpec(memory_space=pltpu.HBM)),
         scratch_shapes=[
             VM((MOVES, block + 8, feature), jnp.float32),
@@ -295,116 +297,137 @@
         ],
         compiler_params=pltpu.CompilerParams(vmem_limit_bytes=ALL_VMEM - ROOM),
         name="leave",
-    )(came_from, go_to, table, acc, got)
-
-
-def stay_kernel(names_ref, slots_ref, table_ref, acc_ref, got_ref, out_ref, accout_ref, arrive_ref, squares_ref, one_ref, two_ref, rates_ref, *, cap, blocks):
-    i = pl.program_id(0)
-    each, block, feature = table_ref.shape
-
-    @pl.when(i == 0)
-    def _():
-        def clear(b, _):
-            at = pl.ds(pl.multiple_of(b * block, block), block)
-            one_ref[at, :] = jnp.zeros((block, feature), jnp.float32)
-            two_ref[at, :] = jnp.zeros((block, feature), jnp.float32)
-            return 0
-
-        lax.fori_loop(0, blocks, clear, 0)
-        add_rows(names_ref, got_ref, (one_ref,), offset=0, count=cap)
-        add_rows(names_ref, got_ref, (two_ref,), offset=cap, count=cap)
-        lane = iota((block, LANES), 1)
-
-        def squares(g, sums):
-            sums = list(sums)
-            for k in range(4):
-                b = g * 4 + k
-                at = pl.ds(pl.multiple_of(b * block, block), block)
-                for n, ref in enumerate((one_ref, two_ref)):
-                    sums[n] = jnp.where(lane == b, square_sums(ref[at, :]), sums[n])
-            return tuple(sums)
-
-        zero = jnp.zeros((block, LANES), jnp.float32)
-        first, second = lax.fori_loop(0, blocks // 4, squares, (zero, zero))
-        old = jnp.concatenate([acc_ref[...], jnp.ones((LANES - blocks, LANES), jnp.float32)], axis=0)
-        fresh = jnp.transpose(old) + first * (1.0 / feature)
-        rates_ref[0] = rate(fresh)
-        fresh = fresh + second * (1.0 / feature)
-        rates_ref[1] = rate(fresh)
-        accout_ref[...] = jnp.transpose(fresh)[:blocks, :]
-        arriving = zero
-        for k in range(MOVES):
-            at = pl.ds(pl.multiple_of(slots_ref[k] * block, block), block)
-            arrive_ref[k] = two_ref[at, :]
-            arriving = jnp.where(lane == k, square_sums(two_ref[at, :]), arriving)
-        squares_ref[...] = arriving
-
-    turn = (LANES - each * i) % LANES
-    one_rate = pltpu.roll(rates_ref[0], turn, 1)
-    two_rate = pltpu.roll(rates_ref[1], turn, 1)
-    for k in range(each):
-        at = pl.ds(pl.multiple_of((i * each + k) * block, block), block)
-        weights = table_ref[k] - lane_of(one_rate, k) * one_ref[at, :]
-        out_ref[k] = weights - lane_of(two_rate, k) * two_ref[at, :]
-
-
-def stay(names, slots, table, acc, got, cap, each=8):
+    )(lists, table, acc, got)
+
+
+PIECE = 8
+
+
+def stay_kernel(list_ref, names_ref, table_hbm, acc_ref, got_ref, out_hbm, accout_ref, arrive_ref, squares_ref, table_ref, one_ref, two_ref, rates_ref, sems):
+    blocks, block, feature = table_ref.shape
+    pieces = blocks // PIECE
+    cap = (got_ref.shape[1] - 1) // 2
+
+    def take(i):
+        at = pl.ds(i * PIECE, PIECE)
+        return pltpu.make_async_copy(table_hbm.at[at], table_ref.at[at], sems.at[i])
+
+    def give(i):
+        at = pl.ds(i * PIECE, PIECE)
+        return pltpu.make_async_copy(table_ref.at[at], out_hbm.at[at], sems.at[i])
+
+    for i in range(pieces):
+        take(i).start()
+
+    def span(b):
+        return pl.ds(pl.multiple_of(b * block, block), block)
+
+    def clear(b, _):
+        one_ref[span(b), :] = jnp.zeros((block, feature), jnp.float32)
+        two_ref[span(b), :] = jnp.zeros((block, feature), jnp.float32)
+        return 0
+
+    lax.fori_loop(0, blocks, clear, 0)
+    add_rows(names_ref, got_ref, (one_ref,), offset=0, count=cap)
+    add_rows(names_ref, got_ref, (two_ref,), offset=cap, count=cap)
+    lane = iota((block, LANES), 1)
+
+    def squares(g, sums):
+        sums = list(sums)
+        for k in range(4):
+            b = g * 4 + k
+            for n, ref in enumerate((one_ref, two_ref)):
+                sums[n] = jnp.where(lane == b, square_sums(ref[span(b), :]), sums[n])
+        return tuple(sums)
+
+    zero = jnp.zeros((block, LANES), jnp.float32)
+    first, second = lax.fori_loop(0, blocks // 4, squares, (zero, zero))
+    old = jnp.concatenate([acc_ref[...], jnp.ones((LANES - blocks, LANES), jnp.float32)], axis=0)
+    fresh = jnp.transpose(old) + first * (1.0 / feature)
+    rates_ref[0] = rate(fresh)
+    fresh = fresh + second * (1.0 / feature)
+    rates_ref[1] = rate(fresh)
+    accout_ref[...] = jnp.transpose(fresh)[:blocks, :]
+    arriving = zero
+    for k in range(MOVES):
+        gradient = two_ref[span(list_ref[SLOT + k]), :]
+        arrive_ref[k] = gradient
+        arriving = jnp.where(lane == k, square_sums(gradient), arriving)
+    squares_ref[...] = arriving
+
+    def piece(i, _):
+        turn = (LANES - PIECE * i) % LANES
+        one_rate = pltpu.roll(rates_ref[0], turn, 1)
+        two_rate = pltpu.roll(rates_ref[1], turn, 1)
+        take(i).wait()
+        for k in range(PIECE):
+            b = i * PIECE + k
+            weights = table_ref[b] - lane_of(one_rate, k) * one_ref[span(b), :]
+            table_ref[b] = weights - lane_of(two_rate, k) * two_ref[span(b), :]
+        give(i).start()
+        return 0
+
+    lax.fori_loop(0, pieces, piece, 0)
+    for i in range(pieces):
+        give(i).wait()
+
+
+def stay(lists, names, table, acc, got):
     blocks, block, feature = table.shape
     vm = pl.BlockSpec(memory_space=VM)
     sm = pl.BlockSpec(memory_space=SM)
-    piece = pl.BlockSpec((each, block, feature), lambda i: (i, 0, 0))
+    hbm = pl.BlockSpec(memory_space=pltpu.HBM)
     return pl.pallas_call(
-        lambda *refs: stay_kernel(*refs, cap=cap, blocks=blocks),
-        grid=(blocks // each,),
+        stay_kernel,
         out_shape=(
             jax.ShapeDtypeStruct(table.shape, jnp.float32),
             jax.ShapeDtypeStruct(acc.shape, jnp.float32),
             jax.ShapeDtypeStruct((MOVES, block, feature), jnp.float32),
             jax.ShapeDtypeStruct((LANES, LANES), jnp.float32),
         ),
-        in_specs=[sm, sm, piece, vm, vm],
-        out_specs=(piece, vm, vm, vm),
+        in_specs=[sm, sm, hbm, vm, vm],
+        out_specs=(hbm, vm, vm, vm),
         scratch_shapes=[
+            VM(table.shape, jnp.float32),
             VM((blocks * block + 8, feature), jnp.float32),
             VM((blocks * block + 8, feature), jnp.float32),
             VM((2, LANES, LANES), jnp.float32),
+            pltpu.SemaphoreType.DMA((blocks // PIECE,)),
         ],
         compiler_params=pltpu.CompilerParams(vmem_limit_bytes=ALL_VMEM - ROOM),
         name="stay",
-    )(names, slots, table, acc, got)
-
-
-def arrive_kernel(peers_ref, slots_ref, got_hbm, second_hbm, squares_hbm, stayed_ref, accstay_hbm, out_ref, acc_hbm, got_ref, second_ref, squares_ref, acc_ref, buf_ref, old_ref, sems):
+    )(lists, names, table, acc, got)
+
+
+def arrive_kernel(list_ref, got_hbm, second_ref, squares_ref, stayed_ref, accstay_ref, out_ref, acc_hbm, got_ref, acc_ref, buf_ref, old_ref, sems):
     block, feature = stayed_ref.shape[1:]
-    takes = [pltpu.make_async_copy(got_hbm.at[peers_ref[k]], got_ref.at[k], sems.at[k]) for k in range(MOVES)]
-    pairs = ((squares_hbm, squares_ref), (accstay_hbm, acc_ref), (second_hbm, second_ref))
-    rest = [pltpu.make_async_copy(src, dst, sems.at[MOVES + n]) for n, (src, dst) in enumerate(pairs)]
-    for take in takes + rest:
+    takes = [pltpu.make_async_copy(got_hbm.at[list_ref[PEER + k]], got_ref.at[k], sems.at[k]) for k in range(MOVES)]
+    for take in takes:
         take.start()
+    acc_ref[...] = accstay_ref[...]
     lane = iota((block, LANES), 1)
     for k in range(MOVES):
         takes[k].wait()
         old_ref[pl.ds(k, 1), :] = got_ref[k, pl.ds(block, 1), :]
-    rest[0].wait()
     fresh = jnp.transpose(old_ref[...]) + squares_ref[...] * (1.0 / feature)
     rates = rate(jnp.where(lane < MOVES, fresh, 1.0))
+    copies = []
+    for k in range(MOVES):
+        buf_ref[k] = got_ref[k, pl.ds(0, block), :] - lane_of(rates, k) * second_ref[k]
+        copies.append(pltpu.make_async_copy(buf_ref.at[k], out_ref.at[list_ref[SLOT + k]], sems.at[k]))
+        copies[-1].start()
     old_ref[...] = jnp.transpose(fresh)
-    rest[1].wait()
-    for k in range(MOVES):
-        acc_ref[pl.ds(slots_ref[k], 1), :] = old_ref[pl.ds(k, 1), :]
-    copies = [pltpu.make_async_copy(acc_ref, acc_hbm, sems.at[MOVES])]
-    copies[0].start()
-    rest[2].wait()
-    for k in range(MOVES):
-        buf_ref[k] = got_ref[k, pl.ds(0, block), :] - lane_of(rates, k) * second_ref[k]
-        copies.append(pltpu.make_async_copy(buf_ref.at[k], out_ref.at[slots_ref[k]], sems.at[k]))
-        copies[-1].start()
+    for k in range(MOVES):
+        acc_ref[pl.ds(list_ref[SLOT + k], 1), :] = old_ref[pl.ds(k, 1), :]
+    copies.append(pltpu.make_async_copy(acc_ref, acc_hbm, sems.at[MOVES]))
+    copies[-1].start()
     for copy in copies:
         copy.wait()
 
 
-def arrive(peers, slots, got, second, squares, stayed, accstay):
+def arrive(lists, got, second, squares, stayed, accstay):
     blocks, block, feature = stayed.shape
+    vm = pl.BlockSpec(memory_space=VM)
     sm = pl.BlockSpec(memory_space=SM)
     hbm = pl.BlockSpec(memory_space=pltpu.HBM)
     return pl.pallas_call(
@@ -413,21 +436,19 @@
             jax.ShapeDtypeStruct(stayed.shape, jnp.float32),
             jax.ShapeDtypeStruct(accstay.shape, jnp.float32),
         ),
-        in_specs=[sm, sm, hbm, hbm, hbm, hbm, hbm],
+        in_specs=[sm, hbm, vm, vm, hbm, vm],
         out_specs=(hbm, hbm),
         scratch_shapes=[
             VM((MOVES,) + got.shape[1:], jnp.float32),
-            VM(second.shape, jnp.float32),
-            VM(squares.shape, jnp.float32),
             VM(accstay.shape, jnp.float32),
             VM((MOVES, block, feature), jnp.float32),
             VM((LANES, LANES), jnp.float32),
-            pltpu.SemaphoreType.DMA((MOVES + 3,)),
+            pltpu.SemaphoreType.DMA((MOVES + 1,)),
         ],
-        input_output_aliases={5: 0},
-        compiler_params=pltpu.CompilerParams(vmem_limit_bytes=ALL_VMEM),
+        input_output_aliases={4: 0},
+        compiler_params=pltpu.CompilerParams(vmem_limit_bytes=ALL_VMEM - LAST_ROOM),
         name="arrive",
-    )(peers, slots, got, second, squares, stayed, accstay)
+    )(lists, got, second, squares, stayed, accstay)
 
 
 def listed(mask, values):
@@ -452,17 +473,18 @@
 
     here = lax.dynamic_slice_in_dim(new_slot, group * peers * blocks, peers * blocks).reshape(peers, blocks)
     own = lax.dynamic_slice_in_dim(new_slot, device * blocks, blocks)
-    came_from, go_to = listed(own // blocks != device, (jnp.arange(blocks, dtype=jnp.int32), own // blocks % peers))
+    going = listed(own // blocks != device, (jnp.arange(blocks, dtype=jnp.int32), own // blocks % peers))
     peer = jnp.arange(peers, dtype=jnp.int32)
     to_me = (here // blocks == device) & (peer != mine)[:, None]
     slots = jnp.sum(jnp.where(to_me, here - device * blocks + 1, 0), axis=1)
-    from_peer, slots = listed(slots > 0, (peer, slots - 1))
-
-    gone, old = fetch(came_from, table, accumulator)
-    names, moving = leave(came_from, go_to, gone, old, got, peers, cap, blocks * block)
+    coming = listed(slots > 0, (slots - 1, peer))
+    lists = jnp.concatenate(going + coming)
+
+    gone, old = fetch(lists, table, accumulator)
+    names, moving = leave(lists, gone, old, got, peers, cap, blocks * block)
     moved = lax.all_to_all(moving, "row", split_axis=0, concat_axis=0, tiled=True)
-    stayed, accstay, second, squares = stay(names, slots, table, accumulator, got, cap)
-    return arrive(from_peer, slots, moved, second, squares, stayed, accstay)
+    stayed, accstay, second, squares = stay(lists, names, table, accumulator, got)
+    return arrive(lists, moved, second, squares, stayed, accstay)
 
 
 def solution(mesh):

time: 95.5 us -> 94.9 us (level)
  waiting for transfers between devices: 33.2 us -> 40 us
  Pallas kernels: 40.7 us -> 36.2 us
  local copies, waits for them, and re-layouts: 2.56 us -> 0.44 us
    all_to_all x1, waiting for transfers between devices: 4.5 us -> 12.3 us  [on_device(): lax.all_to_all(moving, 'row', split_axis=0, concat_axis=0, tiled=True)]
    pallas_call x1, Pallas kernels: 23.5 us -> 19.3 us  [stay(): pl.pallas_call(stay_kernel, out_shape=(jax.ShapeDtypeStruct(table.shape,...]
    unnamed x12 -> x4, local copies, waits for them, and re-layouts: 2.14 us -> 0.01 us
  transfers between devices with their start and end apart: 2 -> 2, of which waited for: 2 -> 2; matrix products, arithmetic and copies ran while one was open for 2% -> 2% of each run, Pallas kernels for 27% -> 22%
where the time goes in v4:
time: 94.9 us; the launch traced here: 94.4 us
  waiting for transfers between devices  40 us (42%)
  Pallas kernels  36.2 us (38%)
  starting transfers between devices  16 us (17%)
  other arithmetic  1.05 us (1%)
    all_to_all x1, waiting for transfers between devices, on_device(): lax.all_to_all(outgoing, ('table', 'row'), split_axis=0, concat_axis=0, t...  27.7 us
    pallas_call x1, Pallas kernels, stay(): pl.pallas_call(stay_kernel, out_shape=(jax.ShapeDtypeStruct(table.shape,...  19.3 us
    all_to_all x1, waiting for transfers between devices, on_device(): lax.all_to_all(moving, 'row', split_axis=0, concat_axis=0, tiled=True)  12.3 us
    all_to_all x1, starting transfers between devices, on_device(): lax.all_to_all(outgoing, ('table', 'row'), split_axis=0, concat_axis=0, t...  11.2 us
    pallas_call x1, Pallas kernels, pack(): pl.pallas_call(lambda *refs: pack_kernel(*refs, blocks=blocks, cap=cap),...  7.8 us
    all_to_all x1, starting transfers between devices, on_device(): lax.all_to_all(moving, 'row', split_axis=0, concat_axis=0, tiled=True)  4.81 us
    pallas_call x1, Pallas kernels, leave(): pl.pallas_call(lambda *refs: leave_kernel(*refs, cap=cap, rows=rows), out...  4.23 us
    pallas_call x1, Pallas kernels, arrive(): pl.pallas_call(arrive_kernel, out_shape=(jax.ShapeDtypeStruct(stayed.shap...  3.06 us
  transfers between devices with their start and end apart: 2, of which 2 were waited for; matrix products, arithmetic and copies ran while one was open for 2% of the time, Pallas kernels for 22%

profile of v4, /device:TPU:0, one launch (start us, length us, event | category | flops | bytes accessed | tf_op | source)
XLA Modules:
  0.0 94.4 jit_solution(17132838735645923729)
XLA Ops:
  0.6 7.8 %pack.1 = f32[128,33,1,128]{3,2,1,0:T(1,128)} custom-call(s32[1,1024]{1,0:T(1,128)} %bitcast.8, s32[1,1024]{1,0:T(1,128)} %bitcast.9, s32[96,128]{1,0:T(8,128)} %bitcast.7, f32[1024,128]{1,0:T(8,128)} %refs_3_.1, f32[1024,128]{1,0:T(8,128)} %refs_4_.1), custom_call_target="tpu_custom_call" | custom-call | tf_op jit(solution)/shard_map/pack/pallas_call | solution.py:135
  8.4 0.0 copy-start.1
  8.4 0.0 copy-start
  8.5 11.2 %all-to-all-start = ((f32[128,33,1,128]{3,2,1,0:T(1,128)}), f32[128,33,1,128]{3,2,1,0:T(1,128)S(1)}, u32[]{:S(2)}, u32[]{:S(2)}) async-start(f32[128,33,1,128]{3,2,1,0:T(1,128)} %pack.1), calls=%async_computation | async-start | bytes 4325376 | tf_op jit(solution)/shard_map/all_to_all | solution.py:472
  19.7 0.0 copy-done.1
  19.7 0.1 and.48
  19.8 0.1 div.19
  19.9 0.1 add.46
  19.9 0.2 select_reduce_fusion
  20.1 0.1 copy.15
  20.2 0.1 reduce-window.17
  20.3 0.1 and_select_fusion
  20.4 0.1 copy.14
  20.5 0.1 reduce-window.16
  20.6 0.1 add_reduce_fusion.1
  20.8 0.1 select_reduce_fusion.2
  20.9 0.1 add_reduce_fusion
  21.0 0.1 select_reduce_fusion.4
  21.1 0.1 pad_add_fusion.list_ref.refs_0_
  21.2 0.0 copy-done
  21.2 1.8 %fetch.1 = (f32[12,128,128]{2,1,0:T(8,128)S(1)}, f32[128,128]{1,0:T(8,128)S(1)}) custom-call(s32[48]{0:T(128)S(1)} %pad_add_fusion.list_ref.refs_0_, f32[96,128,128]{2,1,0:T(8,128)} %table_hbm.1, f32[96,128]{1,0:T(8,128)S(1)} %copy-done), custom_call_target="tpu_custom_call" | custom-call | tf_op jit(solution)/shard_map/fetch/pallas_call | solution.py:219
  23.0 27.7 %all-to-all-done.refs_3_.got_ref = f32[128,33,1,128]{3,2,1,0:T(1,128)S(1)} async-done(((f32[128,33,1,128]{3,2,1,0:T(1,128)}), f32[128,33,1,128]{3,2,1,0:T(1,128)S(1)}, u32[]{:S(2)}, u32[]{:S(2)}) %all-to-all-start) | async-done | bytes 2162720 | tf_op jit(solution)/shard_map/all_to_all | solution.py:472
  50.7 4.2 %leave.1 = (s32[32,128]{1,0:T(8,128)S(1)}, f32[32,136,128]{2,1,0:T(8,128)}) custom-call(s32[48]{0:T(128)S(1)} %pad_add_fusion.list_ref.refs_0_, f32[12,128,128]{2,1,0:T(8,128)S(1)} %get-tuple-element.10.refs_1_, f32[128,128]{1,0:T(8,128)S(1)} %get-tuple-element.11.refs_2_, f32[128,33,1,128]{3,2,1,0:T(1,128)S(1)} %all-to-all-done.refs_3_.got_ref), custom_call_target="tpu_custom_call" | custom-call | tf_op jit(solution)/shard_map/leave/pallas_call | solution.py:281
  55.0 4.8 %all-to-all-start.1 = ((f32[32,136,128]{2,1,0:T(8,128)}), f32[32,136,128]{2,1,0:T(8,128)}, u32[]{:S(2)}, u32[]{:S(2)}) async-start(f32[32,136,128]{2,1,0:T(8,128)} %get-tuple-element.12), calls=%async_computation.1 | async-start | bytes 4456448 | tf_op jit(solution)/shard_map/all_to_all | solution.py:485
  59.8 19.3 %stay.1 = (f32[96,128,128]{2,1,0:T(8,128)}, f32[96,128]{1,0:T(8,128)S(1)}, f32[12,128,128]{2,1,0:T(8,128)S(1)}, f32[128,128]{1,0:T(8,128)S(1)}) custom-call(s32[48]{0:T(128)S(1)} %pad_add_fusion.list_ref.refs_0_, s32[32,128]{1,0:T(8,128)S(1)} %get-tuple-element.13.names_ref, f32[96,128,128]{2,1,0:T(8,128)} %table_hbm.1, f32[96,128]{1,0:T(8,128)S(1)} %copy-done, ...), custom_call_target="tpu_custom_call" | custom-call | tf_op jit(solution)/shard_map/stay/pallas_call | solution.py:380
  79.1 12.3 %all-to-all-done.1.got_hbm = f32[32,136,128]{2,1,0:T(8,128)} async-done(((f32[32,136,128]{2,1,0:T(8,128)}), f32[32,136,128]{2,1,0:T(8,128)}, u32[]{:S(2)}, u32[]{:S(2)}) %all-to-all-start.1) | async-done | bytes 2228256 | tf_op jit(solution)/shard_map/all_to_all | solution.py:485
  91.4 3.1 %arrive.1 = (f32[96,128,128]{2,1,0:T(8,128)}, f32[96,128]{1,0:T(8,128)}) custom-call(s32[48]{0:T(128)S(1)} %pad_add_fusion.list_ref.refs_0_, f32[32,136,128]{2,1,0:T(8,128)} %all-to-all-done.1.got_hbm, f32[12,128,128]{2,1,0:T(8,128)S(1)} %get-tuple-element.14.second_ref, ...), custom_call_target="tpu_custom_call", output_to_operand_aliasing={{0}: (4, {})} | custom-call | tf_op jit(solution)/shard_map/arrive/pallas_call | solution.py:433
  (6 shorter events, 0.1 us)
Async XLA Ops:
  8.4 11.2 %copy-start.1 = (s32[12288]{0:T(1024)S(1)}, s32[12288]{0:T(1024)}, u32[]{:S(2)}) copy-start(s32[12288]{0:T(1024)} %param.13) | copy-start | bytes 147460
  8.4 12.7 %copy-start = (f32[96,128]{1,0:T(8,128)S(1)}, f32[96,128]{1,0:T(8,128)}, u32[]{:S(2)}) copy-start(f32[96,128]{1,0:T(8,128)} %acc_ref.3) | copy-start | bytes 147460
  8.5 42.3 %all-to-all-start = ((f32[128,33,1,128]{3,2,1,0:T(1,128)}), f32[128,33,1,128]{3,2,1,0:T(1,128)S(1)}, u32[]{:S(2)}, u32[]{:S(2)}) async-start(f32[128,33,1,128]{3,2,1,0:T(1,128)} %pack.1), calls=%async_computation | async-start | bytes 4325376 | tf_op jit(solution)/shard_map/all_to_all | solution.py:472
  55.0 36.4 %all-to-all-start.1 = ((f32[32,136,128]{2,1,0:T(8,128)}), f32[32,136,128]{2,1,0:T(8,128)}, u32[]{:S(2)}, u32[]{:S(2)}) async-start(f32[32,136,128]{2,1,0:T(8,128)} %get-tuple-element.12), calls=%async_computation.1 | async-start | bytes 4456448 | tf_op jit(solution)/shard_map/all_to_all | solution.py:485

commit v5 on v4

--- a/solution.py
+++ b/solution.py
@@ -14,7 +14,7 @@
 SM = pltpu.SMEM
 ALL_VMEM = 67043328
 ROOM = 14000000
-LAST_ROOM = 11500000
+LAST_ROOM = 14000000
 
 
 def iota(shape, dim):
@@ -35,6 +35,16 @@
         found += dot(part.astype(jnp.float32).astype(jnp.bfloat16), pick, (1, 0)) * scale
     here = iota(found.shape, 0) == (indices & 127)
     return jnp.sum(jnp.where(here, found, 0.0), axis=0, keepdims=True).astype(jnp.int32)
+
+
+def leaves(which_ref, indices):
+    high, low = which_ref.shape
+    pick = (iota((high, indices.shape[1]), 0) == (indices >> 7)).astype(jnp.bfloat16)
+    moves = jnp.where(which_ref[...] != iota((high, low), 0) * low + iota((high, low), 1), 1.0, 0.0)
+    moves = jnp.concatenate([moves, jnp.zeros((low - high, low), jnp.float32)], axis=0)
+    found = dot(jnp.transpose(moves)[:, :high].astype(jnp.bfloat16), pick, (1, 0))
+    here = iota(found.shape, 0) == (indices & 127)
+    return jnp.sum(jnp.where(here, found, 0.0), axis=0, keepdims=True) > 0.5
 
 
 def pack_kernel(one_ids, two_ids, slot_hbm, one_hbm, two_hbm, out_hbm, one_ref, two_ref, ids_ref, ids2_ref, slot_ref, place_v, place2_v, place_s, place2_s, names_v, out_ref, sems, *, blocks, cap):
@@ -50,7 +60,7 @@
     ids = ids_ref[...]
     ids2 = ids2_ref[...]
     held = ids >> 7
-    leaving = lookup(slot_ref, held) != held
+    leaving = leaves(slot_ref, held)
     block_slots = (held, lookup(slot_ref, ids2 >> 7))
     inner = (ids & 127, ids2 & 127)
     upper = jnp.where(iota((LANES, 2 * LANES), 0) < iota((LANES, 2 * LANES), 1), 1.0, 0.0).astype(jnp.bfloat16)
@@ -230,13 +240,20 @@
     )(lists, table, acc)
 
 
-ROUND = 4
-
-
-def leave_kernel(list_ref, table_ref, acc_ref, got_ref, names_out, out_hbm, out_ref, even_ref, odd_ref, old_ref, names_v, names_s, sems, *, cap, rows):
+ROUNDS = ((0, 6), (6, 5), (11, 5))
+
+
+def message(ref, peer):
+    peers, rows, _, feature = ref.shape
+    return ref.reshape(peers * rows, feature).at[pl.ds(peer * rows, rows)]
+
+
+def leave_kernel(list_ref, table_ref, acc_ref, got_ref, names_out, out_hbm, kept_hbm, out_ref, even_ref, odd_ref, old_ref, names_v, names_s, sems, *, cap, rows):
     block, feature = table_ref.shape[1:]
     spans = [pl.ds(pl.multiple_of(list_ref[FROM + k] * block, block), block) for k in range(MOVES)]
     to_scalar = pltpu.make_async_copy(names_v, names_s, sems.at[MOVES])
+    keep = pltpu.make_async_copy(got_ref, kept_hbm, sems.at[MOVES + 1])
+    keep.start()
     named = read_names(got_ref, names_v, to_scalar, dump=rows)
     names_out[...] = named
     at = iota(named.shape, 1) & (2 * cap - 1)
@@ -249,11 +266,12 @@
         odd_ref[spans[k], :] = jnp.zeros((block, feature), jnp.float32)
     to_scalar.wait()
 
-    def some(r, _):
-        add_rows(names_s, got_ref, (even_ref, odd_ref), offset=r * ROUND, count=ROUND)
-        return 0
-
-    lax.fori_loop(0, (needed + ROUND - 1) // ROUND, some, 0)
+    for offset, count in ROUNDS:
+
+        @pl.when(needed > offset)
+        def _():
+            add_rows(names_s, got_ref, (even_ref, odd_ref), offset=offset, count=count)
+
     lane = iota((block, LANES), 1)
     squares = jnp.zeros((block, LANES), jnp.float32)
     for k in range(MOVES):
@@ -267,10 +285,11 @@
     for k in range(MOVES):
         out_ref[k, pl.ds(block, 1), :] = old_ref[pl.ds(k, 1), :]
         out_ref[k, pl.ds(0, block), :] = table_ref[k] - lane_of(rates, k) * even_ref[spans[k], :]
-        sends.append(pltpu.make_async_copy(out_ref.at[k], out_hbm.at[list_ref[TO + k]], sems.at[k]))
+        sends.append(pltpu.make_async_copy(out_ref.at[k, pl.ds(0, block + 1)], message(out_hbm, list_ref[TO + k]), sems.at[k]))
         sends[-1].start()
     for send in sends:
         send.wait()
+    keep.wait()
 
 
 def leave(lists, table, acc, got, peers, cap, rows):
@@ -282,10 +301,11 @@
         lambda *refs: leave_kernel(*refs, cap=cap, rows=rows),
         out_shape=(
             jax.ShapeDtypeStruct(names, jnp.int32),
-            jax.ShapeDtypeStruct((peers, block + 8, feature), jnp.float32),
+            pltpu.HBM((peers, block + 1, 1, feature), jnp.float32),
+            pltpu.HBM(got.shape, jnp.float32),
         ),
         in_specs=[sm, vm, vm, vm],
-        out_specs=(vm, pl.BlockSpec(memory_space=pltpu.HBM)),
+        out_specs=(vm, pl.BlockSpec(memory_space=pltpu.HBM), pl.BlockSpec(memory_space=pltpu.HBM)),
         scratch_shapes=[
             VM((MOVES, block + 8, feature), jnp.float32),
             VM((rows + 8, feature), jnp.float32),
@@ -293,7 +313,7 @@
             VM((LANES, LANES), jnp.float32),
             VM(names, jnp.int32),
             SM(names, jnp.int32),
-            pltpu.SemaphoreType.DMA((MOVES + 1,)),
+            pltpu.SemaphoreType.DMA((MOVES + 2,)),
         ],
         compiler_params=pltpu.CompilerParams(vmem_limit_bytes=ALL_VMEM - ROOM),
         name="leave",
@@ -399,21 +419,19 @@
     )(lists, names, table, acc, got)
 
 
-def arrive_kernel(list_ref, got_hbm, second_ref, squares_ref, stayed_ref, accstay_ref, out_ref, acc_hbm, got_ref, acc_ref, buf_ref, old_ref, sems):
+def arrive_kernel(list_ref, got_ref, second_ref, squares_ref, stayed_ref, accstay_ref, out_ref, acc_hbm, acc_ref, buf_ref, old_ref, sems):
     block, feature = stayed_ref.shape[1:]
-    takes = [pltpu.make_async_copy(got_hbm.at[list_ref[PEER + k]], got_ref.at[k], sems.at[k]) for k in range(MOVES)]
-    for take in takes:
-        take.start()
+    stride = got_ref.shape[1]
+    rows_ref = got_ref.reshape(got_ref.shape[0] * stride, feature)
     acc_ref[...] = accstay_ref[...]
     lane = iota((block, LANES), 1)
     for k in range(MOVES):
-        takes[k].wait()
-        old_ref[pl.ds(k, 1), :] = got_ref[k, pl.ds(block, 1), :]
+        old_ref[pl.ds(k, 1), :] = got_ref[list_ref[PEER + k], block]
     fresh = jnp.transpose(old_ref[...]) + squares_ref[...] * (1.0 / feature)
     rates = rate(jnp.where(lane < MOVES, fresh, 1.0))
     copies = []
     for k in range(MOVES):
-        buf_ref[k] = got_ref[k, pl.ds(0, block), :] - lane_of(rates, k) * second_ref[k]
+        buf_ref[k] = rows_ref[pl.ds(list_ref[PEER + k] * stride, block), :] - lane_of(rates, k) * second_ref[k]
         copies.append(pltpu.make_async_copy(buf_ref.at[k], out_ref.at[list_ref[SLOT + k]], sems.at[k]))
         copies[-1].start()
     old_ref[...] = jnp.transpose(fresh)
@@ -436,10 +454,9 @@
             jax.ShapeDtypeStruct(stayed.shape, jnp.float32),
             jax.ShapeDtypeStruct(accstay.shape, jnp.float32),
         ),
-        in_specs=[sm, hbm, vm, vm, hbm, vm],
+        in_specs=[sm, vm, vm, vm, hbm, vm],
         out_specs=(hbm, hbm),
         scratch_shapes=[
-            VM((MOVES,) + got.shape[1:], jnp.float32),
             VM(accstay.shape, jnp.float32),
             VM((MOVES, block, feature), jnp.float32),
             VM((LANES, LANES), jnp.float32),
@@ -481,9 +498,9 @@
     lists = jnp.concatenate(going + coming)
 
     gone, old = fetch(lists, table, accumulator)
-    names, moving = leave(lists, gone, old, got, peers, cap, blocks * block)
+    names, moving, kept = leave(lists, gone, old, got, peers, cap, blocks * block)
     moved = lax.all_to_all(moving, "row", split_axis=0, concat_axis=0, tiled=True)
-    stayed, accstay, second, squares = stay(lists, names, table, accumulator, got)
+    stayed, accstay, second, squares = stay(lists, names, table, accumulator, kept)
     return arrive(lists, moved, second, squares, stayed, accstay)
 
 

time: 94.9 us -> 91 us (0.959)
  waiting for transfers between devices: 40 us -> 37.1 us
  Pallas kernels: 36.2 us -> 34.4 us
  local copies, waits for them, and re-layouts: 0.44 us -> 2.04 us
    all_to_all x1, waiting for transfers between devices: 12.3 us -> 9.36 us  [on_device(): lax.all_to_all(moving, 'row', split_axis=0, concat_axis=0, tiled=True)]
    unnamed x4 -> x6, local copies, waits for them, and re-layouts: 0.01 us -> 1.62 us
    pallas_call x1, Pallas kernels: 3.06 us -> 1.88 us  [arrive(): pl.pallas_call(arrive_kernel, out_shape=(jax.ShapeDtypeStruct(stayed.shap...]
  transfers between devices with their start and end apart: 2 -> 2, of which waited for: 2 -> 2; matrix products, arithmetic and copies ran while one was open for 2% -> 2% of each run, Pallas kernels for 22% -> 23%
where the time goes in v5:
time: 91 us; the launch traced here: 90.6 us
  waiting for transfers between devices  37.1 us (41%)
  Pallas kernels  34.4 us (38%)
  starting transfers between devices  15.2 us (17%)
  local copies, waits for them, and re-layouts  2.04 us (2%)
  other arithmetic  1.05 us (1%)
    all_to_all x1, waiting for transfers between devices, on_device(): lax.all_to_all(outgoing, ('table', 'row'), split_axis=0, concat_axis=0, t...  27.7 us
    pallas_call x1, Pallas kernels, stay(): pl.pallas_call(stay_kernel, out_shape=(jax.ShapeDtypeStruct(table.shape,...  19.3 us
    all_to_all x1, starting transfers between devices, on_device(): lax.all_to_all(outgoing, ('table', 'row'), split_axis=0, concat_axis=0, t...  11.2 us
    all_to_all x1, waiting for transfers between devices, on_device(): lax.all_to_all(moving, 'row', split_axis=0, concat_axis=0, tiled=True)  9.36 us
    pallas_call x1, Pallas kernels, pack(): pl.pallas_call(lambda *refs: pack_kernel(*refs, blocks=blocks, cap=cap),...  7.68 us
    all_to_all x1, starting transfers between devices, on_device(): lax.all_to_all(moving, 'row', split_axis=0, concat_axis=0, tiled=True)  4.07 us
    pallas_call x1, Pallas kernels, leave(): pl.pallas_call(lambda *refs: leave_kernel(*refs, cap=cap, rows=rows), out...  3.76 us
    pallas_call x1, Pallas kernels, arrive(): pl.pallas_call(arrive_kernel, out_shape=(jax.ShapeDtypeStruct(stayed.shap...  1.88 us
  transfers between devices with their start and end apart: 2, of which 2 were waited for; matrix products, arithmetic and copies ran while one was open for 2% of the time, Pallas kernels for 23%

profile of v5, /device:TPU:0, one launch (start us, length us, event | category | flops | bytes accessed | tf_op | source)
XLA Modules:
  0.0 90.6 jit_solution(13104667406511221978)
XLA Ops:
  0.6 7.7 %pack.1 = f32[128,33,1,128]{3,2,1,0:T(1,128)} custom-call(s32[1,1024]{1,0:T(1,128)} %bitcast.8, s32[1,1024]{1,0:T(1,128)} %bitcast.9, s32[96,128]{1,0:T(8,128)} %bitcast.7, f32[1024,128]{1,0:T(8,128)} %refs_3_.1, f32[1024,128]{1,0:T(8,128)} %refs_4_.1), custom_call_target="tpu_custom_call" | custom-call | tf_op jit(solution)/shard_map/pack/pallas_call | solution.py:145
  8.3 0.0 copy-start.2
  8.3 0.0 copy-start.1
  8.3 11.2 %all-to-all-start = ((f32[128,33,1,128]{3,2,1,0:T(1,128)}), f32[128,33,1,128]{3,2,1,0:T(1,128)S(1)}, u32[]{:S(2)}, u32[]{:S(2)}) async-start(f32[128,33,1,128]{3,2,1,0:T(1,128)} %pack.1), calls=%async_computation | async-start | bytes 4325376 | tf_op jit(solution)/shard_map/all_to_all | solution.py:489
  19.5 0.0 copy-done.2
  19.6 0.1 and.48
  19.7 0.1 div.19
  19.7 0.1 add.46
  19.8 0.2 select_reduce_fusion
  20.0 0.1 copy.15
  20.1 0.1 reduce-window.17
  20.2 0.1 and_select_fusion
  20.3 0.1 copy.14
  20.4 0.1 reduce-window.16
  20.5 0.1 add_reduce_fusion.1
  20.6 0.1 select_reduce_fusion.2
  20.8 0.1 add_reduce_fusion
  20.9 0.1 select_reduce_fusion.4
  21.0 0.1 pad_add_fusion.list_ref.refs_0_
  21.1 0.0 copy-done.1
  21.1 1.8 %fetch.1 = (f32[12,128,128]{2,1,0:T(8,128)S(1)}, f32[128,128]{1,0:T(8,128)S(1)}) custom-call(s32[48]{0:T(128)S(1)} %pad_add_fusion.list_ref.refs_0_, f32[96,128,128]{2,1,0:T(8,128)} %table_hbm.1, f32[96,128]{1,0:T(8,128)S(1)} %copy-done.1), custom_call_target="tpu_custom_call" | custom-call | tf_op jit(solution)/shard_map/fetch/pallas_call | solution.py:229
  22.9 27.7 %all-to-all-done.refs_3_ = f32[128,33,1,128]{3,2,1,0:T(1,128)S(1)} async-done(((f32[128,33,1,128]{3,2,1,0:T(1,128)}), f32[128,33,1,128]{3,2,1,0:T(1,128)S(1)}, u32[]{:S(2)}, u32[]{:S(2)}) %all-to-all-start) | async-done | bytes 2162720 | tf_op jit(solution)/shard_map/all_to_all | solution.py:489
  50.6 3.8 %leave.1 = (s32[32,128]{1,0:T(8,128)S(1)}, f32[32,129,1,128]{3,2,1,0:T(1,128)}, f32[128,33,1,128]{3,2,1,0:T(1,128)}) custom-call(s32[48]{0:T(128)S(1)} %pad_add_fusion.list_ref.refs_0_, f32[12,128,128]{2,1,0:T(8,128)S(1)} %get-tuple-element.11.refs_1_, f32[128,128]{1,0:T(8,128)S(1)} %get-tuple-element.12.refs_2_, f32[128,33,1,128]{3,2,1,0:T(1,128)S(1)} %all-to-all-done.refs_3_), custom_call_target="tpu_custom_call" | custom-call | tf_op jit(solution)/shard_map/leave/pallas_call | solution.py:300
  54.4 4.1 %all-to-all-start.1 = ((f32[32,129,1,128]{3,2,1,0:T(1,128)}), f32[32,129,1,128]{3,2,1,0:T(1,128)S(1)}, u32[]{:S(2)}, u32[]{:S(2)}) async-start(f32[32,129,1,128]{3,2,1,0:T(1,128)} %get-tuple-element.13), calls=%async_computation.1 | async-start | bytes 4227072 | tf_op jit(solution)/shard_map/all_to_all | solution.py:502
  58.5 0.0 copy-start
  58.5 1.6 %copy-done = f32[128,33,1,128]{3,2,1,0:T(1,128)S(1)} copy-done((f32[128,33,1,128]{3,2,1,0:T(1,128)S(1)}, f32[128,33,1,128]{3,2,1,0:T(1,128)}, u32[]{:S(2)}) %copy-start) | copy-done | bytes 2162712
  60.1 19.3 %stay.1 = (f32[96,128,128]{2,1,0:T(8,128)}, f32[96,128]{1,0:T(8,128)S(1)}, f32[12,128,128]{2,1,0:T(8,128)S(1)}, f32[128,128]{1,0:T(8,128)S(1)}) custom-call(s32[48]{0:T(128)S(1)} %pad_add_fusion.list_ref.refs_0_, s32[32,128]{1,0:T(8,128)S(1)} %get-tuple-element.14.names_ref, f32[96,128,128]{2,1,0:T(8,128)} %table_hbm.1, f32[96,128]{1,0:T(8,128)S(1)} %copy-done.1, ...), custom_call_target="tpu_custom_call" | custom-call | tf_op jit(solution)/shard_map/stay/pallas_call | solution.py:400
  79.4 9.4 %all-to-all-done.1.got_ref = f32[32,129,1,128]{3,2,1,0:T(1,128)S(1)} async-done(((f32[32,129,1,128]{3,2,1,0:T(1,128)}), f32[32,129,1,128]{3,2,1,0:T(1,128)S(1)}, u32[]{:S(2)}, u32[]{:S(2)}) %all-to-all-start.1) | async-done | bytes 2113568 | tf_op jit(solution)/shard_map/all_to_all | solution.py:502
  88.7 1.9 %arrive.1 = (f32[96,128,128]{2,1,0:T(8,128)}, f32[96,128]{1,0:T(8,128)}) custom-call(s32[48]{0:T(128)S(1)} %pad_add_fusion.list_ref.refs_0_, f32[32,129,1,128]{3,2,1,0:T(1,128)S(1)} %all-to-all-done.1.got_ref, f32[12,128,128]{2,1,0:T(8,128)S(1)} %get-tuple-element.16.second_ref, ...), custom_call_target="tpu_custom_call", output_to_operand_aliasing={{0}: (4, {})} | custom-call | tf_op jit(solution)/shard_map/arrive/pallas_call | solution.py:451
  (6 shorter events, 0.1 us)
Async XLA Ops:
  8.3 11.2 %copy-start.2 = (s32[12288]{0:T(1024)S(1)}, s32[12288]{0:T(1024)}, u32[]{:S(2)}) copy-start(s32[12288]{0:T(1024)} %param.13) | copy-start | bytes 147460
  8.3 12.7 %copy-start.1 = (f32[96,128]{1,0:T(8,128)S(1)}, f32[96,128]{1,0:T(8,128)}, u32[]{:S(2)}) copy-start(f32[96,128]{1,0:T(8,128)} %acc_ref.3) | copy-start | bytes 147460
  8.3 42.3 %all-to-all-start = ((f32[128,33,1,128]{3,2,1,0:T(1,128)}), f32[128,33,1,128]{3,2,1,0:T(1,128)S(1)}, u32[]{:S(2)}, u32[]{:S(2)}) async-start(f32[128,33,1,128]{3,2,1,0:T(1,128)} %pack.1), calls=%async_computation | async-start | bytes 4325376 | tf_op jit(solution)/shard_map/all_to_all | solution.py:489
  54.4 34.3 %all-to-all-start.1 = ((f32[32,129,1,128]{3,2,1,0:T(1,128)}), f32[32,129,1,128]{3,2,1,0:T(1,128)S(1)}, u32[]{:S(2)}, u32[]{:S(2)}) async-start(f32[32,129,1,128]{3,2,1,0:T(1,128)} %get-tuple-element.13), calls=%async_computation.1 | async-start | bytes 4227072 | tf_op jit(solution)/shard_map/all_to_all | solution.py:502
  58.5 1.6 %copy-start = (f32[128,33,1,128]{3,2,1,0:T(1,128)S(1)}, f32[128,33,1,128]{3,2,1,0:T(1,128)}, u32[]{:S(2)}) copy-start(f32[128,33,1,128]{3,2,1,0:T(1,128)} %get-tuple-element.15.got_ref) | copy-start | bytes 6488068

commit v6 on v5

--- a/solution.py
+++ b/solution.py
@@ -47,7 +47,7 @@
     return jnp.sum(jnp.where(here, found, 0.0), axis=0, keepdims=True) > 0.5
 
 
-def pack_kernel(one_ids, two_ids, slot_hbm, one_hbm, two_hbm, out_hbm, one_ref, two_ref, ids_ref, ids2_ref, slot_ref, place_v, place2_v, place_s, place2_s, names_v, out_ref, sems, *, blocks, cap):
+def pack_kernel(one_ids, two_ids, slot_hbm, one_hbm, two_hbm, out_hbm, one_ref, two_ref, ids_ref, ids2_ref, slot_ref, place_v, place2_v, place_s, place2_s, names_v, halves_ref, spots_ref, out_ref, sems, *, blocks, cap):
     total, stride = out_ref.shape[:2]
     rows = one_ref.shape[0]
     chunks = rows // LANES
@@ -66,8 +66,6 @@
     upper = jnp.where(iota((LANES, 2 * LANES), 0) < iota((LANES, 2 * LANES), 1), 1.0, 0.0).astype(jnp.bfloat16)
     everywhere = jnp.ones((LANES, LANES), jnp.bfloat16)
     lane_slot = iota((LANES, LANES), 0) & (2 * cap - 1)
-    high = jnp.zeros((total, LANES), jnp.float32)
-    low = jnp.zeros((total, LANES), jnp.float32)
     places = ((place_v, place_s), (place2_v, place2_s))
     to_scalar = [pltpu.make_async_copy(v, s, sems.at[5 + n]) for n, (v, s) in enumerate(places)]
     for step in range(2):
@@ -97,11 +95,13 @@
                 before = jnp.where(early, before_first, firsts + before - before_first)
             within = jnp.sum(jnp.where(mine, before, 0.0), axis=0, keepdims=True).astype(jnp.int32) + step * cap
             places[step][0][pl.ds(c, 1), :] = own * stride + within
-            where = jnp.where(lane_slot == within, 1.0, 0.0).astype(jnp.bfloat16)
-            high += dot(jnp.where(mine, (name >> 7).astype(jnp.float32), 0.0).astype(jnp.bfloat16), where, (1, 1))
-            low += dot(jnp.where(mine, (name & 127).astype(jnp.float32), 0.0).astype(jnp.bfloat16), where, (1, 1))
+            here = slice(step * rows + c * LANES, step * rows + (c + 1) * LANES)
+            spots_ref[:, here] = jnp.where(lane_slot == within, 1.0, 0.0).astype(jnp.bfloat16)
+            halves_ref[:total, here] = jnp.where(mine, (name >> 7).astype(jnp.float32), 0.0).astype(jnp.bfloat16)
+            halves_ref[total:, here] = jnp.where(mine, (name & 127).astype(jnp.float32), 0.0).astype(jnp.bfloat16)
         to_scalar[step].start()
-    names_v[...] = high * 128.0 + low
+    halves = dot(halves_ref[...], spots_ref[...], (1, 1))
+    names_v[...] = halves[:total] * 128.0 + halves[total:]
     flat = out_ref.reshape(total * stride, 1, LANES)
 
     def move(src, place):
@@ -158,6 +158,8 @@
             SM(place, jnp.int32),
             SM(place, jnp.int32),
             VM((total, LANES), jnp.float32),
+            VM((2 * total, 2 * rows), jnp.bfloat16),
+            VM((LANES, 2 * rows), jnp.bfloat16),
             VM(message, jnp.float32),
             pltpu.SemaphoreType.DMA((9,)),
         ],

time: 91 us -> 88.9 us (0.977)
  Pallas kernels: 34.4 us -> 32.3 us
    pallas_call x1, Pallas kernels: 7.68 us -> 5.58 us  [pack(): pl.pallas_call(lambda *refs: pack_kernel(*refs, blocks=blocks, cap=cap),...]
  transfers between devices with their start and end apart: 2 -> 2, of which waited for: 2 -> 2; matrix products, arithmetic and copies ran while one was open for 2% -> 2% of each run, Pallas kernels for 23% -> 24%
where the time goes in v6:
time: 88.9 us; the launch traced here: 88.5 us
  waiting for transfers between devices  37.1 us (42%)
  Pallas kernels  32.3 us (36%)
  starting transfers between devices  15.2 us (17%)
  local copies, waits for them, and re-layouts  2.04 us (2%)
  other arithmetic  1.05 us (1%)
    all_to_all x1, waiting for transfers between devices, on_device(): lax.all_to_all(outgoing, ('table', 'row'), split_axis=0, concat_axis=0, t...  27.7 us
    pallas_call x1, Pallas kernels, stay(): pl.pallas_call(stay_kernel, out_shape=(jax.ShapeDtypeStruct(table.shape,...  19.3 us
    all_to_all x1, starting transfers between devices, on_device(): lax.all_to_all(outgoing, ('table', 'row'), split_axis=0, concat_axis=0, t...  11.2 us
    all_to_all x1, waiting for transfers between devices, on_device(): lax.all_to_all(moving, 'row', split_axis=0, concat_axis=0, tiled=True)  9.36 us
    pallas_call x1, Pallas kernels, pack(): pl.pallas_call(lambda *refs: pack_kernel(*refs, blocks=blocks, cap=cap),...  5.58 us
    all_to_all x1, starting transfers between devices, on_device(): lax.all_to_all(moving, 'row', split_axis=0, concat_axis=0, tiled=True)  4.07 us
    pallas_call x1, Pallas kernels, leave(): pl.pallas_call(lambda *refs: leave_kernel(*refs, cap=cap, rows=rows), out...  3.77 us
    pallas_call x1, Pallas kernels, arrive(): pl.pallas_call(arrive_kernel, out_shape=(jax.ShapeDtypeStruct(stayed.shap...  1.88 us
  transfers between devices with their start and end apart: 2, of which 2 were waited for; matrix products, arithmetic and copies ran while one was open for 2% of the time, Pallas kernels for 24%

profile of v6, /device:TPU:0, one launch (start us, length us, event | category | flops | bytes accessed | tf_op | source)
XLA Modules:
  0.0 88.5 jit_solution(415818050192753759)
XLA Ops:
  0.6 5.6 %pack.1 = f32[128,33,1,128]{3,2,1,0:T(1,128)} custom-call(s32[1,1024]{1,0:T(1,128)} %bitcast.8, s32[1,1024]{1,0:T(1,128)} %bitcast.9, s32[96,128]{1,0:T(8,128)} %bitcast.7, f32[1024,128]{1,0:T(8,128)} %refs_3_.1, f32[1024,128]{1,0:T(8,128)} %refs_4_.1), custom_call_target="tpu_custom_call" | custom-call | tf_op jit(solution)/shard_map/pack/pallas_call | solution.py:145
  6.2 0.0 copy-start.2
  6.2 0.0 copy-start.1
  6.2 11.2 %all-to-all-start = ((f32[128,33,1,128]{3,2,1,0:T(1,128)}), f32[128,33,1,128]{3,2,1,0:T(1,128)S(1)}, u32[]{:S(2)}, u32[]{:S(2)}) async-start(f32[128,33,1,128]{3,2,1,0:T(1,128)} %pack.1), calls=%async_computation | async-start | bytes 4325376 | tf_op jit(solution)/shard_map/all_to_all | solution.py:491
  17.4 0.0 copy-done.2
  17.5 0.1 and.48
  17.6 0.1 div.19
  17.7 0.1 add.46
  17.7 0.2 select_reduce_fusion
  17.9 0.1 copy.15
  18.0 0.1 reduce-window.17
  18.1 0.1 and_select_fusion
  18.2 0.1 copy.14
  18.3 0.1 reduce-window.16
  18.4 0.1 add_reduce_fusion.1
  18.5 0.1 select_reduce_fusion.2
  18.7 0.1 add_reduce_fusion
  18.8 0.1 select_reduce_fusion.4
  18.9 0.1 pad_add_fusion.list_ref.refs_0_
  19.0 0.0 copy-done.1
  19.0 1.8 %fetch.1 = (f32[12,128,128]{2,1,0:T(8,128)S(1)}, f32[128,128]{1,0:T(8,128)S(1)}) custom-call(s32[48]{0:T(128)S(1)} %pad_add_fusion.list_ref.refs_0_, f32[96,128,128]{2,1,0:T(8,128)} %table_hbm.1, f32[96,128]{1,0:T(8,128)S(1)} %copy-done.1), custom_call_target="tpu_custom_call" | custom-call | tf_op jit(solution)/shard_map/fetch/pallas_call | solution.py:231
  20.8 27.7 %all-to-all-done.refs_3_ = f32[128,33,1,128]{3,2,1,0:T(1,128)S(1)} async-done(((f32[128,33,1,128]{3,2,1,0:T(1,128)}), f32[128,33,1,128]{3,2,1,0:T(1,128)S(1)}, u32[]{:S(2)}, u32[]{:S(2)}) %all-to-all-start) | async-done | bytes 2162720 | tf_op jit(solution)/shard_map/all_to_all | solution.py:491
  48.5 3.8 %leave.1 = (s32[32,128]{1,0:T(8,128)S(1)}, f32[32,129,1,128]{3,2,1,0:T(1,128)}, f32[128,33,1,128]{3,2,1,0:T(1,128)}) custom-call(s32[48]{0:T(128)S(1)} %pad_add_fusion.list_ref.refs_0_, f32[12,128,128]{2,1,0:T(8,128)S(1)} %get-tuple-element.11.refs_1_, f32[128,128]{1,0:T(8,128)S(1)} %get-tuple-element.12.refs_2_, f32[128,33,1,128]{3,2,1,0:T(1,128)S(1)} %all-to-all-done.refs_3_), custom_call_target="tpu_custom_call" | custom-call | tf_op jit(solution)/shard_map/leave/pallas_call | solution.py:302
  52.3 4.1 %all-to-all-start.1 = ((f32[32,129,1,128]{3,2,1,0:T(1,128)}), f32[32,129,1,128]{3,2,1,0:T(1,128)S(1)}, u32[]{:S(2)}, u32[]{:S(2)}) async-start(f32[32,129,1,128]{3,2,1,0:T(1,128)} %get-tuple-element.13), calls=%async_computation.1 | async-start | bytes 4227072 | tf_op jit(solution)/shard_map/all_to_all | solution.py:504
  56.4 0.0 copy-start
  56.4 1.6 %copy-done = f32[128,33,1,128]{3,2,1,0:T(1,128)S(1)} copy-done((f32[128,33,1,128]{3,2,1,0:T(1,128)S(1)}, f32[128,33,1,128]{3,2,1,0:T(1,128)}, u32[]{:S(2)}) %copy-start) | copy-done | bytes 2162712
  58.0 19.3 %stay.1 = (f32[96,128,128]{2,1,0:T(8,128)}, f32[96,128]{1,0:T(8,128)S(1)}, f32[12,128,128]{2,1,0:T(8,128)S(1)}, f32[128,128]{1,0:T(8,128)S(1)}) custom-call(s32[48]{0:T(128)S(1)} %pad_add_fusion.list_ref.refs_0_, s32[32,128]{1,0:T(8,128)S(1)} %get-tuple-element.14.names_ref, f32[96,128,128]{2,1,0:T(8,128)} %table_hbm.1, f32[96,128]{1,0:T(8,128)S(1)} %copy-done.1, ...), custom_call_target="tpu_custom_call" | custom-call | tf_op jit(solution)/shard_map/stay/pallas_call | solution.py:402
  77.3 9.4 %all-to-all-done.1.got_ref = f32[32,129,1,128]{3,2,1,0:T(1,128)S(1)} async-done(((f32[32,129,1,128]{3,2,1,0:T(1,128)}), f32[32,129,1,128]{3,2,1,0:T(1,128)S(1)}, u32[]{:S(2)}, u32[]{:S(2)}) %all-to-all-start.1) | async-done | bytes 2113568 | tf_op jit(solution)/shard_map/all_to_all | solution.py:504
  86.6 1.9 %arrive.1 = (f32[96,128,128]{2,1,0:T(8,128)}, f32[96,128]{1,0:T(8,128)}) custom-call(s32[48]{0:T(128)S(1)} %pad_add_fusion.list_ref.refs_0_, f32[32,129,1,128]{3,2,1,0:T(1,128)S(1)} %all-to-all-done.1.got_ref, f32[12,128,128]{2,1,0:T(8,128)S(1)} %get-tuple-element.16.second_ref, ...), custom_call_target="tpu_custom_call", output_to_operand_aliasing={{0}: (4, {})} | custom-call | tf_op jit(solution)/shard_map/arrive/pallas_call | solution.py:453
  (6 shorter events, 0.1 us)
Async XLA Ops:
  6.2 11.2 %copy-start.2 = (s32[12288]{0:T(1024)S(1)}, s32[12288]{0:T(1024)}, u32[]{:S(2)}) copy-start(s32[12288]{0:T(1024)} %param.13) | copy-start | bytes 147460
  6.2 12.7 %copy-start.1 = (f32[96,128]{1,0:T(8,128)S(1)}, f32[96,128]{1,0:T(8,128)}, u32[]{:S(2)}) copy-start(f32[96,128]{1,0:T(8,128)} %acc_ref.3) | copy-start | bytes 147460
  6.2 42.3 %all-to-all-start = ((f32[128,33,1,128]{3,2,1,0:T(1,128)}), f32[128,33,1,128]{3,2,1,0:T(1,128)S(1)}, u32[]{:S(2)}, u32[]{:S(2)}) async-start(f32[128,33,1,128]{3,2,1,0:T(1,128)} %pack.1), calls=%async_computation | async-start | bytes 4325376 | tf_op jit(solution)/shard_map/all_to_all | solution.py:491
  52.3 34.3 %all-to-all-start.1 = ((f32[32,129,1,128]{3,2,1,0:T(1,128)}), f32[32,129,1,128]{3,2,1,0:T(1,128)S(1)}, u32[]{:S(2)}, u32[]{:S(2)}) async-start(f32[32,129,1,128]{3,2,1,0:T(1,128)} %get-tuple-element.13), calls=%async_computation.1 | async-start | bytes 4227072 | tf_op jit(solution)/shard_map/all_to_all | solution.py:504
  56.4 1.6 %copy-start = (f32[128,33,1,128]{3,2,1,0:T(1,128)S(1)}, f32[128,33,1,128]{3,2,1,0:T(1,128)}, u32[]{:S(2)}) copy-start(f32[128,33,1,128]{3,2,1,0:T(1,128)} %get-tuple-element.15.got_ref) | copy-start | bytes 6488068

commit v7 on v6

--- a/solution.py
+++ b/solution.py
@@ -12,7 +12,7 @@
 FROM, TO, SLOT, PEER = 0, MOVES, 2 * MOVES, 3 * MOVES
 VM = pltpu.VMEM
 SM = pltpu.SMEM
-ALL_VMEM = 67043328
+GRANT = 67043328
 ROOM = 14000000
 LAST_ROOM = 14000000
 
@@ -28,11 +28,11 @@
 def lookup(which_ref, indices):
     high, low = which_ref.shape
     pick = (iota((high, indices.shape[1]), 0) == (indices >> 7)).astype(jnp.bfloat16)
-    found = jnp.zeros((low, indices.shape[1]), jnp.float32)
     table = jnp.concatenate([which_ref[...].astype(jnp.float32), jnp.zeros((low - high, low), jnp.float32)], axis=0)
     table = jnp.transpose(table)[:, :high].astype(jnp.int32)
-    for part, scale in ((table >> 7, 128.0), (table & 127, 1.0)):
-        found += dot(part.astype(jnp.float32).astype(jnp.bfloat16), pick, (1, 0)) * scale
+    halves = jnp.concatenate([(table >> 7).astype(jnp.float32), (table & 127).astype(jnp.float32)], axis=0)
+    found = dot(halves.astype(jnp.bfloat16), pick, (1, 0))
+    found = found[:low] * 128.0 + found[low:]
     here = iota(found.shape, 0) == (indices & 127)
     return jnp.sum(jnp.where(here, found, 0.0), axis=0, keepdims=True).astype(jnp.int32)
 
@@ -163,7 +163,7 @@
             VM(message, jnp.float32),
             pltpu.SemaphoreType.DMA((9,)),
         ],
-        compiler_params=pltpu.CompilerParams(vmem_limit_bytes=ALL_VMEM),
+        compiler_params=pltpu.CompilerParams(vmem_limit_bytes=GRANT),
         name="pack",
     )(one_ids, two_ids, slots, one, two)
 
@@ -214,13 +214,14 @@
     return columns[:, k : k + 1]
 
 
-def fetch_kernel(list_ref, table_ref, acc_ref, out_ref, old_ref, sems):
-    copies = [pltpu.make_async_copy(table_ref.at[list_ref[FROM + k]], out_ref.at[k], sems.at[k]) for k in range(MOVES)]
+def fetch_kernel(list_ref, table_ref, acc_ref, out_ref, columns_ref, old_ref, sems):
+    copies = [pltpu.make_async_copy(table_ref.at[list_ref[0, FROM + k]], out_ref.at[k], sems.at[k]) for k in range(MOVES)]
     for copy in copies:
         copy.start()
     old_ref[...] = jnp.zeros_like(old_ref)
     for k in range(MOVES):
-        old_ref[pl.ds(k, 1), :] = acc_ref[pl.ds(list_ref[FROM + k], 1), :]
+        old_ref[pl.ds(k, 1), :] = acc_ref[pl.ds(list_ref[0, FROM + k], 1), :]
+    columns_ref[...] = jnp.transpose(old_ref[...])
     for copy in copies:
         copy.wait()
 
@@ -236,8 +237,8 @@
         ),
         in_specs=[pl.BlockSpec(memory_space=SM), hbm, vm],
         out_specs=(vm, vm),
-        scratch_shapes=[pltpu.SemaphoreType.DMA((MOVES,))],
-        compiler_params=pltpu.CompilerParams(vmem_limit_bytes=ALL_VMEM - ROOM),
+        scratch_shapes=[VM((LANES, LANES), jnp.float32), pltpu.SemaphoreType.DMA((MOVES,))],
+        compiler_params=pltpu.CompilerParams(vmem_limit_bytes=GRANT - ROOM),
         name="fetch",
     )(lists, table, acc)
 
@@ -250,18 +251,21 @@
     return ref.reshape(peers * rows, feature).at[pl.ds(peer * rows, rows)]
 
 
-def leave_kernel(list_ref, table_ref, acc_ref, got_ref, names_out, out_hbm, kept_hbm, out_ref, even_ref, odd_ref, old_ref, names_v, names_s, sems, *, cap, rows):
+def leave_kernel(list_hbm, table_ref, acc_ref, got_ref, names_out, out_hbm, kept_hbm, out_ref, even_ref, odd_ref, old_ref, names_v, names_s, list_ref, sems, *, cap, rows):
     block, feature = table_ref.shape[1:]
-    spans = [pl.ds(pl.multiple_of(list_ref[FROM + k] * block, block), block) for k in range(MOVES)]
+    scalars = pltpu.make_async_copy(list_hbm, list_ref, sems.at[MOVES + 2])
+    scalars.start()
     to_scalar = pltpu.make_async_copy(names_v, names_s, sems.at[MOVES])
     keep = pltpu.make_async_copy(got_ref, kept_hbm, sems.at[MOVES + 1])
     keep.start()
     named = read_names(got_ref, names_v, to_scalar, dump=rows)
     names_out[...] = named
+    scalars.wait()
+    spans = [pl.ds(pl.multiple_of(list_ref[0, FROM + k] * block, block), block) for k in range(MOVES)]
     at = iota(named.shape, 1) & (2 * cap - 1)
     goes = jnp.zeros(named.shape, jnp.bool_)
     for k in range(MOVES):
-        goes = goes | ((named >> 7) == list_ref[FROM + k])
+        goes = goes | ((named >> 7) == list_ref[0, FROM + k])
     needed = jnp.max(jnp.where(goes & (at < cap), at + 1, 0))
     for k in range(MOVES):
         even_ref[spans[k], :] = jnp.zeros((block, feature), jnp.float32)
@@ -280,14 +284,14 @@
         gradient = even_ref[spans[k], :] + odd_ref[spans[k], :]
         even_ref[spans[k], :] = gradient
         squares = jnp.where(lane == k, square_sums(gradient), squares)
-    fresh = jnp.transpose(acc_ref[...]) + squares * (1.0 / feature)
+    fresh = acc_ref[...] + squares * (1.0 / feature)
     rates = rate(jnp.where(lane < MOVES, fresh, 1.0))
     old_ref[...] = jnp.transpose(fresh)
     sends = []
     for k in range(MOVES):
         out_ref[k, pl.ds(block, 1), :] = old_ref[pl.ds(k, 1), :]
         out_ref[k, pl.ds(0, block), :] = table_ref[k] - lane_of(rates, k) * even_ref[spans[k], :]
-        sends.append(pltpu.make_async_copy(out_ref.at[k, pl.ds(0, block + 1)], message(out_hbm, list_ref[TO + k]), sems.at[k]))
+        sends.append(pltpu.make_async_copy(out_ref.at[k, pl.ds(0, block + 1)], message(out_hbm, list_ref[0, TO + k]), sems.at[k]))
         sends[-1].start()
     for send in sends:
         send.wait()
@@ -297,7 +301,6 @@
 def leave(lists, table, acc, got, peers, cap, rows):
     block, feature = table.shape[1:]
     vm = pl.BlockSpec(memory_space=VM)
-    sm = pl.BlockSpec(memory_space=SM)
     names = (got.shape[0] * 2 * cap // LANES, LANES)
     return pl.pallas_call(
         lambda *refs: leave_kernel(*refs, cap=cap, rows=rows),
@@ -306,7 +309,7 @@
             pltpu.HBM((peers, block + 1, 1, feature), jnp.float32),
             pltpu.HBM(got.shape, jnp.float32),
         ),
-        in_specs=[sm, vm, vm, vm],
+        in_specs=[pl.BlockSpec(memory_space=pltpu.HBM), vm, vm, vm],
         out_specs=(vm, pl.BlockSpec(memory_space=pltpu.HBM), pl.BlockSpec(memory_space=pltpu.HBM)),
         scratch_shapes=[
             VM((MOVES, block + 8, feature), jnp.float32),
@@ -315,9 +318,10 @@
             VM((LANES, LANES), jnp.float32),
             VM(names, jnp.int32),
             SM(names, jnp.int32),
-            pltpu.SemaphoreType.DMA((MOVES + 2,)),
+            SM(lists.shape, jnp.int32),
+            pltpu.SemaphoreType.DMA((MOVES + 3,)),
         ],
-        compiler_params=pltpu.CompilerParams(vmem_limit_bytes=ALL_VMEM - ROOM),
+        compiler_params=pltpu.CompilerParams(vmem_limit_bytes=GRANT - ROOM),
         name="leave",
     )(lists, table, acc, got)
 
@@ -372,7 +376,7 @@
     accout_ref[...] = jnp.transpose(fresh)[:blocks, :]
     arriving = zero
     for k in range(MOVES):
-        gradient = two_ref[span(list_ref[SLOT + k]), :]
+        gradient = two_ref[span(list_ref[0, SLOT + k]), :]
         arrive_ref[k] = gradient
         arriving = jnp.where(lane == k, square_sums(gradient), arriving)
     squares_ref[...] = arriving
@@ -416,7 +420,7 @@
             VM((2, LANES, LANES), jnp.float32),
             pltpu.SemaphoreType.DMA((blocks // PIECE,)),
         ],
-        compiler_params=pltpu.CompilerParams(vmem_limit_bytes=ALL_VMEM - ROOM),
+        compiler_params=pltpu.CompilerParams(vmem_limit_bytes=GRANT - ROOM),
         name="stay",
     )(lists, names, table, acc, got)
 
@@ -428,17 +432,17 @@
     acc_ref[...] = accstay_ref[...]
     lane = iota((block, LANES), 1)
     for k in range(MOVES):
-        old_ref[pl.ds(k, 1), :] = got_ref[list_ref[PEER + k], block]
+        old_ref[pl.ds(k, 1), :] = got_ref[list_ref[0, PEER + k], block]
     fresh = jnp.transpose(old_ref[...]) + squares_ref[...] * (1.0 / feature)
     rates = rate(jnp.where(lane < MOVES, fresh, 1.0))
     copies = []
     for k in range(MOVES):
-        buf_ref[k] = rows_ref[pl.ds(list_ref[PEER + k] * stride, block), :] - lane_of(rates, k) * second_ref[k]
-        copies.append(pltpu.make_async_copy(buf_ref.at[k], out_ref.at[list_ref[SLOT + k]], sems.at[k]))
+        buf_ref[k] = rows_ref[pl.ds(list_ref[0, PEER + k] * stride, block), :] - lane_of(rates, k) * second_ref[k]
+        copies.append(pltpu.make_async_copy(buf_ref.at[k], out_ref.at[list_ref[0, SLOT + k]], sems.at[k]))
         copies[-1].start()
     old_ref[...] = jnp.transpose(fresh)
     for k in range(MOVES):
-        acc_ref[pl.ds(list_ref[SLOT + k], 1), :] = old_ref[pl.ds(k, 1), :]
+        acc_ref[pl.ds(list_ref[0, SLOT + k], 1), :] = old_ref[pl.ds(k, 1), :]
     copies.append(pltpu.make_async_copy(acc_ref, acc_hbm, sems.at[MOVES]))
     copies[-1].start()
     for copy in copies:
@@ -465,7 +469,7 @@
             pltpu.SemaphoreType.DMA((MOVES + 1,)),
         ],
         input_output_aliases={4: 0},
-        compiler_params=pltpu.CompilerParams(vmem_limit_bytes=ALL_VMEM - LAST_ROOM),
+        compiler_params=pltpu.CompilerParams(vmem_limit_bytes=GRANT - LAST_ROOM),
         name="arrive",
     )(lists, got, second, squares, stayed, accstay)
 
@@ -498,6 +502,7 @@
     slots = jnp.sum(jnp.where(to_me, here - device * blocks + 1, 0), axis=1)
     coming = listed(slots > 0, (slots - 1, peer))
     lists = jnp.concatenate(going + coming)
+    lists = jnp.pad(lists, (0, LANES - lists.shape[0]))[None, :]
 
     gone, old = fetch(lists, table, accumulator)
     names, moving, kept = leave(lists, gone, old, got, peers, cap, blocks * block)

time: 88.9 us -> 88.2 us (level)
  no operation moved by 1% of the time
where the time goes in v7:
time: 88.2 us; the launch traced here: 87.8 us
  waiting for transfers between devices  37.1 us (42%)
  Pallas kernels  31.6 us (36%)
  starting transfers between devices  15.2 us (17%)
  local copies, waits for them, and re-layouts  2.05 us (2%)
  other arithmetic  1.05 us (1%)
    all_to_all x1, waiting for transfers between devices, on_device(): lax.all_to_all(outgoing, ('table', 'row'), split_axis=0, concat_axis=0, t...  27.7 us
    pallas_call x1, Pallas kernels, stay(): pl.pallas_call(stay_kernel, out_shape=(jax.ShapeDtypeStruct(table.shape,...  19.3 us
    all_to_all x1, starting transfers between devices, on_device(): lax.all_to_all(outgoing, ('table', 'row'), split_axis=0, concat_axis=0, t...  11.2 us
    all_to_all x1, waiting for transfers between devices, on_device(): lax.all_to_all(moving, 'row', split_axis=0, concat_axis=0, tiled=True)  9.36 us
    pallas_call x1, Pallas kernels, pack(): pl.pallas_call(lambda *refs: pack_kernel(*refs, blocks=blocks, cap=cap),...  5.46 us
    all_to_all x1, starting transfers between devices, on_device(): lax.all_to_all(moving, 'row', split_axis=0, concat_axis=0, tiled=True)  4.07 us
    pallas_call x1, Pallas kernels, leave(): pl.pallas_call(lambda *refs: leave_kernel(*refs, cap=cap, rows=rows), out...  3.17 us
    pallas_call x1, Pallas kernels, arrive(): pl.pallas_call(arrive_kernel, out_shape=(jax.ShapeDtypeStruct(stayed.shap...  1.87 us
  transfers between devices with their start and end apart: 2, of which 2 were waited for; matrix products, arithmetic and copies ran while one was open for 2% of the time, Pallas kernels for 24%

profile of v7, /device:TPU:0, one launch (start us, length us, event | category | flops | bytes accessed | tf_op | source)
XLA Modules:
  0.0 87.8 jit_solution(7907134551510628051)
XLA Ops:
  0.6 5.5 %pack.1 = f32[128,33,1,128]{3,2,1,0:T(1,128)} custom-call(s32[1,1024]{1,0:T(1,128)} %bitcast.10, s32[1,1024]{1,0:T(1,128)} %bitcast.11, s32[96,128]{1,0:T(8,128)} %bitcast.9, f32[1024,128]{1,0:T(8,128)} %refs_3_.1, f32[1024,128]{1,0:T(8,128)} %refs_4_.1), custom_call_target="tpu_custom_call" | custom-call | tf_op jit(solution)/shard_map/pack/pallas_call | solution.py:145
  6.1 0.0 copy-start.2
  6.1 0.0 copy-start.1
  6.1 11.2 %all-to-all-start = ((f32[128,33,1,128]{3,2,1,0:T(1,128)}), f32[128,33,1,128]{3,2,1,0:T(1,128)S(1)}, u32[]{:S(2)}, u32[]{:S(2)}) async-start(f32[128,33,1,128]{3,2,1,0:T(1,128)} %pack.1), calls=%async_computation | async-start | bytes 4325376 | tf_op jit(solution)/shard_map/all_to_all | solution.py:495
  17.3 0.0 copy-done.2
  17.4 0.1 and.48
  17.5 0.1 div.19
  17.5 0.1 add.48
  17.6 0.2 select_reduce_fusion
  17.8 0.1 copy.15
  17.9 0.1 reduce-window.17
  18.0 0.1 and_select_fusion
  18.1 0.1 copy.14
  18.2 0.1 reduce-window.16
  18.3 0.1 add_reduce_fusion.1
  18.4 0.1 select_reduce_fusion.2
  18.5 0.1 add_reduce_fusion
  18.7 0.1 select_reduce_fusion.4
  18.8 0.1 pad_add_fusion
  18.9 0.0 copy-done.1
  18.9 1.8 %fetch.1 = (f32[12,128,128]{2,1,0:T(8,128)S(1)}, f32[128,128]{1,0:T(8,128)S(1)}) custom-call(s32[1,128]{1,0:T(1,128)S(1)} %pad_bitcast_fusion.list_ref.refs_0_, f32[96,128,128]{2,1,0:T(8,128)} %table_hbm.1, f32[96,128]{1,0:T(8,128)S(1)} %copy-done.1), custom_call_target="tpu_custom_call" | custom-call | tf_op jit(solution)/shard_map/fetch/pallas_call | solution.py:232
  20.7 27.7 %all-to-all-done.refs_3_ = f32[128,33,1,128]{3,2,1,0:T(1,128)S(1)} async-done(((f32[128,33,1,128]{3,2,1,0:T(1,128)}), f32[128,33,1,128]{3,2,1,0:T(1,128)S(1)}, u32[]{:S(2)}, u32[]{:S(2)}) %all-to-all-start) | async-done | bytes 2162720 | tf_op jit(solution)/shard_map/all_to_all | solution.py:495
  48.4 3.2 %leave.1 = (s32[32,128]{1,0:T(8,128)S(1)}, f32[32,129,1,128]{3,2,1,0:T(1,128)}, f32[128,33,1,128]{3,2,1,0:T(1,128)}) custom-call(s32[1,128]{1,0:T(1,128)S(1)} %pad_bitcast_fusion.list_ref.refs_0_, f32[12,128,128]{2,1,0:T(8,128)S(1)} %get-tuple-element.11.refs_1_, f32[128,128]{1,0:T(8,128)S(1)} %get-tuple-element.12.refs_2_, ...), custom_call_target="tpu_custom_call" | custom-call | tf_op jit(solution)/shard_map/leave/pallas_call | solution.py:305
  51.6 4.1 %all-to-all-start.1 = ((f32[32,129,1,128]{3,2,1,0:T(1,128)}), f32[32,129,1,128]{3,2,1,0:T(1,128)S(1)}, u32[]{:S(2)}, u32[]{:S(2)}) async-start(f32[32,129,1,128]{3,2,1,0:T(1,128)} %get-tuple-element.13), calls=%async_computation.1 | async-start | bytes 4227072 | tf_op jit(solution)/shard_map/all_to_all | solution.py:509
  55.7 0.0 copy-start
  55.7 1.6 %copy-done = f32[128,33,1,128]{3,2,1,0:T(1,128)S(1)} copy-done((f32[128,33,1,128]{3,2,1,0:T(1,128)S(1)}, f32[128,33,1,128]{3,2,1,0:T(1,128)}, u32[]{:S(2)}) %copy-start) | copy-done | bytes 2162712
  57.3 19.3 %stay.1 = (f32[96,128,128]{2,1,0:T(8,128)}, f32[96,128]{1,0:T(8,128)S(1)}, f32[12,128,128]{2,1,0:T(8,128)S(1)}, f32[128,128]{1,0:T(8,128)S(1)}) custom-call(s32[1,128]{1,0:T(1,128)S(1)} %pad_bitcast_fusion.list_ref.refs_0_, s32[32,128]{1,0:T(8,128)S(1)} %get-tuple-element.14.names_ref, f32[96,128,128]{2,1,0:T(8,128)} %table_hbm.1, f32[96,128]{1,0:T(8,128)S(1)} %copy-done.1, ...), custom_call_target="tpu_custom_call" | custom-call | tf_op jit(solution)/shard_map/stay/pallas_call | solution.py:406
  76.6 9.4 %all-to-all-done.1.got_ref = f32[32,129,1,128]{3,2,1,0:T(1,128)S(1)} async-done(((f32[32,129,1,128]{3,2,1,0:T(1,128)}), f32[32,129,1,128]{3,2,1,0:T(1,128)S(1)}, u32[]{:S(2)}, u32[]{:S(2)}) %all-to-all-start.1) | async-done | bytes 2113568 | tf_op jit(solution)/shard_map/all_to_all | solution.py:509
  85.9 1.9 %arrive.1 = (f32[96,128,128]{2,1,0:T(8,128)}, f32[96,128]{1,0:T(8,128)}) custom-call(s32[1,128]{1,0:T(1,128)S(1)} %pad_bitcast_fusion.list_ref.refs_0_, f32[32,129,1,128]{3,2,1,0:T(1,128)S(1)} %all-to-all-done.1.got_ref, f32[12,128,128]{2,1,0:T(8,128)S(1)} %get-tuple-element.16.second_ref, ...), custom_call_target="tpu_custom_call", output_to_operand_aliasing={{0}: (4, {})} | custom-call | tf_op jit(solution)/shard_map/arrive/pallas_call | solution.py:457
  (7 shorter events, 0.1 us)
Async XLA Ops:
  6.1 11.2 %copy-start.2 = (s32[12288]{0:T(1024)S(1)}, s32[12288]{0:T(1024)}, u32[]{:S(2)}) copy-start(s32[12288]{0:T(1024)} %param.13) | copy-start | bytes 147460
  6.1 12.7 %copy-start.1 = (f32[96,128]{1,0:T(8,128)S(1)}, f32[96,128]{1,0:T(8,128)}, u32[]{:S(2)}) copy-start(f32[96,128]{1,0:T(8,128)} %acc_ref.3) | copy-start | bytes 147460
  6.1 42.3 %all-to-all-start = ((f32[128,33,1,128]{3,2,1,0:T(1,128)}), f32[128,33,1,128]{3,2,1,0:T(1,128)S(1)}, u32[]{:S(2)}, u32[]{:S(2)}) async-start(f32[128,33,1,128]{3,2,1,0:T(1,128)} %pack.1), calls=%async_computation | async-start | bytes 4325376 | tf_op jit(solution)/shard_map/all_to_all | solution.py:495
  51.6 34.3 %all-to-all-start.1 = ((f32[32,129,1,128]{3,2,1,0:T(1,128)}), f32[32,129,1,128]{3,2,1,0:T(1,128)S(1)}, u32[]{:S(2)}, u32[]{:S(2)}) async-start(f32[32,129,1,128]{3,2,1,0:T(1,128)} %get-tuple-element.13), calls=%async_computation.1 | async-start | bytes 4227072 | tf_op jit(solution)/shard_map/all_to_all | solution.py:509
  55.7 1.6 %copy-start = (f32[128,33,1,128]{3,2,1,0:T(1,128)S(1)}, f32[128,33,1,128]{3,2,1,0:T(1,128)}, u32[]{:S(2)}) copy-start(f32[128,33,1,128]{3,2,1,0:T(1,128)} %get-tuple-element.15.got_ref) | copy-start | bytes 6488068

commit v8 on v7

--- a/solution.py
+++ b/solution.py
@@ -378,7 +378,7 @@
     for k in range(MOVES):
         gradient = two_ref[span(list_ref[0, SLOT + k]), :]
         arrive_ref[k] = gradient
-        arriving = jnp.where(lane == k, square_sums(gradient), arriving)
+        arriving = jnp.where(lane == list_ref[0, PEER + k], square_sums(gradient), arriving)
     squares_ref[...] = arriving
 
     def piece(i, _):
@@ -425,24 +425,29 @@
     )(lists, names, table, acc, got)
 
 
-def arrive_kernel(list_ref, got_ref, second_ref, squares_ref, stayed_ref, accstay_ref, out_ref, acc_hbm, acc_ref, buf_ref, old_ref, sems):
+def arrive_kernel(list_hbm, got_ref, second_ref, squares_ref, stayed_ref, accstay_ref, out_ref, acc_hbm, acc_ref, buf_ref, old_ref, list_ref, sems):
     block, feature = stayed_ref.shape[1:]
     stride = got_ref.shape[1]
     rows_ref = got_ref.reshape(got_ref.shape[0] * stride, feature)
+    scalars = pltpu.make_async_copy(list_hbm, list_ref, sems.at[MOVES + 1])
+    scalars.start()
     acc_ref[...] = accstay_ref[...]
     lane = iota((block, LANES), 1)
-    for k in range(MOVES):
-        old_ref[pl.ds(k, 1), :] = got_ref[list_ref[0, PEER + k], block]
+    peers = got_ref.shape[0]
+    for p in range(peers):
+        old_ref[pl.ds(p, 1), :] = got_ref[p, block]
     fresh = jnp.transpose(old_ref[...]) + squares_ref[...] * (1.0 / feature)
-    rates = rate(jnp.where(lane < MOVES, fresh, 1.0))
+    rates = rate(jnp.where(lane < peers, fresh, 1.0))
+    scalars.wait()
     copies = []
     for k in range(MOVES):
-        buf_ref[k] = rows_ref[pl.ds(list_ref[0, PEER + k] * stride, block), :] - lane_of(rates, k) * second_ref[k]
+        rates_of = jnp.sum(jnp.where(lane == list_ref[0, PEER + k], rates, 0.0), axis=1, keepdims=True)
+        buf_ref[k] = rows_ref[pl.ds(list_ref[0, PEER + k] * stride, block), :] - rates_of * second_ref[k]
         copies.append(pltpu.make_async_copy(buf_ref.at[k], out_ref.at[list_ref[0, SLOT + k]], sems.at[k]))
         copies[-1].start()
     old_ref[...] = jnp.transpose(fresh)
     for k in range(MOVES):
-        acc_ref[pl.ds(list_ref[0, SLOT + k], 1), :] = old_ref[pl.ds(k, 1), :]
+        acc_ref[pl.ds(list_ref[0, SLOT + k], 1), :] = old_ref[pl.ds(list_ref[0, PEER + k], 1), :]
     copies.append(pltpu.make_async_copy(acc_ref, acc_hbm, sems.at[MOVES]))
     copies[-1].start()
     for copy in copies:
@@ -452,7 +457,6 @@
 def arrive(lists, got, second, squares, stayed, accstay):
     blocks, block, feature = stayed.shape
     vm = pl.BlockSpec(memory_space=VM)
-    sm = pl.BlockSpec(memory_space=SM)
     hbm = pl.BlockSpec(memory_space=pltpu.HBM)
     return pl.pallas_call(
         arrive_kernel,
@@ -460,13 +464,14 @@
             jax.ShapeDtypeStruct(stayed.shape, jnp.float32),
             jax.ShapeDtypeStruct(accstay.shape, jnp.float32),
         ),
-        in_specs=[sm, vm, vm, vm, hbm, vm],
+        in_specs=[hbm, vm, vm, vm, hbm, vm],
         out_specs=(hbm, hbm),
         scratch_shapes=[
             VM(accstay.shape, jnp.float32),
             VM((MOVES, block, feature), jnp.float32),
             VM((LANES, LANES), jnp.float32),
-            pltpu.SemaphoreType.DMA((MOVES + 1,)),
+            SM(lists.shape, jnp.int32),
+            pltpu.SemaphoreType.DMA((MOVES + 2,)),
         ],
         input_output_aliases={4: 0},
         compiler_params=pltpu.CompilerParams(vmem_limit_bytes=GRANT - LAST_ROOM),

time: 88.2 us -> 88 us (level)
  no operation moved by 1% of the time
where the time goes in v8:
time: 88 us; the launch traced here: 87.5 us
  waiting for transfers between devices  37.1 us (42%)
  Pallas kernels  31.3 us (36%)
  starting transfers between devices  15.2 us (17%)
  local copies, waits for them, and re-layouts  2.05 us (2%)
  other arithmetic  1.05 us (1%)
    all_to_all x1, waiting for transfers between devices, on_device(): lax.all_to_all(outgoing, ('table', 'row'), split_axis=0, concat_axis=0, t...  27.7 us
    pallas_call x1, Pallas kernels, stay(): pl.pallas_call(stay_kernel, out_shape=(jax.ShapeDtypeStruct(table.shape,...  19.3 us
    all_to_all x1, starting transfers between devices, on_device(): lax.all_to_all(outgoing, ('table', 'row'), split_axis=0, concat_axis=0, t...  11.2 us
    all_to_all x1, waiting for transfers between devices, on_device(): lax.all_to_all(moving, 'row', split_axis=0, concat_axis=0, tiled=True)  9.36 us
    pallas_call x1, Pallas kernels, pack(): pl.pallas_call(lambda *refs: pack_kernel(*refs, blocks=blocks, cap=cap),...  5.46 us
    all_to_all x1, starting transfers between devices, on_device(): lax.all_to_all(moving, 'row', split_axis=0, concat_axis=0, tiled=True)  4.07 us
    pallas_call x1, Pallas kernels, leave(): pl.pallas_call(lambda *refs: leave_kernel(*refs, cap=cap, rows=rows), out...  3.12 us
    pallas_call x1, Pallas kernels, fetch(): pl.pallas_call(fetch_kernel, out_shape=(jax.ShapeDtypeStruct((MOVES,) + t...  1.82 us
  transfers between devices with their start and end apart: 2, of which 2 were waited for; matrix products, arithmetic and copies ran while one was open for 2% of the time, Pallas kernels for 24%

profile of v8, /device:TPU:0, one launch (start us, length us, event | category | flops | bytes accessed | tf_op | source)
XLA Modules:
  0.0 87.5 jit_solution(11108530065680992888)
XLA Ops:
  0.6 5.5 %pack.1 = f32[128,33,1,128]{3,2,1,0:T(1,128)} custom-call(s32[1,1024]{1,0:T(1,128)} %bitcast.10, s32[1,1024]{1,0:T(1,128)} %bitcast.11, s32[96,128]{1,0:T(8,128)} %bitcast.9, f32[1024,128]{1,0:T(8,128)} %refs_3_.1, f32[1024,128]{1,0:T(8,128)} %refs_4_.1), custom_call_target="tpu_custom_call" | custom-call | tf_op jit(solution)/shard_map/pack/pallas_call | solution.py:145
  6.1 0.0 copy-start.2
  6.1 0.0 copy-start.1
  6.1 11.2 %all-to-all-start = ((f32[128,33,1,128]{3,2,1,0:T(1,128)}), f32[128,33,1,128]{3,2,1,0:T(1,128)S(1)}, u32[]{:S(2)}, u32[]{:S(2)}) async-start(f32[128,33,1,128]{3,2,1,0:T(1,128)} %pack.1), calls=%async_computation | async-start | bytes 4325376 | tf_op jit(solution)/shard_map/all_to_all | solution.py:500
  17.3 0.0 copy-done.2
  17.4 0.1 and.48
  17.5 0.1 div.19
  17.5 0.1 add.48
  17.6 0.2 select_reduce_fusion
  17.8 0.1 copy.15
  17.9 0.1 reduce-window.17
  18.0 0.1 and_select_fusion
  18.1 0.1 copy.14
  18.2 0.1 reduce-window.16
  18.3 0.1 add_reduce_fusion.1
  18.4 0.1 select_reduce_fusion.2
  18.5 0.1 add_reduce_fusion
  18.7 0.1 select_reduce_fusion.4
  18.8 0.1 pad_add_fusion
  18.9 0.0 copy-done.1
  18.9 1.8 %fetch.1 = (f32[12,128,128]{2,1,0:T(8,128)S(1)}, f32[128,128]{1,0:T(8,128)S(1)}) custom-call(s32[1,128]{1,0:T(1,128)S(1)} %pad_bitcast_fusion.list_ref.refs_0_.list_hbm, f32[96,128,128]{2,1,0:T(8,128)} %table_hbm.1, f32[96,128]{1,0:T(8,128)S(1)} %copy-done.1), custom_call_target="tpu_custom_call" | custom-call | tf_op jit(solution)/shard_map/fetch/pallas_call | solution.py:232
  20.7 27.7 %all-to-all-done.refs_3_ = f32[128,33,1,128]{3,2,1,0:T(1,128)S(1)} async-done(((f32[128,33,1,128]{3,2,1,0:T(1,128)}), f32[128,33,1,128]{3,2,1,0:T(1,128)S(1)}, u32[]{:S(2)}, u32[]{:S(2)}) %all-to-all-start) | async-done | bytes 2162720 | tf_op jit(solution)/shard_map/all_to_all | solution.py:500
  48.4 3.1 %leave.1 = (s32[32,128]{1,0:T(8,128)S(1)}, f32[32,129,1,128]{3,2,1,0:T(1,128)}, f32[128,33,1,128]{3,2,1,0:T(1,128)}) custom-call(s32[1,128]{1,0:T(1,128)S(1)} %pad_bitcast_fusion.list_ref.refs_0_.list_hbm, f32[12,128,128]{2,1,0:T(8,128)S(1)} %get-tuple-element.11.refs_1_, f32[128,128]{1,0:T(8,128)S(1)} %get-tuple-element.12.refs_2_, ...), custom_call_target="tpu_custom_call" | custom-call | tf_op jit(solution)/shard_map/leave/pallas_call | solution.py:305
  51.5 4.1 %all-to-all-start.1 = ((f32[32,129,1,128]{3,2,1,0:T(1,128)}), f32[32,129,1,128]{3,2,1,0:T(1,128)S(1)}, u32[]{:S(2)}, u32[]{:S(2)}) async-start(f32[32,129,1,128]{3,2,1,0:T(1,128)} %get-tuple-element.13), calls=%async_computation.1 | async-start | bytes 4227072 | tf_op jit(solution)/shard_map/all_to_all | solution.py:514
  55.6 0.0 copy-start
  55.6 1.6 %copy-done = f32[128,33,1,128]{3,2,1,0:T(1,128)S(1)} copy-done((f32[128,33,1,128]{3,2,1,0:T(1,128)S(1)}, f32[128,33,1,128]{3,2,1,0:T(1,128)}, u32[]{:S(2)}) %copy-start) | copy-done | bytes 2162712
  57.2 19.3 %stay.1 = (f32[96,128,128]{2,1,0:T(8,128)}, f32[96,128]{1,0:T(8,128)S(1)}, f32[12,128,128]{2,1,0:T(8,128)S(1)}, f32[128,128]{1,0:T(8,128)S(1)}) custom-call(s32[1,128]{1,0:T(1,128)S(1)} %pad_bitcast_fusion.list_ref.refs_0_.list_hbm, s32[32,128]{1,0:T(8,128)S(1)} %get-tuple-element.14.names_ref, f32[96,128,128]{2,1,0:T(8,128)} %table_hbm.1, ...), custom_call_target="tpu_custom_call" | custom-call | tf_op jit(solution)/shard_map/stay/pallas_call | solution.py:406
  76.5 9.4 %all-to-all-done.1.got_ref = f32[32,129,1,128]{3,2,1,0:T(1,128)S(1)} async-done(((f32[32,129,1,128]{3,2,1,0:T(1,128)}), f32[32,129,1,128]{3,2,1,0:T(1,128)S(1)}, u32[]{:S(2)}, u32[]{:S(2)}) %all-to-all-start.1) | async-done | bytes 2113568 | tf_op jit(solution)/shard_map/all_to_all | solution.py:514
  85.9 1.6 %arrive.1 = (f32[96,128,128]{2,1,0:T(8,128)}, f32[96,128]{1,0:T(8,128)}) custom-call(s32[1,128]{1,0:T(1,128)S(1)} %pad_bitcast_fusion.list_ref.refs_0_.list_hbm, f32[32,129,1,128]{3,2,1,0:T(1,128)S(1)} %all-to-all-done.1.got_ref, f32[12,128,128]{2,1,0:T(8,128)S(1)} %get-tuple-element.16.second_ref, ...), custom_call_target="tpu_custom_call", output_to_operand_aliasing={{0}: (4, {})} | custom-call | tf_op jit(solution)/shard_map/arrive/pallas_call | solution.py:461
  (7 shorter events, 0.1 us)
Async XLA Ops:
  6.1 11.2 %copy-start.2 = (s32[12288]{0:T(1024)S(1)}, s32[12288]{0:T(1024)}, u32[]{:S(2)}) copy-start(s32[12288]{0:T(1024)} %param.13) | copy-start | bytes 147460
  6.1 12.7 %copy-start.1 = (f32[96,128]{1,0:T(8,128)S(1)}, f32[96,128]{1,0:T(8,128)}, u32[]{:S(2)}) copy-start(f32[96,128]{1,0:T(8,128)} %acc_ref.3) | copy-start | bytes 147460
  6.1 42.3 %all-to-all-start = ((f32[128,33,1,128]{3,2,1,0:T(1,128)}), f32[128,33,1,128]{3,2,1,0:T(1,128)S(1)}, u32[]{:S(2)}, u32[]{:S(2)}) async-start(f32[128,33,1,128]{3,2,1,0:T(1,128)} %pack.1), calls=%async_computation | async-start | bytes 4325376 | tf_op jit(solution)/shard_map/all_to_all | solution.py:500
  51.5 34.3 %all-to-all-start.1 = ((f32[32,129,1,128]{3,2,1,0:T(1,128)}), f32[32,129,1,128]{3,2,1,0:T(1,128)S(1)}, u32[]{:S(2)}, u32[]{:S(2)}) async-start(f32[32,129,1,128]{3,2,1,0:T(1,128)} %get-tuple-element.13), calls=%async_computation.1 | async-start | bytes 4227072 | tf_op jit(solution)/shard_map/all_to_all | solution.py:514
  55.6 1.6 %copy-start = (f32[128,33,1,128]{3,2,1,0:T(1,128)S(1)}, f32[128,33,1,128]{3,2,1,0:T(1,128)}, u32[]{:S(2)}) copy-start(f32[128,33,1,128]{3,2,1,0:T(1,128)} %get-tuple-element.15.got_ref) | copy-start | bytes 6488068
